TPU v7x, 32 devices: a whole 2x2x4 slice. The times are simulated.
32 devices in a mesh: data: 2 (over x), fsdp: 4 (over z), ep: 4 (over y, core).
Axes of the slice: x: 2, y: 2, z: 4, core: 2. Of those that a mesh axis runs over, the one named last changes fastest.
Arguments:
- x_in: bfloat16 [32, 512, 1024], P(('data', 'fsdp', 'ep')), parts along dimension 0
- expert_idx: int32 [32, 512, 8], P(('data', 'fsdp', 'ep')), parts along dimension 0
- expert_slot: int32 [32, 512, 8], P(('data', 'fsdp', 'ep')), parts along dimension 0
- expert_gate: bfloat16 [32, 512, 8], P(('data', 'fsdp', 'ep')), parts along dimension 0
- attn_gain: bfloat16 [1024], replicated
- w_qkv: bfloat16 [1024, 3, 16, 64], P('fsdp')
- w_out: bfloat16 [16, 64, 1024], P('fsdp')
- moe_gain: bfloat16 [1024], replicated
- w_gate: bfloat16 [32, 1024, 512], P('ep', 'fsdp')
- w_up: bfloat16 [32, 1024, 512], P('ep', 'fsdp')
- w_down: bfloat16 [32, 512, 1024], P('ep', None, 'fsdp')
Outputs:
- output: bfloat16 [32, 512, 1024], P(('data', 'fsdp', 'ep')), parts along dimension 0
There are 2 independent parts. A program takes and returns all parts, laid end to end along the dimension named above; an argument that names none is the same for every part.
All inputs are finite; a program needn't handle non-finite values.
Results may differ from a plain program's by a relative error of at most 0.0144674.
Values are sent between devices in bfloat16 or wider.
A program may use at most 1 GiB of HBM per device.

v0:
```python
import jax
import jax.numpy as jnp
from jax import lax
from jax.sharding import PartitionSpec as P

NORM_EPS = 1e-6
ROPE_BASE = 10000.0


def rms_norm(hidden, gain_vec):
    wide = hidden.astype(jnp.float32)
    inv_rms = lax.rsqrt(jnp.mean(wide * wide, axis=-1, keepdims=True) + NORM_EPS)
    return (wide * inv_rms * gain_vec.astype(jnp.float32)).astype(jnp.bfloat16)


def attention_block(x_blk, attn_gain, w_qkv, w_out):
    seq_len = x_blk.shape[1]
    head_dim = w_qkv.shape[3]
    half_dim = head_dim // 2
    normed = rms_norm(x_blk, attn_gain)
    qkv_proj = jnp.einsum('bsd,dthe->bsthe', normed, w_qkv, preferred_element_type=jnp.float32)
    inv_freq = ROPE_BASE ** (-jnp.arange(half_dim, dtype=jnp.float32) / half_dim)
    angles = jnp.arange(seq_len, dtype=jnp.float32)[:, None] * inv_freq[None, :]
    cos_tab = jnp.cos(angles)[None, :, None, :]
    sin_tab = jnp.sin(angles)[None, :, None, :]

    def rotate(heads_in):
        first_half = heads_in[..., :half_dim]
        second_half = heads_in[..., half_dim:]
        return jnp.concatenate([first_half * cos_tab - second_half * sin_tab, second_half * cos_tab + first_half * sin_tab], axis=-1)

    query_rot = rotate(qkv_proj[:, :, 0]).astype(jnp.bfloat16)
    keys_rot = rotate(qkv_proj[:, :, 1]).astype(jnp.bfloat16)
    values = qkv_proj[:, :, 2].astype(jnp.bfloat16)
    scores = jnp.einsum('bqhe,bkhe->bhqk', query_rot, keys_rot, preferred_element_type=jnp.float32) * (head_dim ** -0.5)
    causal = jnp.arange(seq_len)[:, None] >= jnp.arange(seq_len)[None, :]
    attn_probs = jax.nn.softmax(jnp.where(causal, scores, -1e30), axis=-1).astype(jnp.bfloat16)
    context = jnp.einsum('bhqk,bkhe->bqhe', attn_probs, values, preferred_element_type=jnp.float32).astype(jnp.bfloat16)
    attn_out = jnp.einsum('crif,ife->cre', context, w_out, preferred_element_type=jnp.float32)
    return (x_blk.astype(jnp.float32) + attn_out).astype(jnp.bfloat16)


def capacity_of(tok_count, top_k, experts):
    return 8 * ((5 * tok_count * top_k) // (32 * experts) + 1)


def route_tables(idx_blk, slot_blk, gate_blk, experts, capacity):
    dest_pos = jnp.where(slot_blk >= 0, idx_blk * capacity + slot_blk, -1)
    positions = jnp.arange(experts * capacity)
    slot_match = dest_pos[..., None] == positions
    dispatch = jnp.sum(slot_match, axis=-2).astype(jnp.bfloat16)
    combine = jnp.sum(jnp.where(slot_match, gate_blk[..., None], jnp.zeros((), jnp.bfloat16)), axis=-2)
    return dispatch, combine


def solution(mesh):
    ep_count = mesh.shape['ep']
    tok_spec = P(('data', 'fsdp', 'ep'), None, None)

    def local_step(x_blk, idx_blk, slot_blk, gate_blk, attn_gain, qkv_shard, out_shard, moe_gain, gate_shard, up_shard, down_shard):
        w_qkv = lax.all_gather(qkv_shard, 'fsdp', axis=0, tiled=True)
        w_out = lax.all_gather(out_shard, 'fsdp', axis=0, tiled=True)
        hidden = attention_block(x_blk, attn_gain, w_qkv, w_out)
        w_gate = lax.all_gather(gate_shard, 'fsdp', axis=1, tiled=True)
        w_up = lax.all_gather(up_shard, 'fsdp', axis=1, tiled=True)
        w_down = lax.all_gather(down_shard, 'fsdp', axis=2, tiled=True)
        batch_rows, seq_len, d_model = x_blk.shape
        tok_count = batch_rows * seq_len
        top_k = idx_blk.shape[-1]
        experts = gate_shard.shape[0] * ep_count
        capacity = capacity_of(tok_count, top_k, experts)
        dispatch, combine = route_tables(idx_blk.reshape(tok_count, top_k), slot_blk.reshape(tok_count, top_k), gate_blk.reshape(tok_count, top_k), experts, capacity)
        normed = rms_norm(hidden, moe_gain).reshape(tok_count, d_model)
        send_buf = jnp.einsum('ts,td->sd', dispatch, normed, preferred_element_type=jnp.float32).astype(jnp.bfloat16)
        recv_buf = lax.all_to_all(send_buf.reshape(experts, capacity, d_model), 'ep', 0, 1, tiled=True)
        gate_act = jnp.einsum('ecd,edf->ecf', recv_buf, w_gate, preferred_element_type=jnp.float32)
        up_act = jnp.einsum('ecd,edf->ecf', recv_buf, w_up, preferred_element_type=jnp.float32)
        inner_act = (jax.nn.silu(gate_act) * up_act).astype(jnp.bfloat16)
        expert_out = jnp.einsum('ecf,efd->ecd', inner_act, w_down, preferred_element_type=jnp.float32).astype(jnp.bfloat16)
        back_buf = lax.all_to_all(expert_out, 'ep', 1, 0, tiled=True).reshape(experts * capacity, d_model)
        moe_sum = jnp.dot(combine, back_buf, preferred_element_type=jnp.float32)
        result = hidden.reshape(tok_count, d_model).astype(jnp.float32) + moe_sum
        return result.astype(jnp.bfloat16).reshape(batch_rows, seq_len, d_model)

    return jax.shard_map(local_step, mesh=mesh, in_specs=(tok_spec, tok_spec, tok_spec, tok_spec, P(None), P('fsdp', None, None, None), P('fsdp', None, None), P(None), P('ep', 'fsdp', None), P('ep', 'fsdp', None), P('ep', None, 'fsdp')), out_specs=tok_spec, check_vma=False)
```

profile of v0, /device:TPU:0, one launch (start us, length us, event | category | flops | bytes accessed | tf_op | source)
XLA Modules:
  0.0 819.6 jit_solution(5716250027911035679)
XLA Ops:
  6.5 0.0 copy-start.2
  6.5 0.0 copy-start.6
  6.5 0.0 copy-start.4
  6.5 0.0 copy-start.3
  6.5 0.0 all-gather.6.cloned.1.call-start
  6.6 0.7 all-gather.6.cloned.1.call-update
  7.3 0.0 all-gather.8.cloned.1.call-start
  7.3 0.7 all-gather.8.cloned.1.call-update
  8.0 0.0 all-gather.10.cloned.1.call-start
  8.1 0.7 all-gather.10.cloned.1.call-update
  8.8 0.0 copy-start.7
  8.8 0.0 all-gather.12.cloned.1.call-start
  8.8 0.5 all-gather.12.cloned.1.call-update
  9.3 0.0 all-gather.14.cloned.1.call-start
  9.4 0.5 all-gather.14.cloned.1.call-update
  9.9 0.8 iota_compare_fusion.1
  10.7 0.0 copy-done.2
  10.7 0.3 fusion.12
  11.0 0.0 copy-done.6
  11.0 0.3 fusion.44
  11.4 0.0 copy-done.4
  11.4 0.0 copy-done.3
  11.4 0.1 copy.34
  11.5 112.3 %convert_reduce_fusion = s32[512,5376]{1,0:T(8,128)} fusion(s32[512,8]{1,0:T(8,128)S(1)} %copy.34), kind=kLoop, calls=%fused_computation.1 | loop fusion | flops 63307776 | bytes 11026432 | tf_op jit(solution)/shard_map/reduce_sum | solution.py:51
  123.8 0.0 copy-done.7
  123.8 3.5 all-gather.6.cloned.1.call-done
  127.4 5.8 fusion.32
  133.1 0.0 copy-start.1
  133.1 0.7 slice_bitcast_fusion.1
  133.8 0.7 fusion.39
  134.6 1.5 copy-done.1
  136.1 21.3 %fusion.52 = (f32[16,512]{1,0:T(8,128)S(1)}, f32[16,512,512]{1,2,0:T(8,128)}) fusion(pred[512,512]{0,1:T(8,128)(4,1)} %iota_compare_fusion.1, bf16[512,16,32]{0,2,1:T(8,128)(2,1)S(1)} %get-tuple-element.11, bf16[512,16,32]{0,2,1:T(8,128)(2,1)S(1)} %get-tuple-element.12, bf16[512,16,32]{0,2,1:T(8,128)(2,1)S(1)} %get-tuple-element.8, ...), kind=kOutput, calls=%fused_computation.73 | convolution fusion | flops 557842944 | bytes 19169280 | tf_op jit(solution)/shard_map/sub | solution.py:37
  157.4 15.3 %all-gather.8.cloned.1.call-done = bf16[16,64,1024]{2,1,0:T(8,128)(2,1)} async-done(((bf16[4,64,1024]{2,1,0:T(8,128)(2,1)}), bf16[16,64,1024]{2,1,0:T(8,128)(2,1)}) %all-gather.8.cloned.1.call-update) | async-done | bytes 2097168 | tf_op jit(solution)/shard_map/all_gather | solution.py:62
  172.7 9.8 %fusion.18 = (f32[512]{0:T(512)S(1)}, bf16[1,512,1024]{2,1,0:T(8,128)(2,1)S(1)}) fusion(bf16[16,64,1024]{2,1,0:T(8,128)(2,1)} %all-gather.8.cloned.1.call-done, f32[16,512,512]{1,2,0:T(8,128)} %get-tuple-element.16, f32[16,512]{1,0:T(8,128)S(1)} %get-tuple-element.15, f32[1,512,3,16,64]{1,4,3,2,0:T(8,128)} %bitcast.78, bf16[1,512,1024]{2,1,0:T(8,128)(2,1)S(1)} %copy-done.2), kind=kOutput, calls=%fused_computation.31 | convolution fusion | flops 1622670848 | bytes 22054912 | tf_op jit(solution)/shard_map/crif,ife->cre/dot_general | solution.py:39
  182.5 10.5 %convolution_convert_fusion = bf16[5376,1024]{1,0:T(8,128)(2,1)S(1)} fusion(s32[512,5376]{1,0:T(8,128)} %convert_reduce_fusion, bf16[1,512,1024]{2,1,0:T(8,128)(2,1)S(1)} %get-tuple-element.18, f32[1024]{0:T(1024)S(1)} %convert_element_type.90, f32[512]{0:T(512)S(1)} %add_rsqrt_fusion), kind=kOutput, calls=%fused_computation.9 | convolution fusion | flops 5647499264 | bytes 23074816 | tf_op jit(solution)/shard_map/ts,td->sd/dot_general | solution.py:74
  193.0 124.0 %all_to_all.33 = bf16[32,168,1024]{2,1,0:T(8,128)(2,1)S(1)} all-to-all(bf16[32,168,1024]{2,1,0:T(8,128)(2,1)S(1)} %bitcast.75), channel_id=1, replica_groups=mesh['data'=2,'fsdp'=4,'ep'=4] {'ep'}, dimensions={0} | all-to-all | bytes 22020096 | tf_op jit(solution)/shard_map/all_to_all | solution.py:75
  317.0 4.8 copy.36
  321.8 1.0 all-gather.10.cloned.1.call-done
  322.8 13.5 %fusion.55 = f32[8,672,512]{2,1,0:T(8,128)} fusion(bf16[8,672,1024]{2,1,0:T(8,128)(2,1)} %bitcast.73, bf16[8,1024,512]{2,1,0:T(8,128)(2,1)} %all-gather.10.cloned.1.call-done), kind=kOutput, calls=%fused_computation.74 | convolution fusion | flops 5637144576 | bytes 30408704 | tf_op jit(solution)/shard_map/ecd,edf->ecf/dot_general | solution.py:76
  336.3 135.9 %all-gather.12.cloned.1.call-done = bf16[8,1024,512]{2,1,0:T(8,128)(2,1)} async-done(((bf16[8,256,512]{2,1,0:T(8,128)(2,1)}), bf16[8,1024,512]{2,1,0:T(8,128)(2,1)}) %all-gather.12.cloned.1.call-update) | async-done | bytes 8388624 | tf_op jit(solution)/shard_map/all_gather | solution.py:65
  472.2 150.0 %all-gather.14.cloned.1.call-done = bf16[8,512,1024]{2,1,0:T(8,128)(2,1)} async-done(((bf16[8,512,256]{2,1,0:T(8,128)(2,1)}), bf16[8,512,1024]{2,1,0:T(8,128)(2,1)}) %all-gather.14.cloned.1.call-update) | async-done | bytes 8388624 | tf_op jit(solution)/shard_map/all_gather | solution.py:66
  622.2 20.3 %convolution_convert_fusion.1 = bf16[8,672,1024]{2,1,0:T(8,128)(2,1)} fusion(bf16[8,512,1024]{2,1,0:T(8,128)(2,1)} %all-gather.14.cloned.1.call-done, f32[8,672,512]{2,1,0:T(8,128)} %fusion.55, bf16[8,672,1024]{2,1,0:T(8,128)(2,1)} %bitcast.74, bf16[8,1024,512]{2,1,0:T(8,128)(2,1)} %all-gather.12.cloned.1.call-done), kind=kOutput, calls=%fused_computation.15 | convolution fusion | flops 11296309248 | bytes 49807360 | tf_op jit(solution)/shard_map/ecf,efd->ecd/dot_general | solution.py:79
  642.5 25.3 %copy.37 = bf16[8,672,1024]{2,0,1:T(8,128)(2,1)} copy(bf16[8,672,1024]{2,1,0:T(8,128)(2,1)} %convolution_convert_fusion.1) | data formatting | bytes 22020096 | tf_op jit(solution)/shard_map/convert_element_type | solution.py:79
  667.9 0.0 copy-start.5
  667.9 6.5 all-to-all-start.1
  674.4 0.0 copy-done.5
  674.4 0.2 copy.35
  674.6 119.5 %fusion.2 = bf16[512,5376]{1,0:T(8,128)(2,1)} fusion(s32[512,8]{1,0:T(8,128)S(1)} %copy.34, bf16[512,8]{1,0:T(8,128)(2,1)S(1)} %copy.35), kind=kLoop, calls=%fused_computation.4 | loop fusion | flops 63307776 | bytes 5529600 | tf_op jit(solution)/shard_map/reduce_sum | solution.py:52
  794.1 1.0 all-to-all-done.1
  795.1 0.0 copy-start
  795.1 10.7 %copy.39 = bf16[4,8,168,1024]{3,2,1,0:T(8,128)(2,1)S(1)} copy(bf16[4,8,168,1024]{3,1,2,0:T(8,128)(2,1)} %bitcast.28) | data formatting | bytes 22020096 | tf_op jit(solution)/shard_map/all_to_all | solution.py:80
  805.9 0.0 copy-done
  805.9 6.8 fusion.25
  (6 shorter events, 0.0 us)
Async XLA Ops:
  6.5 4.2 copy-start.2
  6.5 4.5 copy-start.6
  6.5 4.8 copy-start.4
  6.5 4.8 copy-start.3
  6.5 120.8 %all-gather.6.cloned.1.call-start = ((), (), s32[]{:S(2)}) async-start(), calls=%async_computation.2 | async-start | bytes 7864320 | tf_op jit(solution)/shard_map/all_gather | solution.py:61
  7.3 165.4 %all-gather.8.cloned.1.call-start = ((), (), s32[]{:S(2)}) async-start(), calls=%async_computation.3 | async-start | bytes 2621440 | tf_op jit(solution)/shard_map/all_gather | solution.py:62
  8.0 314.8 %all-gather.10.cloned.1.call-start = ((), (), s32[]{:S(2)}) async-start(), calls=%async_computation.4 | async-start | bytes 10485760 | tf_op jit(solution)/shard_map/all_gather | solution.py:64
  8.8 115.0 %copy-start.7 = (bf16[1024]{0:T(1024)(128)(2,1)S(1)}, bf16[1024]{0:T(1024)(128)(2,1)}, u32[]{:S(2)}) copy-start(bf16[1024]{0:T(1024)(128)(2,1)} %param.18) | copy-start | bytes 6148
  8.8 463.4 %all-gather.12.cloned.1.call-start = ((), (), s32[]{:S(2)}) async-start(), calls=%async_computation.5 | async-start | bytes 10485760 | tf_op jit(solution)/shard_map/all_gather | solution.py:65
  9.3 612.9 %all-gather.14.cloned.1.call-start = ((), (), s32[]{:S(2)}) async-start(), calls=%async_computation.6 | async-start | bytes 10485760 | tf_op jit(solution)/shard_map/all_gather | solution.py:66
  133.1 3.0 copy-start.1
  667.9 6.5 copy-start.5
  667.9 127.2 %all-to-all-start.1 = ((bf16[8,672,1024]{2,0,1:T(8,128)(2,1)}), bf16[8,672,1024]{2,0,1:T(8,128)(2,1)}, u32[]{:S(2)}, u32[]{:S(2)}) async-start(bf16[8,672,1024]{2,0,1:T(8,128)(2,1)} %copy.37), calls=%async_computation.1 | async-start | bytes 22020096 | tf_op jit(solution)/shard_map/all_to_all | solution.py:80
  795.1 10.7 %copy-start = (bf16[512,5376]{1,0:T(8,128)(2,1)S(1)}, bf16[512,5376]{1,0:T(8,128)(2,1)}, u32[]{:S(2)}) copy-start(bf16[512,5376]{1,0:T(8,128)(2,1)} %fusion.2) | copy-start | bytes 16515076
Sparse Core Ops, SparseCore 0:
  8.9 118.4 all-gather.5
  128.9 43.7 all-gather.7
  174.3 148.4 all-gather.9
  324.2 147.8 all-gather.11
  473.6 148.5 all-gather.13
where the time goes:
time: 828 us; the launch traced here: 820 us
  waiting for transfers between devices  310 us (37%)
  other arithmetic  234 us (28%)
  blocking collectives  124 us (15%)
  matrix products  88 us (11%)
  local copies, waits for them, and re-layouts  43.3 us (5%)
  between operations  13.7 us (2%)
    all_gather x1, waiting for transfers between devices, local_step(): w_down = lax.all_gather(down_shard, 'fsdp', axis=2, tiled=True)  150 us
    all_gather x1, waiting for transfers between devices, local_step(): w_up = lax.all_gather(up_shard, 'fsdp', axis=1, tiled=True)  136 us
    all_to_all x1, blocking collectives, local_step(): lax.all_to_all(send_buf.reshape(experts, capacity, d_model), 'ep', 0, 1,...  124 us
    reduce_sum x1, other arithmetic, route_tables(): jnp.sum(jnp.where(slot_match, gate_blk[..., None], jnp.zeros((), jnp.bflo...  120 us
    reduce_sum x1, other arithmetic, route_tables(): dispatch = jnp.sum(slot_match, axis=-2).astype(jnp.bfloat16)  112 us
    convert_element_type x1, local copies, waits for them, and re-layouts, local_step(): jnp.einsum('ecf,efd->ecd', inner_act, w_down, preferred_element_type=jnp....  25.3 us
    sub x1, matrix products, attention_block(): jax.nn.softmax(jnp.where(causal, scores, -1e+30), axis=-1)  21.3 us
    dot_general x1, matrix products, local_step(): jnp.einsum('ecf,efd->ecd', inner_act, w_down, preferred_element_type=jnp....  20.3 us
  transfers between devices with their start and end apart: 6, of which 6 were waited for; matrix products, arithmetic and copies ran while one was open for 37% of the time, Pallas kernels for 0%

commit v1 on v0

v1 whole, which is shorter than its diff:
```python
import functools

import jax
import jax.numpy as jnp
from jax import lax
from jax.experimental import pallas as pl
from jax.experimental.pallas import tpu as pltpu
from jax.sharding import PartitionSpec as P

NORM_EPS = 1e-6
ROPE_BASE = 10000.0
MESH_ID = pl.DeviceIdType.MESH
VMEM_LIMIT = 60 * 1024 * 1024


def rms_norm(hidden, gain_vec):
    wide = hidden.astype(jnp.float32)
    inv_rms = lax.rsqrt(jnp.mean(wide * wide, axis=-1, keepdims=True) + NORM_EPS)
    return (wide * inv_rms * gain_vec.astype(jnp.float32)).astype(jnp.bfloat16)


def attention_block(x_blk, attn_gain, w_qkv, w_out):
    seq_len = x_blk.shape[1]
    head_dim = w_qkv.shape[3]
    half_dim = head_dim // 2
    normed = rms_norm(x_blk, attn_gain)
    qkv_proj = jnp.einsum('bsd,dthe->bsthe', normed, w_qkv, preferred_element_type=jnp.float32)
    inv_freq = ROPE_BASE ** (-jnp.arange(half_dim, dtype=jnp.float32) / half_dim)
    angles = jnp.arange(seq_len, dtype=jnp.float32)[:, None] * inv_freq[None, :]
    cos_tab = jnp.cos(angles)[None, :, None, :]
    sin_tab = jnp.sin(angles)[None, :, None, :]

    def rotate(heads_in):
        first_half = heads_in[..., :half_dim]
        second_half = heads_in[..., half_dim:]
        return jnp.concatenate([first_half * cos_tab - second_half * sin_tab, second_half * cos_tab + first_half * sin_tab], axis=-1)

    query_rot = rotate(qkv_proj[:, :, 0]).astype(jnp.bfloat16)
    keys_rot = rotate(qkv_proj[:, :, 1]).astype(jnp.bfloat16)
    values = qkv_proj[:, :, 2].astype(jnp.bfloat16)
    scores = jnp.einsum('bqhe,bkhe->bhqk', query_rot, keys_rot, preferred_element_type=jnp.float32) * (head_dim ** -0.5)
    causal = jnp.arange(seq_len)[:, None] >= jnp.arange(seq_len)[None, :]
    attn_probs = jax.nn.softmax(jnp.where(causal, scores, -1e30), axis=-1).astype(jnp.bfloat16)
    context = jnp.einsum('bhqk,bkhe->bqhe', attn_probs, values, preferred_element_type=jnp.float32).astype(jnp.bfloat16)
    attn_out = jnp.einsum('crif,ife->cre', context, w_out, preferred_element_type=jnp.float32)
    return (x_blk.astype(jnp.float32) + attn_out).astype(jnp.bfloat16)


def capacity_of(tok_count, top_k, experts):
    return 8 * ((5 * tok_count * top_k) // (32 * experts) + 1)


def layer_place():
    dx, dz, ep = lax.axis_index('data'), lax.axis_index('fsdp'), lax.axis_index('ep')
    return dx, dz, ep // 2, ep % 2


def flip(pos, bit):
    return (1 - pos) if bit else pos


def related(place, chip_rel, core_rel):
    dx, dz, dy, dc = place
    return flip(dx, chip_rel & 1), dz, flip(dy, chip_rel & 2), flip(dc, core_rel)


def slot_of(place):
    dx, _, dy, dc = place
    return dx * 4 + dy * 2 + dc


def dev_id(place):
    dx, dz, dy, dc = place
    return (dx, dz, dy * 2 + dc)


def greet(places):
    barrier = pltpu.get_barrier_semaphore()
    for place in places:
        pl.semaphore_signal(barrier, inc=1, device_id=dev_id(place), device_id_type=MESH_ID)
    pl.semaphore_wait(barrier, len(places))


class Sender:
    def __init__(self, send_sems):
        self.send_sems = send_sems
        self.copies = []

    def send(self, src, dst, recv_sem, place):
        copy = pltpu.make_async_remote_copy(src_ref=src, dst_ref=dst, send_sem=self.send_sems.at[len(self.copies)], recv_sem=recv_sem, device_id=dev_id(place), device_id_type=MESH_ID)
        copy.start()
        self.copies.append(copy)
        return copy

    def drain(self):
        for copy in self.copies:
            copy.wait_send()


def wait_in(ref, sem):
    pltpu.make_async_copy(ref, ref, sem).wait()


def spread_in_layer(place, sender, own_src, part_ref, recv_sems):
    across_x, across_y, partner = related(place, 1, 0), related(place, 2, 0), related(place, 0, 1)
    mine = slot_of(place)

    def pass_on(chip_rel, half, target, rel_there, core_there, first=False):
        owner = slot_of(related(place, chip_rel, 0))
        src = own_src(half) if first else part_ref(owner, half)
        sender.send(src, part_ref(owner, half), recv_sems(rel_there, core_there, half), target)

    for half in (0, 1):
        pass_on(0, half, across_x, 1, 0, True)
        pass_on(0, 1 - half, across_y, 2, 0, True)
    for half in (0, 1):
        pass_on(0, half, partner, 0, 1, True)
    yield

    def arrived(chip_rel, core_rel, half):
        owner = slot_of(related(place, chip_rel, core_rel))
        wait_in(part_ref(owner, half), recv_sems(chip_rel, core_rel, half))

    arrived(1, 0, 0)
    pass_on(1, 0, across_y, 3, 0)
    pass_on(1, 0, partner, 1, 1)
    arrived(2, 0, 1)
    pass_on(2, 1, across_x, 3, 0)
    pass_on(2, 1, partner, 2, 1)
    yield
    arrived(1, 0, 1)
    pass_on(1, 1, partner, 1, 1)
    arrived(2, 0, 0)
    pass_on(2, 0, partner, 2, 1)
    yield
    arrived(3, 0, 0)
    pass_on(3, 0, partner, 3, 1)
    arrived(3, 0, 1)
    pass_on(3, 1, partner, 3, 1)
    yield
    for chip_rel in range(4):
        for half in (0, 1):
            arrived(chip_rel, 1, half)
    yield


def attn_gather_kernel(shard_ref, out_ref, send_sems, z_sems, recv_sems, own_sem):
    place = layer_place()
    dx, dz, dy, dc = place
    rows = shard_ref.shape[0]
    piece = rows // 8
    z_peers = [(dx, (dz + step) % 4, dy, dc) for step in (1, 2, 3)]
    layer_peers = [related(place, 1, 0), related(place, 2, 0), related(place, 0, 1)]
    greet(z_peers + layer_peers)
    sender = Sender(send_sems)
    mine = slot_of(place)
    my_rows = pl.ds(pl.multiple_of(mine * piece, piece), piece)
    for index, step in enumerate((1, 3, 2)):
        target = (dx, (dz + step) % 4, dy, dc)
        dst = out_ref.at[pl.ds(pl.multiple_of(dz * rows + mine * piece, piece), piece)]
        sender.send(shard_ref.at[my_rows], dst, z_sems.at[index], target)
    own = pltpu.make_async_copy(shard_ref, out_ref.at[pl.ds(pl.multiple_of(dz * rows, rows), rows)], own_sem)
    own.start()
    streams = []
    for index, step in enumerate((1, 3, 2)):
        source_z = (dz + 4 - step) % 4

        def part_ref(slot, half, source_z=source_z):
            start = source_z * rows + slot * piece + half * (piece // 2)
            return out_ref.at[pl.ds(pl.multiple_of(start, piece // 2), piece // 2)]

        def recv_sem(chip_rel, core_rel, half, index=index):
            return recv_sems.at[index, chip_rel, core_rel, half]

        whole = out_ref.at[pl.ds(pl.multiple_of(source_z * rows + mine * piece, piece), piece)]
        streams.append((whole, index, spread_in_layer(place, sender, functools.partial(part_ref, mine), part_ref, recv_sem)))
    for whole, index, stream in streams:
        wait_in(whole, z_sems.at[index])
        next(stream)
    for _ in range(4):
        for _, _, stream in streams:
            next(stream)
    own.wait()
    sender.drain()


def gather_attention_weights(shard):
    rows, cols = shard.shape
    n_send = 3 + 3 * 14
    return pl.pallas_call(
        attn_gather_kernel,
        out_shape=jax.ShapeDtypeStruct((4 * rows, cols), shard.dtype),
        in_specs=[pl.BlockSpec(memory_space=pltpu.VMEM)],
        out_specs=pl.BlockSpec(memory_space=pl.ANY),
        scratch_shapes=[
            pltpu.SemaphoreType.DMA((n_send,)),
            pltpu.SemaphoreType.DMA((3,)),
            pltpu.SemaphoreType.DMA((3, 4, 2, 2)),
            pltpu.SemaphoreType.DMA,
        ],
        compiler_params=pltpu.CompilerParams(collective_id=1, has_side_effects=True, vmem_limit_bytes=VMEM_LIMIT),
        cost_estimate=pl.CostEstimate(flops=30_000_000_000, bytes_accessed=10_000_000, transcendentals=0),
        name='attn_gather',
    )(shard)


def token_gather_kernel(own_ref, out_ref, send_sems, recv_sems, own_sem):
    place = layer_place()
    greet([related(place, 1, 0), related(place, 2, 0), related(place, 0, 1)])
    sender = Sender(send_sems)
    half_rows = own_ref.shape[0] // 2

    def part_ref(slot, half):
        return out_ref.at[slot, pl.ds(half * half_rows, half_rows)]

    def own_half(half):
        return own_ref.at[pl.ds(half * half_rows, half_rows)]

    def recv_sem(chip_rel, core_rel, half):
        return recv_sems.at[chip_rel, core_rel, half]

    stream = spread_in_layer(place, sender, own_half, part_ref, recv_sem)
    next(stream)
    own = pltpu.make_async_copy(own_ref, out_ref.at[slot_of(place)], own_sem)
    own.start()
    for _ in range(4):
        next(stream)
    own.wait()
    sender.drain()


def gather_tokens(own):
    rows, cols = own.shape
    return pl.pallas_call(
        token_gather_kernel,
        out_shape=jax.ShapeDtypeStruct((8, rows, cols), own.dtype),
        in_specs=[pl.BlockSpec(memory_space=pltpu.VMEM)],
        out_specs=pl.BlockSpec(memory_space=pl.ANY),
        scratch_shapes=[
            pltpu.SemaphoreType.DMA((14,)),
            pltpu.SemaphoreType.DMA((4, 2, 2)),
            pltpu.SemaphoreType.DMA,
        ],
        compiler_params=pltpu.CompilerParams(collective_id=2, has_side_effects=True, vmem_limit_bytes=VMEM_LIMIT),
        cost_estimate=pl.CostEstimate(flops=30_000_000_000, bytes_accessed=10_000_000, transcendentals=0),
        name='token_gather',
    )(own)


def dispatch_kernel(capacity, u_ref, slot_row_ref, slot_col_ref, gate_col_ref, rows_ref, comb_ref):
    tokens = u_ref.shape[0]
    n_exp = slot_row_ref.shape[0]
    slot_ids = lax.broadcasted_iota(jnp.int32, (capacity, tokens), 0).astype(jnp.float32)
    for e in range(n_exp):
        one_hot = jnp.where(slot_ids == slot_row_ref[e:e + 1, :], 1.0, 0.0).astype(jnp.bfloat16)
        rows_ref[e] = jnp.dot(one_hot, u_ref[...], preferred_element_type=jnp.float32).astype(jnp.bfloat16)
    buf_ids = lax.broadcasted_iota(jnp.int32, (tokens, n_exp * capacity), 1).astype(jnp.float32)
    comb = jnp.zeros((tokens, n_exp * capacity), jnp.float32)
    for e in range(n_exp):
        slot_e = slot_col_ref[:, e:e + 1]
        dest_e = jnp.where(slot_e >= 0.0, slot_e + float(e * capacity), -1.0)
        comb = jnp.where(buf_ids == dest_e, gate_col_ref[:, e:e + 1], comb)
    comb_ref[...] = comb.astype(jnp.bfloat16)


def dispatch(gathered, slot_row, slot_col, gate_col, tokens, capacity):
    n_src, _, cols = gathered.shape
    n_exp = slot_row.shape[1]
    return pl.pallas_call(
        functools.partial(dispatch_kernel, capacity),
        grid=(n_src,),
        out_shape=(
            jax.ShapeDtypeStruct((n_exp, n_src, capacity, cols), jnp.bfloat16),
            jax.ShapeDtypeStruct((n_src, tokens, n_exp * capacity), jnp.bfloat16),
        ),
        in_specs=[
            pl.BlockSpec((None, tokens, cols), lambda s: (s, 0, 0)),
            pl.BlockSpec((None, n_exp, tokens), lambda s: (s, 0, 0)),
            pl.BlockSpec((None, tokens, n_exp), lambda s: (s, 0, 0)),
            pl.BlockSpec((None, tokens, n_exp), lambda s: (s, 0, 0)),
        ],
        out_specs=(
            pl.BlockSpec((n_exp, None, capacity, cols), lambda s: (0, s, 0, 0)),
            pl.BlockSpec((None, tokens, n_exp * capacity), lambda s: (s, 0, 0)),
        ),
        compiler_params=pltpu.CompilerParams(vmem_limit_bytes=VMEM_LIMIT),
        cost_estimate=pl.CostEstimate(flops=10_000_000_000, bytes_accessed=30_000_000, transcendentals=0),
        name='dispatch',
    )(gathered, slot_row, slot_col, gate_col)


def inner_kernel(rows_ref, gate_ref, up_ref, inner_ref):
    depth = rows_ref.shape[-1]
    gate_w = gate_ref[...].reshape(depth, gate_ref.shape[-1])
    up_w = up_ref[...].reshape(depth, up_ref.shape[-1])
    gate_act = jnp.dot(rows_ref[...], gate_w, preferred_element_type=jnp.float32)
    up_act = jnp.dot(rows_ref[...], up_w, preferred_element_type=jnp.float32)
    inner_ref[...] = (gate_act * jax.nn.sigmoid(gate_act) * up_act).astype(jnp.bfloat16)


def expert_inner(rows, w_gate, w_up):
    n_exp, n_src, capacity, depth = rows.shape
    parts, _, part_depth, ffn = w_gate.shape
    tall = rows.reshape(n_exp, n_src * capacity, depth)
    tile = n_src * capacity // 2
    weight_spec = pl.BlockSpec((parts, None, part_depth, ffn), lambda e, t: (0, e, 0, 0))
    return pl.pallas_call(
        inner_kernel,
        grid=(n_exp, 2),
        out_shape=jax.ShapeDtypeStruct((n_exp, n_src * capacity, ffn), jnp.bfloat16),
        in_specs=[pl.BlockSpec((None, tile, depth), lambda e, t: (e, t, 0)), weight_spec, weight_spec],
        out_specs=pl.BlockSpec((None, tile, ffn), lambda e, t: (e, t, 0)),
        compiler_params=pltpu.CompilerParams(vmem_limit_bytes=VMEM_LIMIT),
        cost_estimate=pl.CostEstimate(flops=12_000_000_000, bytes_accessed=30_000_000, transcendentals=0),
        name='expert_inner',
    )(tall, w_gate, w_up)


def back_kernel(capacity, inner_ref, comb_ref, down_ref, out_ref, wide_w, y_buf, send_core, got_core, acc, got_x, got_y, got_last, send_sems, core_sems, x_sems, y_sems, last_sems):
    place = layer_place()
    across_x, across_y, partner = related(place, 1, 0), related(place, 2, 0), related(place, 0, 1)
    greet([across_x, across_y, partner])
    sender = Sender(send_sems)
    n_exp, n_rows, ffn = inner_ref.shape
    parts, _, _, part_cols = down_ref.shape
    n_src = n_rows // capacity
    for p in range(parts):
        wide_w[:, :, p * part_cols:(p + 1) * part_cols] = down_ref[p]
    for e in range(n_exp):
        y_tall = jnp.dot(inner_ref[e], wide_w[e], preferred_element_type=jnp.float32).astype(jnp.bfloat16)
        for s in range(n_src):
            y_buf[s, e * capacity:(e + 1) * capacity, :] = y_tall[s * capacity:(s + 1) * capacity]
    half_cols = acc.shape[-1]

    def partial(chip_rel, core_rel, half):
        slot = slot_of(related(place, chip_rel, core_rel))
        cols = pl.ds(half * half_cols, half_cols)
        return jnp.dot(comb_ref[slot], y_buf[slot, :, cols], preferred_element_type=jnp.float32)

    order = (3, 1, 2, 0)
    for chip_rel in order:
        for half in (0, 1):
            send_core[chip_rel, half] = partial(chip_rel, 1, half)
            sender.send(send_core.at[chip_rel, half], got_core.at[chip_rel, half], core_sems.at[chip_rel, half], partner)
    for chip_rel in order:
        for half in (0, 1):
            mine = partial(chip_rel, 0, half)
            wait_in(got_core.at[chip_rel, half], core_sems.at[chip_rel, half])
            acc[chip_rel, half] = mine + got_core[chip_rel, half]
            if chip_rel & 1 and half == 0:
                where = 0 if chip_rel == 3 else 1
                sender.send(acc.at[chip_rel, 0], got_x.at[where], x_sems.at[where], across_x)
            if chip_rel & 2 and half == 1:
                where = 0 if chip_rel == 3 else 1
                sender.send(acc.at[chip_rel, 1], got_y.at[where], y_sems.at[where], across_y)
    wait_in(got_x.at[0], x_sems.at[0])
    acc[2, 0] += got_x[0]
    sender.send(acc.at[2, 0], got_last.at[0], last_sems.at[0], across_y)
    wait_in(got_y.at[0], y_sems.at[0])
    acc[1, 1] += got_y[0]
    sender.send(acc.at[1, 1], got_last.at[1], last_sems.at[1], across_x)
    wait_in(got_x.at[1], x_sems.at[1])
    wait_in(got_y.at[1], y_sems.at[1])
    wait_in(got_last.at[0], last_sems.at[0])
    out_ref[:, :half_cols] = acc[0, 0] + got_x[1] + got_last[0]
    wait_in(got_last.at[1], last_sems.at[1])
    out_ref[:, half_cols:] = acc[0, 1] + got_y[1] + got_last[1]
    sender.drain()


def expert_back(inner, comb, down, capacity, collective_id):
    n_exp, n_rows, ffn = inner.shape
    parts, _, _, part_cols = down.shape
    n_src, tokens, buf_rows = comb.shape
    cols = parts * part_cols
    half = (tokens, cols // 2)
    return pl.pallas_call(
        functools.partial(back_kernel, capacity),
        out_shape=jax.ShapeDtypeStruct((tokens, cols), jnp.float32),
        in_specs=[pl.BlockSpec(memory_space=pltpu.VMEM)] * 3,
        out_specs=pl.BlockSpec(memory_space=pltpu.VMEM),
        scratch_shapes=[
            pltpu.VMEM((n_exp, ffn, cols), jnp.bfloat16),
            pltpu.VMEM((n_src, buf_rows, cols), jnp.bfloat16),
            pltpu.VMEM((4, 2) + half, jnp.float32),
            pltpu.VMEM((4, 2) + half, jnp.float32),
            pltpu.VMEM((4, 2) + half, jnp.float32),
            pltpu.VMEM((2,) + half, jnp.float32),
            pltpu.VMEM((2,) + half, jnp.float32),
            pltpu.VMEM((2,) + half, jnp.float32),
            pltpu.SemaphoreType.DMA((14,)),
            pltpu.SemaphoreType.DMA((4, 2)),
            pltpu.SemaphoreType.DMA((2,)),
            pltpu.SemaphoreType.DMA((2,)),
            pltpu.SemaphoreType.DMA((2,)),
        ],
        compiler_params=pltpu.CompilerParams(collective_id=collective_id, has_side_effects=True, vmem_limit_bytes=VMEM_LIMIT),
        cost_estimate=pl.CostEstimate(flops=30_000_000_000, bytes_accessed=30_000_000, transcendentals=0),
        name='expert_back',
    )(inner, comb, down)


def solution(mesh):
    tok_spec = P(('data', 'fsdp', 'ep'), None, None)

    def local_step(x_blk, idx_blk, slot_blk, gate_blk, attn_gain, qkv_shard, out_shard, moe_gain, gate_shard, up_shard, down_shard):
        batch_rows, seq_len, d_model = x_blk.shape
        tokens = batch_rows * seq_len
        top_k = idx_blk.shape[-1]
        here = gate_shard.shape[0] // 2
        experts = gate_shard.shape[0] * lax.axis_size('ep')
        capacity = capacity_of(tokens, top_k, experts)
        first = lax.axis_index('data') * here
        gate_half = lax.dynamic_slice_in_dim(gate_shard, first, here, 0)
        up_half = lax.dynamic_slice_in_dim(up_shard, first, here, 0)
        down_half = lax.dynamic_slice_in_dim(down_shard, first, here, 0)
        mid = down_half.shape[2] // 2
        w_gate = lax.all_gather(gate_half, 'fsdp')
        w_up = lax.all_gather(up_half, 'fsdp')
        w_down = [lax.all_gather(down_half[:, :, :mid], 'fsdp'), lax.all_gather(down_half[:, :, mid:], 'fsdp')]

        _, triple, heads, head_dim = qkv_shard.shape
        width = heads * head_dim
        flat_shard = jnp.concatenate([qkv_shard.reshape(-1, triple * width), out_shard.reshape(-1, d_model)], axis=1)
        flat = gather_attention_weights(flat_shard)
        w_qkv = flat[:, :triple * width].reshape(d_model, triple, heads, head_dim)
        w_out = flat[:, triple * width:].reshape(heads, head_dim, d_model)
        hidden = attention_block(x_blk, attn_gain, w_qkv, w_out)
        normed = rms_norm(hidden, moe_gain).reshape(tokens, d_model)

        idx_t = idx_blk.reshape(tokens, top_k).T[:, None, :]
        slot_t = slot_blk.reshape(tokens, top_k).T[:, None, :].astype(jnp.float32)
        gate_t = gate_blk.reshape(tokens, top_k).T[:, None, :].astype(jnp.float32)
        hits = idx_t == jnp.arange(experts, dtype=jnp.int32)[None, :, None]
        slot_tab = jnp.sum(jnp.where(hits, slot_t + 1.0, 0.0), axis=0) - 1.0
        gate_tab = jnp.sum(jnp.where(hits, gate_t, 0.0), axis=0)
        tables = jnp.concatenate([slot_tab, gate_tab], axis=1).astype(jnp.bfloat16)
        gathered = gather_tokens(jnp.concatenate([normed, tables], axis=0))
        my_first = lax.axis_index('ep') * gate_shard.shape[0] + first
        my_tables = lax.dynamic_slice_in_dim(gathered[:, tokens:], my_first, here, 1).astype(jnp.float32)
        slot_row = my_tables[:, :, :tokens]
        slot_col = slot_row.transpose(0, 2, 1)
        gate_col = my_tables[:, :, tokens:].transpose(0, 2, 1)
        rows, comb = dispatch(gathered, slot_row, slot_col, gate_col, tokens, capacity)

        inner = expert_inner(rows, w_gate, w_up)
        sums = [expert_back(inner, comb, w_down[i], capacity, 3 + i) for i in range(2)]
        parts = w_down[0].shape[0]
        moe_sum = jnp.stack([part.reshape(tokens, parts, mid) for part in sums], axis=2).reshape(tokens, d_model)
        result = hidden.reshape(tokens, d_model).astype(jnp.float32) + moe_sum
        return result.astype(jnp.bfloat16).reshape(batch_rows, seq_len, d_model)

    return jax.shard_map(local_step, mesh=mesh, in_specs=(tok_spec, tok_spec, tok_spec, tok_spec, P(None), P('fsdp', None, None, None), P('fsdp', None, None), P(None), P('ep', 'fsdp', None), P('ep', 'fsdp', None), P('ep', None, 'fsdp')), out_specs=tok_spec, check_vma=False)
```

time: 828 us -> 368 us (0.44)
  waiting for transfers between devices: 310 us -> 24.1 us
  Pallas kernels: 0 us -> 257 us
  other arithmetic: 234 us -> 12.6 us
  blocking collectives: 124 us -> 0 us
  matrix products: 88 us -> 25.2 us
    all_gather x5 -> x4, waiting for transfers between devices: 306 us -> 23.5 us  [the longest x1 23.5 us: local_step(): lax.all_gather(down_half[:, :, mid:], 'fsdp')]
    pallas_call x0 -> x6, Pallas kernels: none -> 257 us  [the longest x2 103 us: expert_back(): pl.pallas_call(functools.partial(back_kernel, capacity), out_shape=jax.Sh...]
    reduce_sum x2 -> x1, other arithmetic: 232 us -> 0.09 us  [local_step(): slot_tab = jnp.sum(jnp.where(hits, slot_t + 1.0, 0.0), axis=0) - 1.0]
    all_to_all x1 -> x0, blocking collectives: 124 us -> none  [local_step(): lax.all_to_all(send_buf.reshape(experts, capacity, d_model), 'ep', 0, 1,...]
    dot_general x4 -> x0, matrix products: 51.1 us -> none  [the longest x1 20.3 us: local_step(): jnp.einsum('ecf,efd->ecd', inner_act, w_down, preferred_element_type=jnp....]
    convert_element_type x1 -> x0, local copies, waits for them, and re-layouts: 25.3 us -> none  [local_step(): jnp.einsum('ecf,efd->ecd', inner_act, w_down, preferred_element_type=jnp....]
    all_to_all x2 -> x0, local copies, waits for them, and re-layouts: 15.5 us -> none  [the longest x1 10.7 us: local_step(): lax.all_to_all(expert_out, 'ep', 1, 0, tiled=True)]
    sub x1, matrix products: 21.3 us -> 10.8 us  [attention_block(): jax.nn.softmax(jnp.where(causal, scores, -1e+30), axis=-1)]
  transfers between devices with their start and end apart: 6 -> 4, of which waited for: 6 -> 1; matrix products, arithmetic and copies ran while one was open for 37% -> 14% of each run, Pallas kernels for 0% -> 56%
where the time goes in v1:
time: 368 us; the launch traced here: 367 us
  Pallas kernels  257 us (70%)
  local copies, waits for them, and re-layouts  35.2 us (10%)
  matrix products  25.2 us (7%)
  waiting for transfers between devices  24.1 us (7%)
  between operations  13.4 us (4%)
  other arithmetic  12.6 us (3%)
    pallas_call x2, Pallas kernels, expert_back(): pl.pallas_call(functools.partial(back_kernel, capacity), out_shape=jax.Sh...  103 us
    pallas_call x1, Pallas kernels, gather_attention_weights(): pl.pallas_call(attn_gather_kernel, out_shape=jax.ShapeDtypeStruct((4 * ro...  76.3 us
    pallas_call x1, Pallas kernels, gather_tokens(): pl.pallas_call(token_gather_kernel, out_shape=jax.ShapeDtypeStruct((8, ro...  42.7 us
    all_gather x1, waiting for transfers between devices, local_step(): lax.all_gather(down_half[:, :, mid:], 'fsdp')  23.5 us
    pallas_call x1, Pallas kernels, expert_inner(): pl.pallas_call(inner_kernel, grid=(n_exp, 2), out_shape=jax.ShapeDtypeStr...  17.5 us
    pallas_call x1, Pallas kernels, dispatch(): pl.pallas_call(functools.partial(dispatch_kernel, capacity), grid=(n_src,...  17 us
    sub x1, matrix products, attention_block(): jax.nn.softmax(jnp.where(causal, scores, -1e+30), axis=-1)  10.8 us
    dot_general x1, matrix products, attention_block(): jnp.einsum('crif,ife->cre', context, w_out, preferred_element_type=jnp.fl...  8.59 us
  transfers between devices with their start and end apart: 4, of which 1 were waited for; matrix products, arithmetic and copies ran while one was open for 14% of the time, Pallas kernels for 56%

profile of v1, /device:TPU:0, one launch (start us, length us, event | category | flops | bytes accessed | tf_op | source)
XLA Modules:
  0.0 367.3 jit_solution(11745554407425853383)
XLA Ops:
  6.5 0.0 copy-start
  6.5 0.0 all-gather.9.cloned.1.call-start
  6.5 1.6 copy-done
  8.1 1.0 constant_dynamic-slice_fusion.3
  9.2 0.0 copy-start.4
  9.2 0.0 all-gather.9.cloned.1.call-update
  9.2 0.0 all-gather.11.cloned.1.call-start
  9.2 2.4 constant_dynamic-slice_fusion.2
  11.6 0.0 copy-start.7
  11.6 0.0 all-gather.11.cloned.1.call-update
  11.7 0.0 all-gather.15.cloned.1.call-start
  11.7 0.0 copy-done.4
  11.7 1.2 constant_dynamic-slice_fusion
  12.9 0.0 all-gather.15.cloned.1.call-update
  12.9 0.0 all-gather.13.cloned.1.call-start
  13.0 0.0 copy-start.5
  13.0 0.5 all-gather.13.cloned.1.call-update
  13.5 0.1 iota_compare_fusion
  13.6 0.0 copy-done.7
  13.6 0.0 copy-done.8
  13.6 0.0 copy-done.6
  13.6 0.1 select_reduce_fusion.1
  13.8 1.7 copy.30
  15.5 0.0 copy-done.5
  15.5 1.5 pad_maximum_fusion.shard_ref
  17.0 76.3 %attn_gather.1 = bf16[1024,4096]{1,0:T(8,128)(2,1)} custom-call(bf16[256,4096]{1,0:T(8,128)(2,1)} %pad_maximum_fusion.shard_ref), custom_call_target="tpu_custom_call" | custom-call | flops 30000001024 | bytes 10000000 | tf_op jit(solution)/shard_map/attn_gather/pallas_call | solution.py:190
  93.3 0.0 copy-start.9
  93.4 0.0 copy-start.3
  93.4 0.7 copy-done.9
  94.0 0.6 copy-done.3
  94.6 0.3 fusion.8
  94.9 5.8 %fusion.6 = f32[512,3072]{0,1:S(1)} fusion(bf16[1024,4096]{1,0:T(8,128)(2,1)} %attn_gather.1, bf16[1,512,1024]{2,1,0:T(8,128)(2,1)S(1)} %copy-done.3, f32[1024]{0:T(1024)S(1)} %convert_element_type.77, f32[512]{0:T(512)S(1)} %add_rsqrt_fusion.1), kind=kOutput, calls=%fused_computation.9 | convolution fusion | flops 3223322624 | bytes 13637632
  100.7 0.0 copy-start.2
  100.7 0.0 copy-start.10
  100.7 0.7 slice_bitcast_fusion.2
  101.4 2.0 copy-done.2
  103.4 0.3 fusion.34
  103.7 0.0 copy-done.10
  103.8 1.6 fusion.29
  105.4 10.8 %fusion.41 = (f32[16,512]{1,0:T(8,128)S(1)}, f32[16,512,512]{1,2,0:T(8,128)}) fusion(pred[512,512]{0,1:T(8,128)(4,1)S(1)} %iota_compare_fusion, bf16[512,16,32]{0,2,1:T(8,128)(2,1)} %get-tuple-element.21, bf16[512,16,32]{0,2,1:T(8,128)(2,1)} %get-tuple-element.22, bf16[512,16,32]{0,2,1:T(8,128)(2,1)S(1)} %get-tuple-element.16, ...), kind=kOutput, calls=%fused_computation.74 | convolution fusion | flops 557842944 | bytes 19169280 | tf_op jit(solution)/shard_map/sub | solution.py:43
  116.2 0.0 slice-done
  116.2 8.6 %fusion.12 = (f32[512]{0:T(512)S(1)}, bf16[1,512,1024]{2,1,0:T(8,128)(2,1)S(1)}) fusion(bf16[16,64,1024]{2,1,0:T(8,128)(2,1)S(1)} %bitcast.69, f32[16,512,512]{1,2,0:T(8,128)} %get-tuple-element.26, f32[16,512]{1,0:T(8,128)S(1)} %get-tuple-element.25, f32[1,512,3,16,64]{1,4,3,2,0:T(8,128)} %bitcast.68, bf16[1,512,1024]{2,1,0:T(8,128)(2,1)} %param.11), kind=kOutput, calls=%fused_computation.21 | convolution fusion | flops 1622670848 | bytes 22054912 | tf_op jit(solution)/shard_map/crif,ife->cre/dot_general | solution.py:45
  124.8 0.3 fusion.23
  125.1 1.1 maximum_maximum_fusion.own_ref
  126.2 42.7 %token_gather.1.u_ref = bf16[8,544,1024]{2,1,0:T(8,128)(2,1)} custom-call(bf16[544,1024]{1,0:T(8,128)(2,1)} %maximum_maximum_fusion.own_ref), custom_call_target="tpu_custom_call" | custom-call | flops 30000001024 | bytes 10000000 | tf_op jit(solution)/shard_map/token_gather/pallas_call | solution.py:234
  168.9 1.1 slice.52
  170.0 1.1 copy.38
  171.1 1.5 slice.64
  172.6 2.2 convert_element_type.92
  174.9 2.8 copy.34.slot_row_ref
  177.7 4.7 %slice_bitcast_fusion = (f32[8,512,4]{2,1,0:T(8,128)}, f32[8,512,4]{2,1,0:T(8,128)}) fusion(f32[8,4,1024]{1,2,0:T(8,128)} %convert_element_type.92), kind=kLoop, calls=%fused_computation.25 | loop fusion | bytes 262144 | tf_op jit(solution)/shard_map/transpose | solution.py:443
  182.4 17.0 %dispatch.1 = (bf16[4,8,168,1024]{3,2,1,0:T(8,128)(2,1)}, bf16[8,512,672]{2,1,0:T(8,128)(2,1)}) custom-call(bf16[8,544,1024]{2,1,0:T(8,128)(2,1)} %token_gather.1.u_ref, f32[8,4,512]{2,1,0:T(4,128)} %copy.34.slot_row_ref, f32[8,512,4]{2,1,0:T(8,128)} %get-tuple-element.14.slot_col_ref, f32[8,512,4]{2,1,0:T(8,128)} %get-tuple-element.13.gate_col_ref), custom_call_target="tpu_custom_call" | custom-call | flops 10000000000 | bytes 30000000 | tf_op jit(solution)/shard_map/dispatch/pallas_call | solution.py:269
  199.5 0.0 all-gather.11.cloned.1.call-done
  199.5 17.5 %expert_inner.1.inner_ref = bf16[4,1344,512]{2,1,0:T(8,128)(2,1)} custom-call(bf16[4,1344,1024]{2,1,0:T(8,128)(2,1)} %bitcast.77, bf16[4,4,256,512]{3,2,1,0:T(8,128)(2,1)} %bitcast.73, bf16[4,4,256,512]{3,2,1,0:T(8,128)(2,1)} %bitcast.74), custom_call_target="tpu_custom_call" | custom-call | flops 12000000000 | bytes 30000000 | tf_op jit(solution)/shard_map/expert_inner/pallas_call | solution.py:307
  217.0 23.5 %all-gather.15.cloned.1.call-done = bf16[16,512,128]{2,1,0:T(8,128)(2,1)} async-done(((bf16[4,512,128]{2,1,0:T(8,128)(2,1)}), bf16[16,512,128]{2,1,0:T(8,128)(2,1)}) %all-gather.15.cloned.1.call-update) | async-done | bytes 2097168 | tf_op jit(solution)/shard_map/all_gather | solution.py:420
  240.4 51.9 %expert_back.3 = f32[512,512]{1,0:T(8,128)} custom-call(bf16[4,1344,512]{2,1,0:T(8,128)(2,1)} %expert_inner.1.inner_ref, bf16[8,512,672]{2,1,0:T(8,128)(2,1)} %get-tuple-element.8.comb_ref, bf16[4,4,512,128]{3,2,1,0:T(8,128)(2,1)} %bitcast.75), custom_call_target="tpu_custom_call" | custom-call | flops 30000001024 | bytes 30000000 | tf_op jit(solution)/shard_map/expert_back/pallas_call | solution.py:377
  292.3 2.5 stack_reshape.7
  294.9 51.4 %expert_back.2 = f32[512,512]{1,0:T(8,128)} custom-call(bf16[4,1344,512]{2,1,0:T(8,128)(2,1)} %expert_inner.1.inner_ref, bf16[8,512,672]{2,1,0:T(8,128)(2,1)} %get-tuple-element.8.comb_ref, bf16[4,4,512,128]{3,2,1,0:T(8,128)(2,1)} %bitcast.76), custom_call_target="tpu_custom_call" | custom-call | flops 30000001024 | bytes 30000000 | tf_op jit(solution)/shard_map/expert_back/pallas_call | solution.py:377
  346.3 2.5 stack_reshape.6
  348.8 2.0 pad_maximum_fusion.1
  350.8 2.9 copy.35
  353.8 4.1 %reshape.194 = f32[1,512,1024]{2,1,0:T(8,128)} reshape(f32[512,4,2,128]{3,2,1,0:T(2,128)} %copy.35) | data formatting | bytes 4194304 | tf_op jit(solution)/shard_map/reshape | solution.py:449
  357.8 2.9 fusion.15
  360.8 0.0 copy-done.1
  (15 shorter events, 0.1 us)
Async XLA Ops:
  6.5 1.6 copy-start
  6.5 192.9 %all-gather.9.cloned.1.call-start = ((), (), s32[]{:S(2)}) async-start(), calls=%async_computation | async-start | bytes 5242880 | tf_op jit(solution)/shard_map/all_gather | solution.py:418
  9.2 2.6 copy-start.4
  9.2 190.3 %all-gather.11.cloned.1.call-start = ((), (), s32[]{:S(2)}) async-start(), calls=%async_computation.1 | async-start | bytes 5242880 | tf_op jit(solution)/shard_map/all_gather | solution.py:419
  11.6 2.0 copy-start.7
  11.6 2.0 copy-start.8
  11.6 2.0 copy-start.6
  11.7 228.8 %all-gather.15.cloned.1.call-start = ((), (), s32[]{:S(2)}) async-start(), calls=%async_computation.3 | async-start | bytes 2621440 | tf_op jit(solution)/shard_map/all_gather | solution.py:420
  12.9 282.0 %all-gather.13.cloned.1.call-start = ((), (), s32[]{:S(2)}) async-start(), calls=%async_computation.2 | async-start | bytes 2621440 | tf_op jit(solution)/shard_map/all_gather | solution.py:420
  13.0 2.5 copy-start.5
  93.3 0.7 copy-start.9
  93.4 1.2 copy-start.3
  100.7 2.7 copy-start.2
  100.7 3.0 copy-start.10
  105.4 10.8 %slice-start = ((bf16[1024,4096]{1,0:T(8,128)(2,1)}), bf16[1024,1024]{1,0:T(8,128)(2,1)S(1)}, s32[]{:S(2)}) async-start(bf16[1024,4096]{1,0:T(8,128)(2,1)} %attn_gather.1), calls=%async_computation.4 | async-start | bytes 4194304 | tf_op jit(solution)/shard_map/slice | solution.py:427
  353.8 7.0 %copy-start.1 = (bf16[8,256,512]{2,1,0:T(8,128)(2,1)S(1)}, bf16[8,256,512]{2,1,0:T(8,128)(2,1)}, u32[]{:S(2)}) copy-start(bf16[8,256,512]{2,1,0:T(8,128)(2,1)} %param.19) | copy-start | bytes 6291460
Sparse Core Ops, SparseCore 0:
  9.3 105.3 all-gather.8
  116.3 78.5 all-gather.10
  196.4 43.9 all-gather.14
  241.9 44.2 all-gather.12

commit v2 on v1

--- a/solution.py
+++ b/solution.py
@@ -247,157 +247,333 @@
     )(own)
 
 
-def dispatch_kernel(capacity, u_ref, slot_row_ref, slot_col_ref, gate_col_ref, rows_ref, comb_ref):
-    tokens = u_ref.shape[0]
-    n_exp = slot_row_ref.shape[0]
-    slot_ids = lax.broadcasted_iota(jnp.int32, (capacity, tokens), 0).astype(jnp.float32)
+def dispatch_kernel(pad_cap, n_exp, gathered_ref, rows_ref, comb_ref):
+    tokens = comb_ref.shape[0]
+    experts = gathered_ref.shape[0] - tokens
+    first = (lax.axis_index('ep') * 2 + lax.axis_index('data')) * n_exp
+    u = gathered_ref[:tokens]
+    tables = gathered_ref[tokens:]
+    pick_row = (lax.broadcasted_iota(jnp.int32, (8, experts), 1) == first + lax.broadcasted_iota(jnp.int32, (8, experts), 0)).astype(jnp.bfloat16)
+    slot_row = jnp.dot(pick_row, tables, preferred_element_type=jnp.float32)
+    pick_col = (lax.broadcasted_iota(jnp.int32, (experts, 128), 0) == first + lax.broadcasted_iota(jnp.int32, (experts, 128), 1)).astype(jnp.bfloat16)
+    col_tab = lax.dot_general(tables, pick_col, (((0,), (0,)), ((), ())), preferred_element_type=jnp.float32)
+    slot_ids = lax.broadcasted_iota(jnp.int32, (pad_cap, tokens), 0).astype(jnp.float32)
     for e in range(n_exp):
-        one_hot = jnp.where(slot_ids == slot_row_ref[e:e + 1, :], 1.0, 0.0).astype(jnp.bfloat16)
-        rows_ref[e] = jnp.dot(one_hot, u_ref[...], preferred_element_type=jnp.float32).astype(jnp.bfloat16)
-    buf_ids = lax.broadcasted_iota(jnp.int32, (tokens, n_exp * capacity), 1).astype(jnp.float32)
-    comb = jnp.zeros((tokens, n_exp * capacity), jnp.float32)
+        one_hot = jnp.where(slot_ids == slot_row[e:e + 1, :tokens], 1.0, 0.0).astype(jnp.bfloat16)
+        rows_ref[e] = jnp.dot(one_hot, u, preferred_element_type=jnp.float32).astype(jnp.bfloat16)
+    buf_ids = lax.broadcasted_iota(jnp.int32, (tokens, n_exp * pad_cap), 1).astype(jnp.float32)
+    comb = jnp.zeros((tokens, n_exp * pad_cap), jnp.float32)
     for e in range(n_exp):
-        slot_e = slot_col_ref[:, e:e + 1]
-        dest_e = jnp.where(slot_e >= 0.0, slot_e + float(e * capacity), -1.0)
-        comb = jnp.where(buf_ids == dest_e, gate_col_ref[:, e:e + 1], comb)
+        slot_e = col_tab[:tokens, e:e + 1]
+        dest_e = jnp.where(slot_e >= 0.0, slot_e + float(e * pad_cap), -1.0)
+        comb = jnp.where(buf_ids == dest_e, col_tab[tokens:, e:e + 1], comb)
     comb_ref[...] = comb.astype(jnp.bfloat16)
 
 
-def dispatch(gathered, slot_row, slot_col, gate_col, tokens, capacity):
-    n_src, _, cols = gathered.shape
-    n_exp = slot_row.shape[1]
+def dispatch(gathered, tokens, pad_cap, n_exp):
+    n_src, all_rows, cols = gathered.shape
     return pl.pallas_call(
-        functools.partial(dispatch_kernel, capacity),
+        functools.partial(dispatch_kernel, pad_cap, n_exp),
         grid=(n_src,),
         out_shape=(
-            jax.ShapeDtypeStruct((n_exp, n_src, capacity, cols), jnp.bfloat16),
-            jax.ShapeDtypeStruct((n_src, tokens, n_exp * capacity), jnp.bfloat16),
+            jax.ShapeDtypeStruct((n_exp, n_src, pad_cap, cols), jnp.bfloat16),
+            jax.ShapeDtypeStruct((n_src, tokens, n_exp * pad_cap), jnp.bfloat16),
         ),
-        in_specs=[
-            pl.BlockSpec((None, tokens, cols), lambda s: (s, 0, 0)),
-            pl.BlockSpec((None, n_exp, tokens), lambda s: (s, 0, 0)),
-            pl.BlockSpec((None, tokens, n_exp), lambda s: (s, 0, 0)),
-            pl.BlockSpec((None, tokens, n_exp), lambda s: (s, 0, 0)),
-        ],
+        in_specs=[pl.BlockSpec((None, all_rows, cols), lambda s: (s, 0, 0))],
         out_specs=(
-            pl.BlockSpec((n_exp, None, capacity, cols), lambda s: (0, s, 0, 0)),
-            pl.BlockSpec((None, tokens, n_exp * capacity), lambda s: (s, 0, 0)),
+            pl.BlockSpec((n_exp, None, pad_cap, cols), lambda s: (0, s, 0, 0)),
+            pl.BlockSpec((None, tokens, n_exp * pad_cap), lambda s: (s, 0, 0)),
         ),
         compiler_params=pltpu.CompilerParams(vmem_limit_bytes=VMEM_LIMIT),
         cost_estimate=pl.CostEstimate(flops=10_000_000_000, bytes_accessed=30_000_000, transcendentals=0),
         name='dispatch',
-    )(gathered, slot_row, slot_col, gate_col)
-
-
-def inner_kernel(rows_ref, gate_ref, up_ref, inner_ref):
-    depth = rows_ref.shape[-1]
-    gate_w = gate_ref[...].reshape(depth, gate_ref.shape[-1])
-    up_w = up_ref[...].reshape(depth, up_ref.shape[-1])
-    gate_act = jnp.dot(rows_ref[...], gate_w, preferred_element_type=jnp.float32)
-    up_act = jnp.dot(rows_ref[...], up_w, preferred_element_type=jnp.float32)
-    inner_ref[...] = (gate_act * jax.nn.sigmoid(gate_act) * up_act).astype(jnp.bfloat16)
-
-
-def expert_inner(rows, w_gate, w_up):
-    n_exp, n_src, capacity, depth = rows.shape
-    parts, _, part_depth, ffn = w_gate.shape
-    tall = rows.reshape(n_exp, n_src * capacity, depth)
-    tile = n_src * capacity // 2
-    weight_spec = pl.BlockSpec((parts, None, part_depth, ffn), lambda e, t: (0, e, 0, 0))
+    )(gathered)
+
+
+def toggled(pos, bit):
+    return pos + bit - 2 * pos * bit
+
+
+def moe_kernel(rows_hbm, gate_up_hbm, comb_hbm, down_ref, hidden_ref, out_ref,
+               row_buf, gate_buf, up_buf, inner, comb, down_all, y_buf, send_core, acc, got_core, got_x, got_y, got_last,
+               load_sems, comb_sem, z_own_sems, z_pass_sems, z_recv_sems,
+               core_send, core_recv, x_send, x_recv, y_send, y_recv, last_send, last_recv):
+    place = layer_place()
+    dx, dz, dy, dc = place
+    n_exp, n_rows, ffn = inner.shape
+    n_src, tokens, _ = comb.shape
+    pad_cap = n_rows // n_src
+    half_cols = acc.shape[-1]
+    block_cols = 2 * half_cols
+    row_tile = n_rows // 4
+    depth = row_buf.shape[-1]
+    across_x, across_y, partner = related(place, 1, 0), related(place, 2, 0), related(place, 0, 1)
+    upper = dz // 2
+    inside = (dz == 1) | (dz == 2)
+    at_end = (dz == 0) | (dz == 3)
+
+    def at_z(z):
+        return (dx, z, dy, dc)
+
+    def remote(src, dst, send_sem, recv_sem, where):
+        return pltpu.make_async_remote_copy(src_ref=src, dst_ref=dst, send_sem=send_sem, recv_sem=recv_sem, device_id=dev_id(where), device_id_type=MESH_ID)
+
+    def load(e):
+        slot = e % 2
+        return [
+            pltpu.make_async_copy(rows_hbm.at[e], row_buf.at[slot], load_sems.at[0, slot]),
+            pltpu.make_async_copy(gate_up_hbm.at[:, 0, e], gate_buf.at[slot], load_sems.at[1, slot]),
+            pltpu.make_async_copy(gate_up_hbm.at[:, 1, e], up_buf.at[slot], load_sems.at[2, slot]),
+        ]
+
+    for copy in load(0):
+        copy.start()
+    comb_copy = pltpu.make_async_copy(comb_hbm, comb, comb_sem)
+    comb_copy.start()
+
+    barrier = pltpu.get_barrier_semaphore()
+    for target in (across_x, across_y, partner):
+        pl.semaphore_signal(barrier, inc=1, device_id=dev_id(target), device_id_type=MESH_ID)
+
+    @pl.when(dz > 0)
+    def _():
+        pl.semaphore_signal(barrier, inc=1, device_id=dev_id(at_z(dz - 1)), device_id_type=MESH_ID)
+
+    @pl.when(dz < 3)
+    def _():
+        pl.semaphore_signal(barrier, inc=1, device_id=dev_id(at_z(dz + 1)), device_id_type=MESH_ID)
+
+    @pl.when(inside)
+    def _():
+        pl.semaphore_wait(barrier, 5)
+
+    @pl.when(at_end)
+    def _():
+        pl.semaphore_wait(barrier, 4)
+
+    pair = n_exp // 2
+
+    def piece(p, sub):
+        return down_all.at[p, pl.ds(sub * pair, pair)]
+
+    def own_copy(side, sub):
+        target = dz - 1 if side == 0 else dz + 1
+        return remote(down_ref.at[pl.ds(sub * pair, pair)], piece(dz, sub), z_own_sems.at[side, sub], z_recv_sems.at[dz, sub], at_z(target))
+
+    def pass_copy(which, p, target, sub):
+        return remote(piece(p, sub), piece(p, sub), z_pass_sems.at[which, sub], z_recv_sems.at[p, sub], at_z(target))
+
+    for sub in (0, 1):
+        @pl.when(dz > 0)
+        def _():
+            own_copy(0, sub).start()
+
+        @pl.when(dz < 3)
+        def _():
+            own_copy(1, sub).start()
+
+    down_all[dz] = down_ref[...]
+    far, far_target = 3 * (2 - dz), 3 * (dz - 1)
+
+    def pass_near(sub):
+        @pl.when(inside)
+        def _():
+            wait_in(piece(dz - 1, sub), z_recv_sems.at[dz - 1, sub])
+            pass_copy(0, dz - 1, dz + 1, sub).start()
+            wait_in(piece(dz + 1, sub), z_recv_sems.at[dz + 1, sub])
+            pass_copy(1, dz + 1, dz - 1, sub).start()
+
+    def pass_far(sub):
+        @pl.when(inside)
+        def _():
+            wait_in(piece(far, sub), z_recv_sems.at[far, sub])
+            pass_copy(2, far, far_target, sub).start()
+
+    for e in range(n_exp):
+        if e + 1 < n_exp:
+            for copy in load(e + 1):
+                copy.start()
+        for copy in load(e):
+            copy.wait()
+        slot = e % 2
+
+        def tile_body(t, carry):
+            at = pl.ds(pl.multiple_of(t * row_tile, row_tile), row_tile)
+            rows = row_buf[slot, at]
+            gate_act = jnp.dot(rows, gate_buf[slot].reshape(depth, ffn), preferred_element_type=jnp.float32)
+            up_act = jnp.dot(rows, up_buf[slot].reshape(depth, ffn), preferred_element_type=jnp.float32)
+            inner[e, at] = (gate_act * jax.nn.sigmoid(gate_act) * up_act).astype(jnp.bfloat16)
+            return carry
+
+        lax.fori_loop(0, 4, tile_body, 0)
+    pass_near(0)
+    comb_copy.wait()
+
+    def block_of(i):
+        if i == 0:
+            return dz
+        near_end = dz + upper * (3 - 2 * dz)
+        low = i - near_end if i == 1 else i
+        return low + upper * (3 - 2 * low)
+
+    def rel_slot(rel, core_rel):
+        return toggled(dx, rel % 2) * 4 + toggled(dy, rel // 2) * 2 + flip(dc, core_rel)
+
+    def core_copy(i, rel):
+        return remote(send_core.at[i % 2, rel], got_core.at[i, rel], core_send.at[i, rel], core_recv.at[i, rel], partner)
+
+    def x_copy(i, rel):
+        where = (3 - rel) // 2
+        return remote(acc.at[i % 2, rel, 0], got_x.at[i, where], x_send.at[i, where], x_recv.at[i, where], across_x)
+
+    def y_copy(i, rel):
+        where = 3 - rel
+        return remote(acc.at[i % 2, rel, 1], got_y.at[i, where], y_send.at[i, where], y_recv.at[i, where], across_y)
+
+    def last_copy(i, which):
+        rel, half, target = ((2, 0, across_y), (1, 1, across_x))[which]
+        return remote(acc.at[i % 2, rel, half], got_last.at[i, which], last_send.at[i, which], last_recv.at[i, which], target)
+
+    def start_block(i):
+        p = block_of(i)
+        if i:
+            @pl.when(at_end)
+            def _():
+                for sub in (0, 1):
+                    wait_in(piece(p, sub), z_recv_sems.at[p, sub])
+
+        def y_body(e, carry):
+            y_tall = jnp.dot(inner[e], down_all[p, e], preferred_element_type=jnp.float32).astype(jnp.bfloat16)
+            at = pl.ds(pl.multiple_of(e * pad_cap, pad_cap), pad_cap)
+            for s in range(n_src):
+                y_buf[s, at] = y_tall[s * pad_cap:(s + 1) * pad_cap]
+            return carry
+
+        lax.fori_loop(0, n_exp, y_body, 0)
+
+        def partial(rel, core_rel):
+            slot = rel_slot(rel, core_rel)
+            return jnp.dot(comb[slot], y_buf[slot], preferred_element_type=jnp.float32)
+
+        def core_body(k, carry):
+            rel = 3 - k
+            send_core[i % 2, rel] = partial(rel, 1)
+            core_copy(i, rel).start()
+            return carry
+
+        def own_body(k, carry):
+            rel = 3 - k
+            mine = partial(rel, 0)
+            wait_in(got_core.at[i, rel], core_recv.at[i, rel])
+            mine = mine + got_core[i, rel]
+            acc[i % 2, rel, 0] = mine[:, :half_cols]
+            acc[i % 2, rel, 1] = mine[:, half_cols:]
+
+            @pl.when(rel % 2 == 1)
+            def _():
+                x_copy(i, rel).start()
+
+            @pl.when(rel // 2 == 1)
+            def _():
+                y_copy(i, rel).start()
+
+            return carry
+
+        lax.fori_loop(0, 4, core_body, 0)
+        lax.fori_loop(0, 4, own_body, 0)
+
+    def turn_block(i):
+        wait_in(got_x.at[i, 0], x_recv.at[i, 0])
+        acc[i % 2, 2, 0] += got_x[i, 0]
+        last_copy(i, 0).start()
+        wait_in(got_y.at[i, 0], y_recv.at[i, 0])
+        acc[i % 2, 1, 1] += got_y[i, 0]
+        last_copy(i, 1).start()
+
+    def end_block(i):
+        p = block_of(i)
+        for half, got, got_sems in ((0, got_x, x_recv), (1, got_y, y_recv)):
+            wait_in(got.at[i, 1], got_sems.at[i, 1])
+            wait_in(got_last.at[i, half], last_recv.at[i, half])
+            cols = pl.ds(pl.multiple_of(p * block_cols + half * half_cols, half_cols), half_cols)
+            total = acc[i % 2, 0, half] + got[i, 1] + got_last[i, half]
+            out_ref[:, cols] = (hidden_ref[:, cols].astype(jnp.float32) + total).astype(jnp.bfloat16)
+        for rel in range(4):
+            core_copy(i, rel).wait_send()
+        for rel in (3, 1):
+            x_copy(i, rel).wait_send()
+        for rel in (3, 2):
+            y_copy(i, rel).wait_send()
+        for which in (0, 1):
+            last_copy(i, which).wait_send()
+
+    start_block(0)
+    pass_near(1)
+    turn_block(0)
+    start_block(1)
+    end_block(0)
+    pass_far(0)
+    turn_block(1)
+    start_block(2)
+    pass_far(1)
+    end_block(1)
+    turn_block(2)
+    start_block(3)
+    end_block(2)
+    turn_block(3)
+    end_block(3)
+
+    for sub in (0, 1):
+        @pl.when(dz > 0)
+        def _():
+            own_copy(0, sub).wait_send()
+
+        @pl.when(dz < 3)
+        def _():
+            own_copy(1, sub).wait_send()
+
+        @pl.when(inside)
+        def _():
+            pass_copy(0, dz - 1, dz + 1, sub).wait_send()
+            pass_copy(1, dz + 1, dz - 1, sub).wait_send()
+            pass_copy(2, far, far_target, sub).wait_send()
+
+
+def moe(rows, gate_up, comb, down_half, hidden, collective_id):
+    n_exp, n_src, pad_cap, depth = rows.shape
+    parts, _, _, part_depth, ffn = gate_up.shape
+    _, tokens, buf_rows = comb.shape
+    block_cols = down_half.shape[-1]
+    half = block_cols // 2
+    tall = rows.reshape(n_exp, n_src * pad_cap, depth)
+    dma = pltpu.SemaphoreType.DMA
     return pl.pallas_call(
-        inner_kernel,
-        grid=(n_exp, 2),
-        out_shape=jax.ShapeDtypeStruct((n_exp, n_src * capacity, ffn), jnp.bfloat16),
-        in_specs=[pl.BlockSpec((None, tile, depth), lambda e, t: (e, t, 0)), weight_spec, weight_spec],
-        out_specs=pl.BlockSpec((None, tile, ffn), lambda e, t: (e, t, 0)),
-        compiler_params=pltpu.CompilerParams(vmem_limit_bytes=VMEM_LIMIT),
-        cost_estimate=pl.CostEstimate(flops=12_000_000_000, bytes_accessed=30_000_000, transcendentals=0),
-        name='expert_inner',
-    )(tall, w_gate, w_up)
-
-
-def back_kernel(capacity, inner_ref, comb_ref, down_ref, out_ref, wide_w, y_buf, send_core, got_core, acc, got_x, got_y, got_last, send_sems, core_sems, x_sems, y_sems, last_sems):
-    place = layer_place()
-    across_x, across_y, partner = related(place, 1, 0), related(place, 2, 0), related(place, 0, 1)
-    greet([across_x, across_y, partner])
-    sender = Sender(send_sems)
-    n_exp, n_rows, ffn = inner_ref.shape
-    parts, _, _, part_cols = down_ref.shape
-    n_src = n_rows // capacity
-    for p in range(parts):
-        wide_w[:, :, p * part_cols:(p + 1) * part_cols] = down_ref[p]
-    for e in range(n_exp):
-        y_tall = jnp.dot(inner_ref[e], wide_w[e], preferred_element_type=jnp.float32).astype(jnp.bfloat16)
-        for s in range(n_src):
-            y_buf[s, e * capacity:(e + 1) * capacity, :] = y_tall[s * capacity:(s + 1) * capacity]
-    half_cols = acc.shape[-1]
-
-    def partial(chip_rel, core_rel, half):
-        slot = slot_of(related(place, chip_rel, core_rel))
-        cols = pl.ds(half * half_cols, half_cols)
-        return jnp.dot(comb_ref[slot], y_buf[slot, :, cols], preferred_element_type=jnp.float32)
-
-    order = (3, 1, 2, 0)
-    for chip_rel in order:
-        for half in (0, 1):
-            send_core[chip_rel, half] = partial(chip_rel, 1, half)
-            sender.send(send_core.at[chip_rel, half], got_core.at[chip_rel, half], core_sems.at[chip_rel, half], partner)
-    for chip_rel in order:
-        for half in (0, 1):
-            mine = partial(chip_rel, 0, half)
-            wait_in(got_core.at[chip_rel, half], core_sems.at[chip_rel, half])
-            acc[chip_rel, half] = mine + got_core[chip_rel, half]
-            if chip_rel & 1 and half == 0:
-                where = 0 if chip_rel == 3 else 1
-                sender.send(acc.at[chip_rel, 0], got_x.at[where], x_sems.at[where], across_x)
-            if chip_rel & 2 and half == 1:
-                where = 0 if chip_rel == 3 else 1
-                sender.send(acc.at[chip_rel, 1], got_y.at[where], y_sems.at[where], across_y)
-    wait_in(got_x.at[0], x_sems.at[0])
-    acc[2, 0] += got_x[0]
-    sender.send(acc.at[2, 0], got_last.at[0], last_sems.at[0], across_y)
-    wait_in(got_y.at[0], y_sems.at[0])
-    acc[1, 1] += got_y[0]
-    sender.send(acc.at[1, 1], got_last.at[1], last_sems.at[1], across_x)
-    wait_in(got_x.at[1], x_sems.at[1])
-    wait_in(got_y.at[1], y_sems.at[1])
-    wait_in(got_last.at[0], last_sems.at[0])
-    out_ref[:, :half_cols] = acc[0, 0] + got_x[1] + got_last[0]
-    wait_in(got_last.at[1], last_sems.at[1])
-    out_ref[:, half_cols:] = acc[0, 1] + got_y[1] + got_last[1]
-    sender.drain()
-
-
-def expert_back(inner, comb, down, capacity, collective_id):
-    n_exp, n_rows, ffn = inner.shape
-    parts, _, _, part_cols = down.shape
-    n_src, tokens, buf_rows = comb.shape
-    cols = parts * part_cols
-    half = (tokens, cols // 2)
-    return pl.pallas_call(
-        functools.partial(back_kernel, capacity),
-        out_shape=jax.ShapeDtypeStruct((tokens, cols), jnp.float32),
-        in_specs=[pl.BlockSpec(memory_space=pltpu.VMEM)] * 3,
+        moe_kernel,
+        out_shape=jax.ShapeDtypeStruct(hidden.shape, jnp.bfloat16),
+        in_specs=[pl.BlockSpec(memory_space=pl.ANY)] * 3 + [pl.BlockSpec(memory_space=pltpu.VMEM)] * 2,
         out_specs=pl.BlockSpec(memory_space=pltpu.VMEM),
         scratch_shapes=[
-            pltpu.VMEM((n_exp, ffn, cols), jnp.bfloat16),
-            pltpu.VMEM((n_src, buf_rows, cols), jnp.bfloat16),
-            pltpu.VMEM((4, 2) + half, jnp.float32),
-            pltpu.VMEM((4, 2) + half, jnp.float32),
-            pltpu.VMEM((4, 2) + half, jnp.float32),
-            pltpu.VMEM((2,) + half, jnp.float32),
-            pltpu.VMEM((2,) + half, jnp.float32),
-            pltpu.VMEM((2,) + half, jnp.float32),
-            pltpu.SemaphoreType.DMA((14,)),
-            pltpu.SemaphoreType.DMA((4, 2)),
-            pltpu.SemaphoreType.DMA((2,)),
-            pltpu.SemaphoreType.DMA((2,)),
-            pltpu.SemaphoreType.DMA((2,)),
+            pltpu.VMEM((2, n_src * pad_cap, depth), jnp.bfloat16),
+            pltpu.VMEM((2, parts, part_depth, ffn), jnp.bfloat16),
+            pltpu.VMEM((2, parts, part_depth, ffn), jnp.bfloat16),
+            pltpu.VMEM((n_exp, n_src * pad_cap, ffn), jnp.bfloat16),
+            pltpu.VMEM(comb.shape, jnp.bfloat16),
+            pltpu.VMEM((parts,) + down_half.shape, jnp.bfloat16),
+            pltpu.VMEM((n_src, buf_rows, block_cols), jnp.bfloat16),
+            pltpu.VMEM((2, 4, tokens, block_cols), jnp.float32),
+            pltpu.VMEM((2, 4, 2, tokens, half), jnp.float32),
+            pltpu.VMEM((parts, 4, tokens, block_cols), jnp.float32),
+            pltpu.VMEM((parts, 2, tokens, half), jnp.float32),
+            pltpu.VMEM((parts, 2, tokens, half), jnp.float32),
+            pltpu.VMEM((parts, 2, tokens, half), jnp.float32),
+            dma((3, 2)), dma, dma((2, 2)), dma((3, 2)), dma((parts, 2)),
+            dma((parts, 4)), dma((parts, 4)), dma((parts, 2)), dma((parts, 2)),
+            dma((parts, 2)), dma((parts, 2)), dma((parts, 2)), dma((parts, 2)),
         ],
-        compiler_params=pltpu.CompilerParams(collective_id=collective_id, has_side_effects=True, vmem_limit_bytes=VMEM_LIMIT),
+        compiler_params=pltpu.CompilerParams(collective_id=collective_id, has_side_effects=True, vmem_limit_bytes=62 * 1024 * 1024),
         cost_estimate=pl.CostEstimate(flops=30_000_000_000, bytes_accessed=30_000_000, transcendentals=0),
-        name='expert_back',
-    )(inner, comb, down)
+        name='moe',
+    )(tall, gate_up, comb, down_half, hidden)
 
 
 def solution(mesh):
@@ -414,10 +590,7 @@
         gate_half = lax.dynamic_slice_in_dim(gate_shard, first, here, 0)
         up_half = lax.dynamic_slice_in_dim(up_shard, first, here, 0)
         down_half = lax.dynamic_slice_in_dim(down_shard, first, here, 0)
-        mid = down_half.shape[2] // 2
-        w_gate = lax.all_gather(gate_half, 'fsdp')
-        w_up = lax.all_gather(up_half, 'fsdp')
-        w_down = [lax.all_gather(down_half[:, :, :mid], 'fsdp'), lax.all_gather(down_half[:, :, mid:], 'fsdp')]
+        gate_up = lax.all_gather(jnp.stack([gate_half, up_half]), 'fsdp')
 
         _, triple, heads, head_dim = qkv_shard.shape
         width = heads * head_dim
@@ -436,18 +609,9 @@
         gate_tab = jnp.sum(jnp.where(hits, gate_t, 0.0), axis=0)
         tables = jnp.concatenate([slot_tab, gate_tab], axis=1).astype(jnp.bfloat16)
         gathered = gather_tokens(jnp.concatenate([normed, tables], axis=0))
-        my_first = lax.axis_index('ep') * gate_shard.shape[0] + first
-        my_tables = lax.dynamic_slice_in_dim(gathered[:, tokens:], my_first, here, 1).astype(jnp.float32)
-        slot_row = my_tables[:, :, :tokens]
-        slot_col = slot_row.transpose(0, 2, 1)
-        gate_col = my_tables[:, :, tokens:].transpose(0, 2, 1)
-        rows, comb = dispatch(gathered, slot_row, slot_col, gate_col, tokens, capacity)
-
-        inner = expert_inner(rows, w_gate, w_up)
-        sums = [expert_back(inner, comb, w_down[i], capacity, 3 + i) for i in range(2)]
-        parts = w_down[0].shape[0]
-        moe_sum = jnp.stack([part.reshape(tokens, parts, mid) for part in sums], axis=2).reshape(tokens, d_model)
-        result = hidden.reshape(tokens, d_model).astype(jnp.float32) + moe_sum
-        return result.astype(jnp.bfloat16).reshape(batch_rows, seq_len, d_model)
+        pad_cap = 16 * ((capacity + 15) // 16)
+        rows, comb = dispatch(gathered, tokens, pad_cap, here)
+        result = moe(rows, gate_up, comb, down_half, hidden.reshape(tokens, d_model), 3)
+        return result.reshape(batch_rows, seq_len, d_model)
 
     return jax.shard_map(local_step, mesh=mesh, in_specs=(tok_spec, tok_spec, tok_spec, tok_spec, P(None), P('fsdp', None, None, None), P('fsdp', None, None), P(None), P('ep', 'fsdp', None), P('ep', 'fsdp', None), P('ep', None, 'fsdp')), out_specs=tok_spec, check_vma=False)

time: 368 us -> 290 us (0.79)
  Pallas kernels: 257 us -> 232 us
  waiting for transfers between devices: 24.1 us -> 0.02 us
  local copies, waits for them, and re-layouts: 35.2 us -> 11.3 us
  other arithmetic: 12.6 us -> 7.96 us
    all_gather x4 -> x1, waiting for transfers between devices: 23.5 us -> 0.01 us  [local_step(): gate_up = lax.all_gather(jnp.stack([gate_half, up_half]), 'fsdp')]
    pallas_call x4 -> x2, Pallas kernels: 138 us -> 115 us  [the longest x1 98.4 us: moe(): pl.pallas_call(moe_kernel, out_shape=jax.ShapeDtypeStruct(hidden.shape, j...]
    slice x4 -> x0, local copies, waits for them, and re-layouts: 6.57 us -> none  [the longest x2 4.33 us: local_step(): slot_row = my_tables[:, :, :tokens]]
    another operation x3 -> x1, local copies, waits for them, and re-layouts: 8.02 us -> 1.76 us  [local_step(): gate_up = lax.all_gather(jnp.stack([gate_half, up_half]), 'fsdp')]
    convert_element_type x2 -> x0, other arithmetic: 5.15 us -> none  [the longest x1 2.91 us: local_step(): return result.astype(jnp.bfloat16).reshape(batch_rows, seq_len, d_model)]
    transpose x1 -> x0, local copies, waits for them, and re-layouts: 4.73 us -> none  [local_step(): gate_col = my_tables[:, :, tokens:].transpose(0, 2, 1)]
    reshape x1 -> x0, local copies, waits for them, and re-layouts: 4.08 us -> none  [local_step(): jnp.stack([part.reshape(tokens, parts, mid) for part in sums], axis=2)]
  transfers between devices with their start and end apart: 4 -> 1, of which waited for: 1 -> 0; matrix products, arithmetic and copies ran while one was open for 14% -> 12% of each run, Pallas kernels for 56% -> 46%
where the time goes in v2:
time: 290 us
  Pallas kernels  232 us (80%)
  matrix products  25.1 us (9%)
  between operations  13.6 us (5%)
  local copies, waits for them, and re-layouts  11.3 us (4%)
  other arithmetic  7.96 us (3%)
    pallas_call x1, Pallas kernels, moe(): pl.pallas_call(moe_kernel, out_shape=jax.ShapeDtypeStruct(hidden.shape, j...  98.4 us
    pallas_call x1, Pallas kernels, gather_attention_weights(): pl.pallas_call(attn_gather_kernel, out_shape=jax.ShapeDtypeStruct((4 * ro...  73.4 us
    pallas_call x1, Pallas kernels, gather_tokens(): pl.pallas_call(token_gather_kernel, out_shape=jax.ShapeDtypeStruct((8, ro...  43.6 us
    pallas_call x1, Pallas kernels, dispatch(): pl.pallas_call(functools.partial(dispatch_kernel, pad_cap, n_exp), grid=(...  16.4 us
    sub x1, matrix products, attention_block(): jax.nn.softmax(jnp.where(causal, scores, -1e+30), axis=-1)  10.7 us
    dot_general x1, matrix products, attention_block(): jnp.einsum('crif,ife->cre', context, w_out, preferred_element_type=jnp.fl...  8.59 us
    unnamed x21, local copies, waits for them, and re-layouts  7.05 us
    unnamed x1, matrix products  5.8 us
  transfers between devices with their start and end apart: 1, of which 0 were waited for; matrix products, arithmetic and copies ran while one was open for 12% of the time, Pallas kernels for 46%

profile of v2, /device:TPU:0, one launch (start us, length us, event | category | flops | bytes accessed | tf_op | source)
XLA Modules:
  0.0 289.7 jit_solution(2487009672457760820)
XLA Ops:
  6.5 0.0 all-gather.3.cloned.1.call-start
  6.5 1.8 dynamic-slice_bitcast_fusion
  8.3 1.5 pad_maximum_fusion.1
  9.9 0.0 copy-start.1
  9.9 0.0 all-gather.3.cloned.1.call-update
  9.9 1.4 copy-done.1
  11.3 0.9 copy.21
  12.1 2.5 pad_maximum_fusion.shard_ref
  14.7 73.4 %attn_gather.1 = bf16[1024,4096]{1,0:T(8,128)(2,1)} custom-call(bf16[256,4096]{1,0:T(8,128)(2,1)} %pad_maximum_fusion.shard_ref), custom_call_target="tpu_custom_call" | custom-call | flops 30000001024 | bytes 10000000 | tf_op jit(solution)/shard_map/attn_gather/pallas_call | solution.py:190
  88.1 0.0 copy-start.8
  88.1 0.0 copy-start.9
  88.1 0.0 copy-start.7
  88.1 0.0 copy-start.6
  88.1 0.0 copy-start.5
  88.2 0.0 copy-start.4
  88.2 0.6 copy-done.8
  88.8 0.0 copy-start.3
  88.8 0.0 copy-done.9
  88.8 0.1 iota_compare_fusion
  88.9 0.0 copy-done.7
  88.9 0.0 copy-done.6
  88.9 0.0 copy-done.5
  89.0 0.1 select_reduce_fusion.1
  89.1 0.7 copy-done.4
  89.8 1.0 constant_dynamic-slice_fusion.down_ref
  90.8 0.0 copy-done.3
  90.8 0.3 fusion.11
  91.1 0.3 fusion.33
  91.4 5.8 %fusion.6 = f32[512,3072]{0,1:S(1)} fusion(bf16[1024,4096]{1,0:T(8,128)(2,1)} %attn_gather.1, bf16[1,512,1024]{2,1,0:T(8,128)(2,1)S(1)} %copy-done.3, f32[1024]{0:T(1024)S(1)} %convert_element_type.68, f32[512]{0:T(512)S(1)} %add_rsqrt_fusion.1), kind=kOutput, calls=%fused_computation.9 | convolution fusion | flops 3223322624 | bytes 13637632
  97.2 0.0 copy-start
  97.2 0.6 slice_bitcast_fusion.1
  97.8 2.0 copy-done
  99.8 1.7 fusion.28
  101.5 0.0 slice-start
  101.5 10.7 %fusion.40 = (f32[16,512]{1,0:T(8,128)S(1)}, f32[16,512,512]{1,2,0:T(8,128)}) fusion(pred[512,512]{0,1:T(8,128)(4,1)S(1)} %iota_compare_fusion, bf16[512,16,32]{0,2,1:T(8,128)(2,1)} %get-tuple-element.17, bf16[512,16,32]{0,2,1:T(8,128)(2,1)} %get-tuple-element.18, bf16[512,16,32]{0,2,1:T(8,128)(2,1)S(1)} %get-tuple-element.14, ...), kind=kOutput, calls=%fused_computation.68 | convolution fusion | flops 557842944 | bytes 19169280 | tf_op jit(solution)/shard_map/sub | solution.py:43
  112.2 0.0 slice-done
  112.2 8.6 %fusion.8 = (f32[512]{0:T(512)S(1)}, bf16[1,512,1024]{2,1,0:T(8,128)(2,1)S(1)}) fusion(bf16[16,64,1024]{2,1,0:T(8,128)(2,1)S(1)} %bitcast.68, f32[16,512,512]{1,2,0:T(8,128)} %get-tuple-element.22, f32[16,512]{1,0:T(8,128)S(1)} %get-tuple-element.21, f32[1,512,3,16,64]{1,4,3,2,0:T(8,128)} %bitcast.67, bf16[1,512,1024]{2,1,0:T(8,128)(2,1)} %param.11), kind=kOutput, calls=%fused_computation.16 | convolution fusion | flops 1622670848 | bytes 22054912 | tf_op jit(solution)/shard_map/crif,ife->cre/dot_general | solution.py:45
  120.8 0.0 copy-start.2
  120.9 0.3 fusion.24
  121.2 1.1 maximum_maximum_fusion.own_ref
  122.3 0.0 copy-done.2
  122.3 43.6 %token_gather.1.gathered_ref = bf16[8,544,1024]{2,1,0:T(8,128)(2,1)} custom-call(bf16[544,1024]{1,0:T(8,128)(2,1)} %maximum_maximum_fusion.own_ref), custom_call_target="tpu_custom_call" | custom-call | flops 30000001024 | bytes 10000000 | tf_op jit(solution)/shard_map/token_gather/pallas_call | solution.py:234
  165.9 16.4 %dispatch.1 = (bf16[4,8,176,1024]{3,2,1,0:T(8,128)(2,1)}, bf16[8,512,704]{2,1,0:T(8,128)(2,1)}) custom-call(bf16[8,544,1024]{2,1,0:T(8,128)(2,1)} %token_gather.1.gathered_ref), custom_call_target="tpu_custom_call" | custom-call | flops 10000000000 | bytes 30000000 | tf_op jit(solution)/shard_map/dispatch/pallas_call | solution.py:275
  182.2 0.0 all-gather.3.cloned.1.call-done
  182.2 98.4 %moe.1 = bf16[512,1024]{1,0:T(8,128)(2,1)} custom-call(bf16[4,1408,1024]{2,1,0:T(8,128)(2,1)} %bitcast.75, bf16[4,2,4,256,512]{4,3,2,1,0:T(8,128)(2,1)} %bitcast.74, bf16[8,512,704]{2,1,0:T(8,128)(2,1)} %get-tuple-element.8.comb_hbm, bf16[4,512,256]{2,1,0:T(8,128)(2,1)} %constant_dynamic-slice_fusion.down_ref, bf16[512,1024]{1,0:T(8,128)(2,1)} %bitcast.70), custom_call_target="tpu_custom_call" | custom-call | flops 30000001024 | bytes 30000000 | tf_op jit(solution)/shard_map/moe/pallas_call | solution.py:550
  280.6 2.3 copy.26
  (8 shorter events, 0.0 us)
Async XLA Ops:
  6.5 175.7 %all-gather.3.cloned.1.call-start = ((), (), s32[]{:S(2)}) async-start(), calls=%async_computation | async-start | bytes 10485760 | tf_op jit(solution)/shard_map/all_gather | solution.py:593
  9.9 1.4 copy-start.1
  88.1 0.7 copy-start.8
  88.1 0.7 copy-start.9
  88.1 0.8 copy-start.7
  88.1 0.8 copy-start.6
  88.1 0.8 copy-start.5
  88.2 1.6 copy-start.4
  88.8 2.0 copy-start.3
  97.2 2.6 copy-start
  101.5 10.7 %slice-start = ((bf16[1024,4096]{1,0:T(8,128)(2,1)}), bf16[1024,1024]{1,0:T(8,128)(2,1)S(1)}, s32[]{:S(2)}) async-start(bf16[1024,4096]{1,0:T(8,128)(2,1)} %attn_gather.1), calls=%async_computation.1 | async-start | bytes 4194304 | tf_op jit(solution)/shard_map/slice | solution.py:600
  120.8 1.5 copy-start.2
Sparse Core Ops, SparseCore 0:
  10.0 169.8 all-gather.2

commit v3 on v0

v3 whole, which is shorter than its diff:
```python
import functools

import jax
import jax.numpy as jnp
import numpy as np
from jax import lax
from jax.experimental import pallas as pl
from jax.experimental.pallas import tpu as pltpu
from jax.sharding import PartitionSpec as P

NORM_EPS = 1e-6
ROPE_BASE = 10000.0
MESH_ID = pl.DeviceIdType.MESH
LANES = 128


def capacity_of(tok_count, top_k, experts):
    return 8 * ((5 * tok_count * top_k) // (32 * experts) + 1)


def rope_tables(seq_len, head_dim):
    half = head_dim // 2
    lane = np.arange(LANES)
    inv_freq = ROPE_BASE ** (-(lane % half) / half)
    angles = np.arange(seq_len)[:, None] * inv_freq[None, :]
    sign = np.where(lane % head_dim < half, -1.0, 1.0)
    return np.cos(angles).astype(np.float32), (np.sin(angles) * sign).astype(np.float32)


def layer_place():
    dx, dz, ep = lax.axis_index('data'), lax.axis_index('fsdp'), lax.axis_index('ep')
    return dx, dz, ep // 2, ep % 2


def flip(pos, bit):
    return (1 - pos) if bit else pos


def toggled(pos, bit):
    return pos + bit - 2 * pos * bit


def related(place, chip_rel, core_rel):
    dx, dz, dy, dc = place
    return flip(dx, chip_rel & 1), dz, flip(dy, chip_rel & 2), flip(dc, core_rel)


def slot_of(place):
    dx, _, dy, dc = place
    return dx * 4 + dy * 2 + dc


def dev_id(place):
    dx, dz, dy, dc = place
    return (dx, dz, dy * 2 + dc)


def remote(src, dst, send_sem, recv_sem, where):
    return pltpu.make_async_remote_copy(src_ref=src, dst_ref=dst, send_sem=send_sem, recv_sem=recv_sem, device_id=dev_id(where), device_id_type=MESH_ID)


def wait_in(ref, sem):
    pltpu.make_async_copy(ref, ref, sem).wait()


class Sender:
    def __init__(self, send_sems):
        self.send_sems = send_sems
        self.copies = []

    def send(self, src, dst, recv_sem, place):
        copy = remote(src, dst, self.send_sems.at[len(self.copies)], recv_sem, place)
        copy.start()
        self.copies.append(copy)

    def drain(self):
        for copy in self.copies:
            copy.wait_send()


def spread_in_layer(place, sender, own_src, part_ref, recv_sems):
    across_x, across_y, partner = related(place, 1, 0), related(place, 2, 0), related(place, 0, 1)

    def pass_on(chip_rel, half, target, rel_there, core_there, first=False):
        owner = slot_of(related(place, chip_rel, 0))
        src = own_src(half) if first else part_ref(owner, half)
        sender.send(src, part_ref(owner, half), recv_sems(rel_there, core_there, half), target)

    for half in (0, 1):
        pass_on(0, half, across_x, 1, 0, True)
        pass_on(0, 1 - half, across_y, 2, 0, True)
    for half in (0, 1):
        pass_on(0, half, partner, 0, 1, True)
    yield

    def arrived(chip_rel, core_rel, half):
        owner = slot_of(related(place, chip_rel, core_rel))
        wait_in(part_ref(owner, half), recv_sems(chip_rel, core_rel, half))

    arrived(1, 0, 0)
    pass_on(1, 0, across_y, 3, 0)
    pass_on(1, 0, partner, 1, 1)
    arrived(2, 0, 1)
    pass_on(2, 1, across_x, 3, 0)
    pass_on(2, 1, partner, 2, 1)
    yield
    arrived(1, 0, 1)
    pass_on(1, 1, partner, 1, 1)
    arrived(2, 0, 0)
    pass_on(2, 0, partner, 2, 1)
    yield
    arrived(3, 0, 0)
    pass_on(3, 0, partner, 3, 1)
    arrived(3, 0, 1)
    pass_on(3, 1, partner, 3, 1)
    yield
    for chip_rel in range(4):
        for half in (0, 1):
            arrived(chip_rel, 1, half)
    yield


def norm_rows(src, gain_ref, dst, rows):
    tile = 128

    def body(t, carry):
        at = pl.ds(pl.multiple_of(t * tile, tile), tile)
        wide = src[at].astype(jnp.float32)
        inv_rms = lax.rsqrt(jnp.mean(wide * wide, axis=-1, keepdims=True) + NORM_EPS)
        dst[at] = (wide * inv_rms * gain_ref[...]).astype(jnp.bfloat16)
        return carry

    lax.fori_loop(0, rows // tile, body, 0)


def attend(x_ref, normed, weights, cos_ref, sin_ref, qkv, hidden, head_dim):
    tokens, d_model = x_ref.shape
    lane = lax.broadcasted_iota(jnp.int32, (tokens, LANES), 1)
    low_half = lane % head_dim < head_dim // 2
    first_head = lax.broadcasted_iota(jnp.int32, (tokens // 2, LANES), 1) < head_dim
    group = 2 * LANES
    q_tile = tokens // 2
    scale = head_dim ** -0.5

    def rotate(val):
        swapped = jnp.where(low_half, pltpu.roll(val, LANES - head_dim // 2, 1), pltpu.roll(val, head_dim // 2, 1))
        return (val * cos_ref[...] + swapped * sin_ref[...]).astype(jnp.bfloat16)

    def project(b, cols):
        return jnp.dot(normed[:tokens], weights[b, :d_model, cols], preferred_element_type=jnp.float32)

    def group_body(g, carry):
        cols = pl.ds(pl.multiple_of(g * group, group), group)
        query, keys = project(0, cols), project(1, cols)
        values = project(2, cols).astype(jnp.bfloat16)
        for pair in (0, 1):
            at = slice(pair * LANES, (pair + 1) * LANES)
            qkv[0, :tokens, at] = rotate(query[:, at])
            qkv[1, :tokens, at] = rotate(keys[:, at])
            qkv[2, :tokens, at] = values[:, at]
        for pair in (0, 1):
            at = slice(pair * LANES, (pair + 1) * LANES)
            for tile in (0, 1):
                n_keys = (tile + 1) * q_tile
                q_pair = qkv[0, tile * q_tile:(tile + 1) * q_tile, at]
                k_pair, v_pair = qkv[1, :n_keys, at], qkv[2, :n_keys, at]
                row_id = lax.broadcasted_iota(jnp.int32, (q_tile, n_keys), 0) + tile * q_tile
                causal = row_id >= lax.broadcasted_iota(jnp.int32, (q_tile, n_keys), 1)
                outs = []
                for head in (0, 1):
                    q_head = jnp.where(first_head if head == 0 else ~first_head, q_pair, jnp.zeros((), jnp.bfloat16))
                    scores = lax.dot_general(q_head, k_pair, (((1,), (1,)), ((), ())), preferred_element_type=jnp.float32)
                    scores = jnp.where(causal, scores * scale, -1e30)
                    top = jnp.max(scores, axis=-1, keepdims=True)
                    weight = jnp.exp(scores - top)
                    probs = (weight * (1.0 / jnp.sum(weight, axis=-1, keepdims=True))).astype(jnp.bfloat16)
                    outs.append(jnp.dot(probs, v_pair, preferred_element_type=jnp.float32))
                out_cols = pl.ds(pl.multiple_of(g * group + pair * LANES, LANES), LANES)
                qkv[3, tile * q_tile:(tile + 1) * q_tile, out_cols] = jnp.where(first_head, outs[0], outs[1]).astype(jnp.bfloat16)
        return carry

    lax.fori_loop(0, d_model // group, group_body, 0)

    def out_body(g, carry):
        cols = pl.ds(pl.multiple_of(g * group, group), group)
        attn_out = jnp.dot(qkv[3, :tokens], weights[3, :d_model, cols], preferred_element_type=jnp.float32)
        hidden[:, cols] = (x_ref[:, cols].astype(jnp.float32) + attn_out).astype(jnp.bfloat16)
        return carry

    lax.fori_loop(0, d_model // group, out_body, 0)


def layer_kernel(head_dim, pad_cap,
                 x_ref, idx_ref, slot_ref, gate_ref, attn_gain_ref, moe_gain_ref, cos_ref, sin_ref,
                 qkv_hbm, proj_hbm, gate_hbm, up_hbm, down_hbm,
                 out_ref, tok_hbm,
                 big, gate_up, down_all, work, own_tok, hidden, inner, comb, y_buf, send_core, acc, got_core, got_x, got_y, got_last,
                 attn_send, attn_z_send, attn_z_recv, attn_recv, load_sems, tok_send, tok_recv, tok_sem, tok_load,
                 z_own, z_pass, z_recv, core_send, core_recv, x_send, x_recv, y_send, y_recv, last_send, last_recv):
    place = layer_place()
    dx, dz, dy, dc = place
    tokens, d_model = x_ref.shape
    experts = own_tok.shape[0] - tokens
    n_exp, n_rows, ffn = inner.shape
    n_src = comb.shape[0]
    block_cols = acc.shape[-1]
    half_tok = tokens // 2
    n_sub = down_all.shape[1]
    chunks = n_exp + n_sub
    across_x, across_y, partner = related(place, 1, 0), related(place, 2, 0), related(place, 0, 1)
    upper = dz // 2
    inside = (dz == 1) | (dz == 2)
    at_end = (dz == 0) | (dz == 3)
    first_exp = dx * n_exp
    mine = slot_of(place)

    def at_z(z):
        return (dx, z, dy, dc)

    barrier = pltpu.get_barrier_semaphore()
    for target in [at_z((dz + step) % 4) for step in (1, 2, 3)] + [across_x, across_y, partner]:
        pl.semaphore_signal(barrier, inc=1, device_id=dev_id(target), device_id_type=MESH_ID)
    pl.semaphore_wait(barrier, 6)

    shard_rows = qkv_hbm.shape[0]
    piece = shard_rows // 8

    def attn_src(b, rows):
        return proj_hbm.at[rows] if b == 3 else qkv_hbm.at[rows, pl.ds(b * d_model, d_model)]

    my_rows = pl.ds(pl.multiple_of(mine * piece, piece), piece)
    landing = pl.ds(pl.multiple_of(dz * shard_rows + mine * piece, piece), piece)
    z_copies = []
    for index, step in enumerate((1, 3, 2)):
        for b in range(4):
            copy = remote(attn_src(b, my_rows), big.at[b, landing], attn_z_send.at[index, b], attn_z_recv.at[index, b], at_z((dz + step) % 4))
            copy.start()
            z_copies.append(copy)

    def chunk_refs(p, j):
        if j < n_exp:
            return [gate_up.at[p, j, m] for m in (0, 1)]
        return [down_all.at[p, j - n_exp]]

    def chunk_srcs(j):
        if j < n_exp:
            return [gate_hbm.at[first_exp + j], up_hbm.at[first_exp + j]]
        return [down_hbm.at[pl.ds(first_exp, n_exp), :, pl.ds((j - n_exp) * block_cols, block_cols)]]

    def own_copies(side, j):
        target = at_z(dz - 1 if side == 0 else dz + 1)
        return [remote(src, dst, z_own.at[side, j, m], z_recv.at[dz, j, m], target) for m, (src, dst) in enumerate(zip(chunk_srcs(j), chunk_refs(dz, j)))]

    def pass_copies(which, p, j, z):
        return [remote(ref, ref, z_pass.at[which, j, m], z_recv.at[p, j, m], at_z(z)) for m, ref in enumerate(chunk_refs(p, j))]

    def wait_chunk(p, j):
        for m, ref in enumerate(chunk_refs(p, j)):
            wait_in(ref, z_recv.at[p, j, m])

    end_z, mid_z, far_z = 3 * (dz - 1), 3 - dz, 3 * (2 - dz)
    passes = ((end_z, mid_z), (mid_z, end_z), (far_z, end_z))

    def send_own(j):
        if j >= chunks:
            return

        @pl.when(dz > 0)
        def _():
            for copy in own_copies(0, j):
                copy.start()

        @pl.when(dz < 3)
        def _():
            for copy in own_copies(1, j):
                copy.start()

    def serve(j):
        @pl.when(inside)
        def _():
            for which, (p, z) in enumerate(passes):
                wait_chunk(p, j)
                for copy in pass_copies(which, p, j, z):
                    copy.start()
        send_own(j + 2)

    def need(j):
        @pl.when(at_end)
        def _():
            for k in range(3):
                wait_chunk(k + 1 - upper, j)

    send_own(0)
    send_own(1)
    own_loads = []
    for b in range(4):
        rows = pl.ds(pl.multiple_of(dz * shard_rows, shard_rows), shard_rows)
        own_loads.append(pltpu.make_async_copy(attn_src(b, pl.ds(0, shard_rows)), big.at[b, rows], load_sems.at[b]))
    for j in range(chunks):
        for m, (src, dst) in enumerate(zip(chunk_srcs(j), chunk_refs(dz, j))):
            own_loads.append(pltpu.make_async_copy(src, dst, load_sems.at[4 + 2 * j + m]))
    for copy in own_loads:
        copy.start()

    norm_rows(x_ref, attn_gain_ref, own_tok, tokens)

    expert_ids = lax.broadcasted_iota(jnp.int32, (experts, tokens), 0)
    slot_tab = jnp.zeros((experts, tokens), jnp.float32)
    gate_tab = jnp.zeros((experts, tokens), jnp.float32)
    for k in range(idx_ref.shape[0]):
        hit = expert_ids == idx_ref[k:k + 1, :]
        slot_tab = slot_tab + jnp.where(hit, slot_ref[k:k + 1, :].astype(jnp.float32) + 1.0, 0.0)
        gate_tab = gate_tab + jnp.where(hit, gate_ref[k:k + 1, :].astype(jnp.float32), 0.0)
    own_tok[tokens:, :tokens] = (slot_tab - 1.0).astype(jnp.bfloat16)
    own_tok[tokens:, tokens:] = gate_tab.astype(jnp.bfloat16)

    sender = Sender(attn_send)
    streams = []
    for index, step in enumerate((1, 3, 2)):
        source_z = (dz + 4 - step) % 4

        def part_ref(slot, half, source_z=source_z):
            start = source_z * shard_rows + slot * piece + half * (piece // 2)
            return big.at[:, pl.ds(pl.multiple_of(start, piece // 2), piece // 2)]

        def recv_sem(chip_rel, core_rel, half, index=index):
            return attn_recv.at[index, chip_rel, core_rel, half]

        arrival = pl.ds(pl.multiple_of(source_z * shard_rows + mine * piece, piece), piece)
        streams.append((arrival, index, spread_in_layer(place, sender, functools.partial(part_ref, mine), part_ref, recv_sem)))
    for arrival, index, stream in streams:
        for b in range(4):
            wait_in(big.at[b, arrival], attn_z_recv.at[index, b])
        next(stream)
    for _ in range(4):
        for _, _, stream in streams:
            next(stream)
    serve(0)
    for copy in own_loads:
        copy.wait()

    attend(x_ref, own_tok, big, cos_ref, sin_ref, work, hidden, head_dim)
    norm_rows(hidden, moe_gain_ref, own_tok, tokens)
    sender.drain()
    for copy in z_copies:
        copy.wait_send()

    tok_sender = Sender(tok_send)
    half_rows = own_tok.shape[0] // 2

    def tok_part(slot, half):
        return tok_hbm.at[slot, pl.ds(half * half_rows, half_rows)]

    def tok_half(half):
        return own_tok.at[pl.ds(half * half_rows, half_rows)]

    stream = spread_in_layer(place, tok_sender, tok_half, tok_part, lambda chip_rel, core_rel, half: tok_recv.at[chip_rel, core_rel, half])
    next(stream)
    tok_copy = pltpu.make_async_copy(own_tok, tok_hbm.at[mine], tok_sem)
    tok_copy.start()
    serve(1)
    for _ in range(4):
        next(stream)
    tok_copy.wait()
    tok_sender.drain()
    serve(2)

    def tok_in(s):
        return pltpu.make_async_copy(tok_hbm.at[s], work.at[s % 2], tok_load.at[s % 2])

    my_first = (lax.axis_index('ep') * 2 + dx) * n_exp
    pick_row = (lax.broadcasted_iota(jnp.int32, (8, experts), 1) == my_first + lax.broadcasted_iota(jnp.int32, (8, experts), 0)).astype(jnp.bfloat16)
    pick_col = (lax.broadcasted_iota(jnp.int32, (experts, LANES), 0) == my_first + lax.broadcasted_iota(jnp.int32, (experts, LANES), 1)).astype(jnp.bfloat16)
    tok_in(0).start()

    def dispatch_body(s, carry):
        @pl.when(s + 1 < n_src)
        def _():
            tok_in(s + 1).start()

        tok_in(s).wait()
        u = work[s % 2, :tokens]
        tables = work[s % 2, tokens:]
        slot_row = jnp.dot(pick_row, tables, preferred_element_type=jnp.float32)
        col_tab = lax.dot_general(tables, pick_col, (((0,), (0,)), ((), ())), preferred_element_type=jnp.float32)
        slot_ids = lax.broadcasted_iota(jnp.int32, (pad_cap, tokens), 0).astype(jnp.float32)
        rows = pl.ds(pl.multiple_of(s * pad_cap, pad_cap), pad_cap)
        for e in range(n_exp):
            one_hot = jnp.where(slot_ids == slot_row[e:e + 1, :tokens], 1.0, 0.0).astype(jnp.bfloat16)
            big[e, rows] = jnp.dot(one_hot, u, preferred_element_type=jnp.float32).astype(jnp.bfloat16)
        buf_ids = lax.broadcasted_iota(jnp.int32, (tokens, n_exp * pad_cap), 1).astype(jnp.float32)
        gates = jnp.zeros((tokens, n_exp * pad_cap), jnp.float32)
        for e in range(n_exp):
            slot_e = col_tab[:tokens, e:e + 1]
            dest_e = jnp.where(slot_e >= 0.0, slot_e + float(e * pad_cap), -1.0)
            gates = jnp.where(buf_ids == dest_e, col_tab[tokens:, e:e + 1], gates)
        comb[s] = gates.astype(jnp.bfloat16)
        return carry

    lax.fori_loop(0, n_src, dispatch_body, 0)
    serve(3)

    row_tile = n_rows // 4

    def expert_inner(e):
        need(e)

        def tile_body(t, carry):
            at = pl.ds(pl.multiple_of(t * row_tile, row_tile), row_tile)
            rows = big[e, at]
            gate_act = jnp.dot(rows, gate_up[:, e, 0].reshape(d_model, ffn), preferred_element_type=jnp.float32)
            up_act = jnp.dot(rows, gate_up[:, e, 1].reshape(d_model, ffn), preferred_element_type=jnp.float32)
            inner[e, at] = (gate_act * jax.nn.sigmoid(gate_act) * up_act).astype(jnp.bfloat16)
            return carry

        lax.fori_loop(0, 4, tile_body, 0)

    for e in range(n_exp - 1):
        expert_inner(e)
    serve(4)
    expert_inner(n_exp - 1)

    def block_of(i):
        if isinstance(i, int) and i < n_sub:
            return dz, i
        k, sub = (i - n_sub) % 3 + 1, (i - n_sub) // 3
        near_end = dz + upper * (3 - 2 * dz)
        low = k - near_end * ((3 - k) // 2)
        return low + upper * (3 - 2 * low), sub

    def rel_slot(rel, core_rel):
        return toggled(dx, rel % 2) * 4 + toggled(dy, rel // 2) * 2 + flip(dc, core_rel)

    halves = (pl.ds(0, half_tok), pl.ds(half_tok, half_tok))

    def core_copy(i, rel):
        return remote(send_core.at[i % 2, rel], got_core.at[i % 2, rel], core_send.at[i, rel], core_recv.at[i, rel], partner)

    def x_copy(i, rel):
        where = (3 - rel) // 2
        return remote(acc.at[i % 2, rel, halves[0]], got_x.at[i % 3, where], x_send.at[i, where], x_recv.at[i, where], across_x)

    def y_copy(i, rel):
        where = 3 - rel
        return remote(acc.at[i % 2, rel, halves[1]], got_y.at[i % 3, where], y_send.at[i, where], y_recv.at[i, where], across_y)

    def last_copy(i, which):
        rel, target = ((2, across_y), (1, across_x))[which]
        return remote(acc.at[i % 2, rel, halves[which]], got_last.at[i % 3, which], last_send.at[i, which], last_recv.at[i, which], target)

    def start_block(i):
        p, sub = block_of(i)
        if not (isinstance(i, int) and i < n_sub):
            @pl.when(at_end)
            def _():
                wait_in(down_all.at[p, sub], z_recv.at[p, n_exp + sub, 0])

        def y_body(e, carry):
            y_tall = jnp.dot(inner[e], down_all[p, sub, e], preferred_element_type=jnp.float32).astype(jnp.bfloat16)
            at = pl.ds(pl.multiple_of(e * pad_cap, pad_cap), pad_cap)
            for s in range(n_src):
                y_buf[s, at] = y_tall[s * pad_cap:(s + 1) * pad_cap]
            return carry

        lax.fori_loop(0, n_exp, y_body, 0)

        def partial(rel, core_rel):
            slot = rel_slot(rel, core_rel)
            return jnp.dot(comb[slot], y_buf[slot], preferred_element_type=jnp.float32)

        def core_body(k, carry):
            rel = 3 - k
            send_core[i % 2, rel] = partial(rel, 1)
            core_copy(i, rel).start()
            return carry

        def own_body(k, carry):
            rel = 3 - k
            own = partial(rel, 0)
            wait_in(got_core.at[i % 2, rel], core_recv.at[i, rel])
            acc[i % 2, rel] = own + got_core[i % 2, rel]

            @pl.when(rel % 2 == 1)
            def _():
                x_copy(i, rel).start()

            @pl.when(rel // 2 == 1)
            def _():
                y_copy(i, rel).start()

            return carry

        lax.fori_loop(0, 4, core_body, 0)
        lax.fori_loop(0, 4, own_body, 0)

    def turn_block(i):
        wait_in(got_x.at[i % 3, 0], x_recv.at[i, 0])
        acc[i % 2, 2, halves[0]] += got_x[i % 3, 0]
        last_copy(i, 0).start()
        wait_in(got_y.at[i % 3, 0], y_recv.at[i, 0])
        acc[i % 2, 1, halves[1]] += got_y[i % 3, 0]
        last_copy(i, 1).start()

    def end_block(i):
        p, sub = block_of(i)
        cols = pl.ds(pl.multiple_of((p * n_sub + sub) * block_cols, block_cols), block_cols)
        for half, got, got_sems in ((0, got_x, x_recv), (1, got_y, y_recv)):
            wait_in(got.at[i % 3, 1], got_sems.at[i, 1])
            wait_in(got_last.at[i % 3, half], last_recv.at[i, half])
            total = acc[i % 2, 0, halves[half]] + got[i % 3, 1] + got_last[i % 3, half]
            out_ref[halves[half], cols] = (hidden[halves[half], cols].astype(jnp.float32) + total).astype(jnp.bfloat16)
        for rel in range(4):
            core_copy(i, rel).wait_send()
        for rel in (3, 1):
            x_copy(i, rel).wait_send()
        for rel in (3, 2):
            y_copy(i, rel).wait_send()
        for which in (0, 1):
            last_copy(i, which).wait_send()

    blocks = 4 * n_sub
    start_block(0)
    turn_block(0)
    start_block(1)
    serve(5)
    end_block(0)
    turn_block(1)
    start_block(2)
    end_block(1)

    def block_body(i, carry):
        turn_block(i)

        @pl.when(i + 1 < blocks)
        def _():
            start_block(i + 1)

        end_block(i)
        return carry

    lax.fori_loop(2, blocks, block_body, 0)

    for j in range(chunks):
        @pl.when(dz > 0)
        def _():
            for copy in own_copies(0, j):
                copy.wait_send()

        @pl.when(dz < 3)
        def _():
            for copy in own_copies(1, j):
                copy.wait_send()

        @pl.when(inside)
        def _():
            for which, (p, z) in enumerate(passes):
                for copy in pass_copies(which, p, j, z):
                    copy.wait_send()


def whole_layer(head_dim, pad_cap, x, idx_t, slot_t, gate_t, attn_gain, moe_gain, qkv, proj, gate_w, up_w, down_w, experts):
    tokens, d_model = x.shape
    n_exp = gate_w.shape[0] // 2
    part_depth, ffn = gate_w.shape[1:]
    parts, n_src, block_cols = 4, 8, LANES
    n_sub = down_w.shape[2] // block_cols
    blocks = parts * n_sub
    chunks = n_exp + n_sub
    n_rows = n_src * pad_cap
    half = tokens // 2
    cos_tab, sin_tab = rope_tables(tokens, head_dim)
    dma = pltpu.SemaphoreType.DMA
    bf16, f32 = jnp.bfloat16, jnp.float32
    vmem, hbm = pl.BlockSpec(memory_space=pltpu.VMEM), pl.BlockSpec(memory_space=pl.ANY)
    return pl.pallas_call(
        functools.partial(layer_kernel, head_dim, pad_cap),
        out_shape=(jax.ShapeDtypeStruct(x.shape, bf16), jax.ShapeDtypeStruct((n_src, tokens + experts, d_model), bf16)),
        in_specs=[vmem] * 8 + [hbm] * 5,
        out_specs=(vmem, hbm),
        scratch_shapes=[
            pltpu.VMEM((n_exp, n_rows, d_model), bf16),
            pltpu.VMEM((parts, n_exp, 2, part_depth, ffn), bf16),
            pltpu.VMEM((parts, n_sub, n_exp, ffn, block_cols), bf16),
            pltpu.VMEM((4, tokens + experts, d_model), bf16),
            pltpu.VMEM((tokens + experts, d_model), bf16),
            pltpu.VMEM((tokens, d_model), bf16),
            pltpu.VMEM((n_exp, n_rows, ffn), bf16),
            pltpu.VMEM((n_src, tokens, n_exp * pad_cap), bf16),
            pltpu.VMEM((n_src, n_exp * pad_cap, block_cols), bf16),
            pltpu.VMEM((2, 4, tokens, block_cols), f32),
            pltpu.VMEM((2, 4, tokens, block_cols), f32),
            pltpu.VMEM((2, 4, tokens, block_cols), f32),
            pltpu.VMEM((3, 2, half, block_cols), f32),
            pltpu.VMEM((3, 2, half, block_cols), f32),
            pltpu.VMEM((3, 2, half, block_cols), f32),
            dma((42,)), dma((3, 4)), dma((3, 4)), dma((3, 4, 2, 2)), dma((4 + 2 * chunks,)),
            dma((14,)), dma((4, 2, 2)), dma, dma((2,)),
            dma((2, chunks, 2)), dma((3, chunks, 2)), dma((parts, chunks, 2)),
            dma((blocks, 4)), dma((blocks, 4)), dma((blocks, 2)), dma((blocks, 2)),
            dma((blocks, 2)), dma((blocks, 2)), dma((blocks, 2)), dma((blocks, 2)),
        ],
        compiler_params=pltpu.CompilerParams(collective_id=1, has_side_effects=True, vmem_limit_bytes=63 * 1024 * 1024),
        cost_estimate=pl.CostEstimate(flops=40_000_000_000, bytes_accessed=30_000_000, transcendentals=0),
        name='whole_layer',
    )(x, idx_t, slot_t, gate_t, attn_gain, moe_gain, cos_tab, sin_tab, qkv, proj, gate_w, up_w, down_w)[0]


def solution(mesh):
    tok_spec = P(('data', 'fsdp', 'ep'), None, None)
    ep_count = mesh.shape['ep']

    def local_step(x_blk, idx_blk, slot_blk, gate_blk, attn_gain, qkv_shard, out_shard, moe_gain, gate_shard, up_shard, down_shard):
        batch_rows, seq_len, d_model = x_blk.shape
        tokens = batch_rows * seq_len
        top_k = idx_blk.shape[-1]
        head_dim = qkv_shard.shape[3]
        experts = gate_shard.shape[0] * ep_count
        capacity = capacity_of(tokens, top_k, experts)
        pad_cap = 16 * ((capacity + 15) // 16)
        by_choice = [blk.reshape(tokens, top_k).T for blk in (idx_blk, slot_blk, gate_blk)]
        gains = [gain.astype(jnp.float32)[None, :] for gain in (attn_gain, moe_gain)]
        qkv = qkv_shard.reshape(qkv_shard.shape[0], -1)
        proj = out_shard.reshape(-1, d_model)
        result = whole_layer(head_dim, pad_cap, x_blk.reshape(tokens, d_model), *by_choice, *gains, qkv, proj, gate_shard, up_shard, down_shard, experts)
        return result.reshape(batch_rows, seq_len, d_model)

    return jax.shard_map(local_step, mesh=mesh, in_specs=(tok_spec, tok_spec, tok_spec, tok_spec, P(None), P('fsdp', None, None, None), P('fsdp', None, None), P(None), P('ep', 'fsdp', None), P('ep', 'fsdp', None), P('ep', None, 'fsdp')), out_specs=tok_spec, check_vma=False)
```

time: 828 us -> 293 us (0.35)
  the two profiles are of different devices: /device:TPU:0 before, /device:TPU:8 now
where the time goes in v3:
time: 293 us; the launch traced here: 292 us
  Pallas kernels  285 us (97%)
  local copies, waits for them, and re-layouts  4.86 us (2%)
    pallas_call x1, Pallas kernels, whole_layer(): pl.pallas_call(functools.partial(layer_kernel, head_dim, pad_cap), out_sh...  285 us

profile of v3, /device:TPU:8, one launch (start us, length us, event | category | flops | bytes accessed | tf_op | source)
XLA Modules:
  0.0 292.4 jit_solution(3001452507512625385)
XLA Ops:
  0.0 1.3 broadcast_in_dim.14
  1.3 1.3 broadcast_in_dim.15
  2.5 2.6 copy.15.qkv_hbm
  5.1 285.0 %whole_layer.1 = (bf16[512,1024]{1,0:T(8,128)(2,1)}, bf16[8,544,1024]{2,1,0:T(8,128)(2,1)}) custom-call(bf16[512,1024]{1,0:T(8,128)(2,1)} %bitcast.19, s32[8,512]{1,0:T(8,128)} %bitcast.21, s32[8,512]{1,0:T(8,128)} %bitcast.22, bf16[8,512]{1,0:T(8,128)(2,1)} %bitcast.23, f32[1,1024]{1,0:T(1,128)} %bitcast.17, f32[1,1024]{1,0:T(1,128)} %bitcast.18, ...), custom_call_target="tpu_custom_call" | custom-call | flops 40000000000 | bytes 30000000 | tf_op jit(solution)/shard_map/whole_layer/pallas_call | solution.py:575
  290.1 2.3 copy.17

commit v4 on v3

--- a/solution.py
+++ b/solution.py
@@ -262,9 +262,6 @@
     passes = ((end_z, mid_z), (mid_z, end_z), (far_z, end_z))
 
     def send_own(j):
-        if j >= chunks:
-            return
-
         @pl.when(dz > 0)
         def _():
             for copy in own_copies(0, j):
@@ -275,14 +272,17 @@
             for copy in own_copies(1, j):
                 copy.start()
 
-    def serve(j):
+    def forward(kinds, js):
         @pl.when(inside)
         def _():
-            for which, (p, z) in enumerate(passes):
-                wait_chunk(p, j)
-                for copy in pass_copies(which, p, j, z):
-                    copy.start()
-        send_own(j + 2)
+            for j in js:
+                for which in kinds:
+                    p, z = passes[which]
+                    wait_chunk(p, j)
+                    for copy in pass_copies(which, p, j, z):
+                        copy.start()
+
+    near, far, expert_js, down_js = (0, 1), (2,), range(n_exp), range(n_exp, chunks)
 
     def need(j):
         @pl.when(at_end)
@@ -290,8 +290,8 @@
             for k in range(3):
                 wait_chunk(k + 1 - upper, j)
 
-    send_own(0)
-    send_own(1)
+    for j in expert_js:
+        send_own(j)
     own_loads = []
     for b in range(4):
         rows = pl.ds(pl.multiple_of(dz * shard_rows, shard_rows), shard_rows)
@@ -335,7 +335,6 @@
     for _ in range(4):
         for _, _, stream in streams:
             next(stream)
-    serve(0)
     for copy in own_loads:
         copy.wait()
 
@@ -358,12 +357,14 @@
     next(stream)
     tok_copy = pltpu.make_async_copy(own_tok, tok_hbm.at[mine], tok_sem)
     tok_copy.start()
-    serve(1)
+    forward(near, expert_js)
     for _ in range(4):
         next(stream)
     tok_copy.wait()
     tok_sender.drain()
-    serve(2)
+    forward(far, expert_js)
+    for j in down_js:
+        send_own(j)
 
     def tok_in(s):
         return pltpu.make_async_copy(tok_hbm.at[s], work.at[s % 2], tok_load.at[s % 2])
@@ -398,7 +399,6 @@
         return carry
 
     lax.fori_loop(0, n_src, dispatch_body, 0)
-    serve(3)
 
     row_tile = n_rows // 4
 
@@ -415,15 +415,13 @@
 
         lax.fori_loop(0, 4, tile_body, 0)
 
-    for e in range(n_exp - 1):
+    for e in range(n_exp):
         expert_inner(e)
-    serve(4)
-    expert_inner(n_exp - 1)
 
     def block_of(i):
-        if isinstance(i, int) and i < n_sub:
-            return dz, i
-        k, sub = (i - n_sub) % 3 + 1, (i - n_sub) // 3
+        k, sub = i // n_sub, i % n_sub
+        if isinstance(i, int) and k == 0:
+            return dz, sub
         near_end = dz + upper * (3 - 2 * dz)
         low = k - near_end * ((3 - k) // 2)
         return low + upper * (3 - 2 * low), sub
@@ -448,7 +446,7 @@
         rel, target = ((2, across_y), (1, across_x))[which]
         return remote(acc.at[i % 2, rel, halves[which]], got_last.at[i % 3, which], last_send.at[i, which], last_recv.at[i, which], target)
 
-    def start_block(i):
+    def y_block(i):
         p, sub = block_of(i)
         if not (isinstance(i, int) and i < n_sub):
             @pl.when(at_end)
@@ -464,6 +462,7 @@
 
         lax.fori_loop(0, n_exp, y_body, 0)
 
+    def sum_block(i):
         def partial(rel, core_rel):
             slot = rel_slot(rel, core_rel)
             return jnp.dot(comb[slot], y_buf[slot], preferred_element_type=jnp.float32)
@@ -519,26 +518,38 @@
             last_copy(i, which).wait_send()
 
     blocks = 4 * n_sub
-    start_block(0)
+    y_block(0)
+    sum_block(0)
+    forward(near, down_js)
+    y_block(1)
     turn_block(0)
-    start_block(1)
-    serve(5)
+    sum_block(1)
     end_block(0)
+    y_block(2)
     turn_block(1)
-    start_block(2)
+    sum_block(2)
+    forward(far, down_js)
     end_block(1)
 
     def block_body(i, carry):
+        y_block(i + 1)
         turn_block(i)
-
-        @pl.when(i + 1 < blocks)
-        def _():
-            start_block(i + 1)
-
+        sum_block(i + 1)
         end_block(i)
         return carry
 
-    lax.fori_loop(2, blocks, block_body, 0)
+    lax.fori_loop(2, blocks - 3, block_body, 0)
+
+    def late_body(i, carry):
+        turn_block(i)
+        y_block(i + 1)
+        sum_block(i + 1)
+        end_block(i)
+        return carry
+
+    lax.fori_loop(blocks - 3, blocks - 1, late_body, 0)
+    turn_block(blocks - 1)
+    end_block(blocks - 1)
 
     for j in range(chunks):
         @pl.when(dz > 0)

time: 293 us -> 254 us (0.87)
  the two profiles are of different devices: /device:TPU:8 before, /device:TPU:0 now
where the time goes in v4:
time: 254 us
  Pallas kernels  246 us (97%)
  local copies, waits for them, and re-layouts  4.86 us (2%)
  other arithmetic  2.55 us (1%)
    pallas_call x1, Pallas kernels, whole_layer(): pl.pallas_call(functools.partial(layer_kernel, head_dim, pad_cap), out_sh...  246 us

profile of v4, /device:TPU:0, one launch (start us, length us, event | category | flops | bytes accessed | tf_op | source)
XLA Modules:
  0.0 253.9 jit_solution(16271633018142849656)
XLA Ops:
  0.0 1.3 broadcast_in_dim.14
  1.3 1.3 broadcast_in_dim.15
  2.5 2.6 %copy.15.qkv_hbm = bf16[256,3072]{1,0:T(8,128)(2,1)} copy(bf16[256,3072]{0,1:T(8,128)(2,1)} %bitcast.15) | data formatting | bytes 3145728 | tf_op jit(solution)/shard_map/reshape | solution.py:633
  5.1 246.5 %whole_layer.1 = (bf16[512,1024]{1,0:T(8,128)(2,1)}, bf16[8,544,1024]{2,1,0:T(8,128)(2,1)}) custom-call(bf16[512,1024]{1,0:T(8,128)(2,1)} %bitcast.19, s32[8,512]{1,0:T(8,128)} %bitcast.21, s32[8,512]{1,0:T(8,128)} %bitcast.22, bf16[8,512]{1,0:T(8,128)(2,1)} %bitcast.23, f32[1,1024]{1,0:T(1,128)} %bitcast.17, f32[1,1024]{1,0:T(1,128)} %bitcast.18, ...), custom_call_target="tpu_custom_call" | custom-call | flops 40000000000 | bytes 30000000 | tf_op jit(solution)/shard_map/whole_layer/pallas_call | solution.py:586
  251.6 2.3 copy.17

commit v5 on v4

--- a/solution.py
+++ b/solution.py
@@ -63,77 +63,64 @@
     pltpu.make_async_copy(ref, ref, sem).wait()
 
 
-class Sender:
-    def __init__(self, send_sems):
-        self.send_sems = send_sems
-        self.copies = []
-
-    def send(self, src, dst, recv_sem, place):
-        copy = remote(src, dst, self.send_sems.at[len(self.copies)], recv_sem, place)
-        copy.start()
-        self.copies.append(copy)
-
-    def drain(self):
-        for copy in self.copies:
-            copy.wait_send()
-
-
-def spread_in_layer(place, sender, own_src, part_ref, recv_sems):
+def spread_in_layer(place, own_refs, part_refs, send_sem, direct_sems, partner_sem, half_size, partner_size):
     across_x, across_y, partner = related(place, 1, 0), related(place, 2, 0), related(place, 0, 1)
 
-    def pass_on(chip_rel, half, target, rel_there, core_there, first=False):
+    def pass_on(chip_rel, half, target, sem, first=False):
         owner = slot_of(related(place, chip_rel, 0))
-        src = own_src(half) if first else part_ref(owner, half)
-        sender.send(src, part_ref(owner, half), recv_sems(rel_there, core_there, half), target)
+        dsts = part_refs(owner, half)
+        for src, dst in zip(own_refs(half) if first else dsts, dsts):
+            remote(src, dst, send_sem, sem, target).start()
+
+    def direct(rel_there, half):
+        return direct_sems.at[rel_there - 1, half]
 
     for half in (0, 1):
-        pass_on(0, half, across_x, 1, 0, True)
-        pass_on(0, 1 - half, across_y, 2, 0, True)
+        pass_on(0, half, across_x, direct(1, half), True)
+        pass_on(0, 1 - half, across_y, direct(2, 1 - half), True)
     for half in (0, 1):
-        pass_on(0, half, partner, 0, 1, True)
+        pass_on(0, half, partner, partner_sem, True)
     yield
 
-    def arrived(chip_rel, core_rel, half):
-        owner = slot_of(related(place, chip_rel, core_rel))
-        wait_in(part_ref(owner, half), recv_sems(chip_rel, core_rel, half))
-
-    arrived(1, 0, 0)
-    pass_on(1, 0, across_y, 3, 0)
-    pass_on(1, 0, partner, 1, 1)
-    arrived(2, 0, 1)
-    pass_on(2, 1, across_x, 3, 0)
-    pass_on(2, 1, partner, 2, 1)
+    def arrived(chip_rel, half):
+        wait_in(half_size, direct(chip_rel, half))
+
+    arrived(1, 0)
+    pass_on(1, 0, across_y, direct(3, 0))
+    pass_on(1, 0, partner, partner_sem)
+    arrived(2, 1)
+    pass_on(2, 1, across_x, direct(3, 1))
+    pass_on(2, 1, partner, partner_sem)
     yield
-    arrived(1, 0, 1)
-    pass_on(1, 1, partner, 1, 1)
-    arrived(2, 0, 0)
-    pass_on(2, 0, partner, 2, 1)
+    arrived(1, 1)
+    pass_on(1, 1, partner, partner_sem)
+    arrived(2, 0)
+    pass_on(2, 0, partner, partner_sem)
     yield
-    arrived(3, 0, 0)
-    pass_on(3, 0, partner, 3, 1)
-    arrived(3, 0, 1)
-    pass_on(3, 1, partner, 3, 1)
+    arrived(3, 0)
+    pass_on(3, 0, partner, partner_sem)
+    arrived(3, 1)
+    pass_on(3, 1, partner, partner_sem)
     yield
-    for chip_rel in range(4):
-        for half in (0, 1):
-            arrived(chip_rel, 1, half)
+    wait_in(partner_size, partner_sem)
     yield
 
 
 def norm_rows(src, gain_ref, dst, rows):
     tile = 128
+    gain = gain_ref[...].astype(jnp.float32).reshape(1, -1)
 
     def body(t, carry):
         at = pl.ds(pl.multiple_of(t * tile, tile), tile)
         wide = src[at].astype(jnp.float32)
         inv_rms = lax.rsqrt(jnp.mean(wide * wide, axis=-1, keepdims=True) + NORM_EPS)
-        dst[at] = (wide * inv_rms * gain_ref[...]).astype(jnp.bfloat16)
+        dst[at] = (wide * inv_rms * gain).astype(jnp.bfloat16)
         return carry
 
     lax.fori_loop(0, rows // tile, body, 0)
 
 
-def attend(x_ref, normed, weights, cos_ref, sin_ref, qkv, hidden, head_dim):
+def attend(x_ref, normed, weights, rope, qkv, hidden, head_dim):
     tokens, d_model = x_ref.shape
     lane = lax.broadcasted_iota(jnp.int32, (tokens, LANES), 1)
     low_half = lane % head_dim < head_dim // 2
@@ -144,10 +131,10 @@
 
     def rotate(val):
         swapped = jnp.where(low_half, pltpu.roll(val, LANES - head_dim // 2, 1), pltpu.roll(val, head_dim // 2, 1))
-        return (val * cos_ref[...] + swapped * sin_ref[...]).astype(jnp.bfloat16)
+        return (val * rope[0] + swapped * rope[1]).astype(jnp.bfloat16)
 
     def project(b, cols):
-        return jnp.dot(normed[:tokens], weights[b, :d_model, cols], preferred_element_type=jnp.float32)
+        return lax.dot_general(normed[:tokens], weights[b, cols, :], (((1,), (1,)), ((), ())), preferred_element_type=jnp.float32)
 
     def group_body(g, carry):
         cols = pl.ds(pl.multiple_of(g * group, group), group)
@@ -191,11 +178,11 @@
 
 
 def layer_kernel(head_dim, pad_cap,
-                 x_ref, idx_ref, slot_ref, gate_ref, attn_gain_ref, moe_gain_ref, cos_ref, sin_ref,
-                 qkv_hbm, proj_hbm, gate_hbm, up_hbm, down_hbm,
+                 idx_ref, slot_ref, gate_ref, attn_gain_ref, moe_gain_ref,
+                 x_hbm, rope_hbm, qkv_hbm, proj_hbm, gate_hbm, up_hbm, down_hbm,
                  out_ref, tok_hbm,
-                 big, gate_up, down_all, work, own_tok, hidden, inner, comb, y_buf, send_core, acc, got_core, got_x, got_y, got_last,
-                 attn_send, attn_z_send, attn_z_recv, attn_recv, load_sems, tok_send, tok_recv, tok_sem, tok_load,
+                 x_ref, rope, big, gate_up, down_all, work, own_tok, hidden, inner, comb, y_buf, send_core, acc, got_core, got_x, got_y, got_last,
+                 attn_send, attn_z_send, attn_z_recv, attn_direct, attn_partner, load_sems, tok_send, tok_direct, tok_partner, tok_sem, tok_load,
                  z_own, z_pass, z_recv, core_send, core_recv, x_send, x_recv, y_send, y_recv, last_send, last_recv):
     place = layer_place()
     dx, dz, dy, dc = place
@@ -217,25 +204,35 @@
     def at_z(z):
         return (dx, z, dy, dc)
 
+    x_copy_in = pltpu.make_async_copy(x_hbm, x_ref, load_sems.at[0])
+    rope_copy_in = pltpu.make_async_copy(rope_hbm, rope, load_sems.at[1])
+    x_copy_in.start()
+    rope_copy_in.start()
     barrier = pltpu.get_barrier_semaphore()
     for target in [at_z((dz + step) % 4) for step in (1, 2, 3)] + [across_x, across_y, partner]:
         pl.semaphore_signal(barrier, inc=1, device_id=dev_id(target), device_id_type=MESH_ID)
     pl.semaphore_wait(barrier, 6)
 
-    shard_rows = qkv_hbm.shape[0]
-    piece = shard_rows // 8
-
-    def attn_src(b, rows):
-        return proj_hbm.at[rows] if b == 3 else qkv_hbm.at[rows, pl.ds(b * d_model, d_model)]
-
-    my_rows = pl.ds(pl.multiple_of(mine * piece, piece), piece)
-    landing = pl.ds(pl.multiple_of(dz * shard_rows + mine * piece, piece), piece)
-    z_copies = []
-    for index, step in enumerate((1, 3, 2)):
-        for b in range(4):
-            copy = remote(attn_src(b, my_rows), big.at[b, landing], attn_z_send.at[index, b], attn_z_recv.at[index, b], at_z((dz + step) % 4))
-            copy.start()
-            z_copies.append(copy)
+    shard_rows = proj_hbm.shape[0]
+    row_piece, col_piece = shard_rows // 8, d_model // 8
+
+    def qkv_rows(start, rows, col_z=None):
+        at = pl.ds(pl.multiple_of(start, rows), rows)
+        if col_z is None:
+            return qkv_hbm.at[:, at]
+        return big.at[pl.ds(0, 3), at, pl.ds(pl.multiple_of(col_z * shard_rows, shard_rows), shard_rows)]
+
+    def proj_rows(start, rows):
+        return big.at[3, pl.ds(pl.multiple_of(start, rows), rows)]
+
+    def size_of(halves):
+        return big.at[0, pl.ds(0, halves * row_piece * 2)]
+
+    z_steps = (1, 3, 2)
+    for index, step in enumerate(z_steps):
+        proj_src = proj_hbm.at[pl.ds(pl.multiple_of(mine * row_piece, row_piece), row_piece)]
+        for src, dst in ((qkv_rows(mine * col_piece, col_piece), qkv_rows(mine * col_piece, col_piece, dz)), (proj_src, proj_rows(dz * shard_rows + mine * row_piece, row_piece))):
+            remote(src, dst, attn_z_send.at[index], attn_z_recv.at[index], at_z((dz + step) % 4)).start()
 
     def chunk_refs(p, j):
         if j < n_exp:
@@ -249,14 +246,16 @@
 
     def own_copies(side, j):
         target = at_z(dz - 1 if side == 0 else dz + 1)
-        return [remote(src, dst, z_own.at[side, j, m], z_recv.at[dz, j, m], target) for m, (src, dst) in enumerate(zip(chunk_srcs(j), chunk_refs(dz, j)))]
-
-    def pass_copies(which, p, j, z):
-        return [remote(ref, ref, z_pass.at[which, j, m], z_recv.at[p, j, m], at_z(z)) for m, ref in enumerate(chunk_refs(p, j))]
+        return [remote(src, dst, z_own.at[side, j // n_exp], z_recv.at[dz, j], target) for src, dst in zip(chunk_srcs(j), chunk_refs(dz, j))]
+
+    def whole_chunk(p, j):
+        return gate_up.at[p, j] if j < n_exp else down_all.at[p, j - n_exp]
+
+    def pass_copy(which, p, j, z):
+        return remote(whole_chunk(p, j), whole_chunk(p, j), z_pass.at[which, j // n_exp], z_recv.at[p, j], at_z(z))
 
     def wait_chunk(p, j):
-        for m, ref in enumerate(chunk_refs(p, j)):
-            wait_in(ref, z_recv.at[p, j, m])
+        wait_in(whole_chunk(p, j), z_recv.at[p, j])
 
     end_z, mid_z, far_z = 3 * (dz - 1), 3 - dz, 3 * (2 - dz)
     passes = ((end_z, mid_z), (mid_z, end_z), (far_z, end_z))
@@ -279,8 +278,7 @@
                 for which in kinds:
                     p, z = passes[which]
                     wait_chunk(p, j)
-                    for copy in pass_copies(which, p, j, z):
-                        copy.start()
+                    pass_copy(which, p, j, z).start()
 
     near, far, expert_js, down_js = (0, 1), (2,), range(n_exp), range(n_exp, chunks)
 
@@ -292,16 +290,16 @@
 
     for j in expert_js:
         send_own(j)
-    own_loads = []
-    for b in range(4):
-        rows = pl.ds(pl.multiple_of(dz * shard_rows, shard_rows), shard_rows)
-        own_loads.append(pltpu.make_async_copy(attn_src(b, pl.ds(0, shard_rows)), big.at[b, rows], load_sems.at[b]))
+    own_loads = [
+        (qkv_hbm, big.at[pl.ds(0, 3), pl.ds(0, d_model), pl.ds(pl.multiple_of(dz * shard_rows, shard_rows), shard_rows)], 2),
+        (proj_hbm, proj_rows(dz * shard_rows, shard_rows), 2),
+    ]
     for j in range(chunks):
-        for m, (src, dst) in enumerate(zip(chunk_srcs(j), chunk_refs(dz, j))):
-            own_loads.append(pltpu.make_async_copy(src, dst, load_sems.at[4 + 2 * j + m]))
-    for copy in own_loads:
-        copy.start()
-
+        own_loads += [(src, dst, 3 + j // n_exp) for src, dst in zip(chunk_srcs(j), chunk_refs(dz, j))]
+    for src, dst, sem in own_loads:
+        pltpu.make_async_copy(src, dst, load_sems.at[sem]).start()
+
+    x_copy_in.wait()
     norm_rows(x_ref, attn_gain_ref, own_tok, tokens)
 
     expert_ids = lax.broadcasted_iota(jnp.int32, (experts, tokens), 0)
@@ -314,46 +312,39 @@
     own_tok[tokens:, :tokens] = (slot_tab - 1.0).astype(jnp.bfloat16)
     own_tok[tokens:, tokens:] = gate_tab.astype(jnp.bfloat16)
 
-    sender = Sender(attn_send)
     streams = []
-    for index, step in enumerate((1, 3, 2)):
+    for index, step in enumerate(z_steps):
         source_z = (dz + 4 - step) % 4
 
-        def part_ref(slot, half, source_z=source_z):
-            start = source_z * shard_rows + slot * piece + half * (piece // 2)
-            return big.at[:, pl.ds(pl.multiple_of(start, piece // 2), piece // 2)]
-
-        def recv_sem(chip_rel, core_rel, half, index=index):
-            return attn_recv.at[index, chip_rel, core_rel, half]
-
-        arrival = pl.ds(pl.multiple_of(source_z * shard_rows + mine * piece, piece), piece)
-        streams.append((arrival, index, spread_in_layer(place, sender, functools.partial(part_ref, mine), part_ref, recv_sem)))
-    for arrival, index, stream in streams:
-        for b in range(4):
-            wait_in(big.at[b, arrival], attn_z_recv.at[index, b])
+        def part_refs(slot, half, source_z=source_z):
+            cols, rows = col_piece // 2, row_piece // 2
+            return [qkv_rows(slot * col_piece + half * cols, cols, source_z), proj_rows(source_z * shard_rows + slot * row_piece + half * rows, rows)]
+
+        streams.append(spread_in_layer(place, functools.partial(part_refs, mine), part_refs, attn_send.at[index], attn_direct.at[index], attn_partner.at[index], size_of(1), size_of(8)))
+    for index, stream in enumerate(streams):
+        wait_in(size_of(2), attn_z_recv.at[index])
         next(stream)
     for _ in range(4):
-        for _, _, stream in streams:
+        for stream in streams:
             next(stream)
-    for copy in own_loads:
-        copy.wait()
-
-    attend(x_ref, own_tok, big, cos_ref, sin_ref, work, hidden, head_dim)
+    wait_in(size_of(16), load_sems.at[2])
+    rope_copy_in.wait()
+
+    attend(x_ref, own_tok, big, rope, work, hidden, head_dim)
     norm_rows(hidden, moe_gain_ref, own_tok, tokens)
-    sender.drain()
-    for copy in z_copies:
-        copy.wait_send()
-
-    tok_sender = Sender(tok_send)
+    for index in range(3):
+        wait_in(size_of(14), attn_send.at[index])
+        wait_in(size_of(2), attn_z_send.at[index])
+
     half_rows = own_tok.shape[0] // 2
 
     def tok_part(slot, half):
-        return tok_hbm.at[slot, pl.ds(half * half_rows, half_rows)]
+        return [tok_hbm.at[slot, pl.ds(half * half_rows, half_rows)]]
 
     def tok_half(half):
-        return own_tok.at[pl.ds(half * half_rows, half_rows)]
-
-    stream = spread_in_layer(place, tok_sender, tok_half, tok_part, lambda chip_rel, core_rel, half: tok_recv.at[chip_rel, core_rel, half])
+        return [own_tok.at[pl.ds(half * half_rows, half_rows)]]
+
+    stream = spread_in_layer(place, tok_half, tok_part, tok_send, tok_direct, tok_partner, tok_part(0, 0)[0], tok_hbm.at[pl.ds(0, 4)])
     next(stream)
     tok_copy = pltpu.make_async_copy(own_tok, tok_hbm.at[mine], tok_sem)
     tok_copy.start()
@@ -361,7 +352,7 @@
     for _ in range(4):
         next(stream)
     tok_copy.wait()
-    tok_sender.drain()
+    wait_in(tok_hbm.at[pl.ds(0, 7)], tok_send)
     forward(far, expert_js)
     for j in down_js:
         send_own(j)
@@ -415,6 +406,8 @@
 
         lax.fori_loop(0, 4, tile_body, 0)
 
+    wait_in(gate_up.at[0], load_sems.at[3])
+    wait_in(down_all.at[0], load_sems.at[4])
     for e in range(n_exp):
         expert_inner(e)
 
@@ -432,26 +425,26 @@
     halves = (pl.ds(0, half_tok), pl.ds(half_tok, half_tok))
 
     def core_copy(i, rel):
-        return remote(send_core.at[i % 2, rel], got_core.at[i % 2, rel], core_send.at[i, rel], core_recv.at[i, rel], partner)
+        return remote(send_core.at[i % 2, rel], got_core.at[i % 2, rel], core_send.at[i % 2, rel], core_recv.at[i % 2, rel], partner)
 
     def x_copy(i, rel):
         where = (3 - rel) // 2
-        return remote(acc.at[i % 2, rel, halves[0]], got_x.at[i % 3, where], x_send.at[i, where], x_recv.at[i, where], across_x)
+        return remote(acc.at[i % 2, rel, halves[0]], got_x.at[i % 3, where], x_send.at[i % 3, where], x_recv.at[i % 3, where], across_x)
 
     def y_copy(i, rel):
         where = 3 - rel
-        return remote(acc.at[i % 2, rel, halves[1]], got_y.at[i % 3, where], y_send.at[i, where], y_recv.at[i, where], across_y)
+        return remote(acc.at[i % 2, rel, halves[1]], got_y.at[i % 3, where], y_send.at[i % 3, where], y_recv.at[i % 3, where], across_y)
 
     def last_copy(i, which):
         rel, target = ((2, across_y), (1, across_x))[which]
-        return remote(acc.at[i % 2, rel, halves[which]], got_last.at[i % 3, which], last_send.at[i, which], last_recv.at[i, which], target)
+        return remote(acc.at[i % 2, rel, halves[which]], got_last.at[i % 3, which], last_send.at[i % 3, which], last_recv.at[i % 3, which], target)
 
     def y_block(i):
         p, sub = block_of(i)
         if not (isinstance(i, int) and i < n_sub):
             @pl.when(at_end)
             def _():
-                wait_in(down_all.at[p, sub], z_recv.at[p, n_exp + sub, 0])
+                wait_in(down_all.at[p, sub], z_recv.at[p, n_exp + sub])
 
         def y_body(e, carry):
             y_tall = jnp.dot(inner[e], down_all[p, sub, e], preferred_element_type=jnp.float32).astype(jnp.bfloat16)
@@ -476,7 +469,7 @@
         def own_body(k, carry):
             rel = 3 - k
             own = partial(rel, 0)
-            wait_in(got_core.at[i % 2, rel], core_recv.at[i, rel])
+            wait_in(got_core.at[i % 2, rel], core_recv.at[i % 2, rel])
             acc[i % 2, rel] = own + got_core[i % 2, rel]
 
             @pl.when(rel % 2 == 1)
@@ -493,10 +486,10 @@
         lax.fori_loop(0, 4, own_body, 0)
 
     def turn_block(i):
-        wait_in(got_x.at[i % 3, 0], x_recv.at[i, 0])
+        wait_in(got_x.at[i % 3, 0], x_recv.at[i % 3, 0])
         acc[i % 2, 2, halves[0]] += got_x[i % 3, 0]
         last_copy(i, 0).start()
-        wait_in(got_y.at[i % 3, 0], y_recv.at[i, 0])
+        wait_in(got_y.at[i % 3, 0], y_recv.at[i % 3, 0])
         acc[i % 2, 1, halves[1]] += got_y[i % 3, 0]
         last_copy(i, 1).start()
 
@@ -504,8 +497,8 @@
         p, sub = block_of(i)
         cols = pl.ds(pl.multiple_of((p * n_sub + sub) * block_cols, block_cols), block_cols)
         for half, got, got_sems in ((0, got_x, x_recv), (1, got_y, y_recv)):
-            wait_in(got.at[i % 3, 1], got_sems.at[i, 1])
-            wait_in(got_last.at[i % 3, half], last_recv.at[i, half])
+            wait_in(got.at[i % 3, 1], got_sems.at[i % 3, 1])
+            wait_in(got_last.at[i % 3, half], last_recv.at[i % 3, half])
             total = acc[i % 2, 0, halves[half]] + got[i % 3, 1] + got_last[i % 3, half]
             out_ref[halves[half], cols] = (hidden[halves[half], cols].astype(jnp.float32) + total).astype(jnp.bfloat16)
         for rel in range(4):
@@ -551,22 +544,19 @@
     turn_block(blocks - 1)
     end_block(blocks - 1)
 
-    for j in range(chunks):
+    for kind, size in ((0, gate_up.at[0]), (1, down_all.at[0])):
         @pl.when(dz > 0)
         def _():
-            for copy in own_copies(0, j):
-                copy.wait_send()
+            wait_in(size, z_own.at[0, kind])
 
         @pl.when(dz < 3)
         def _():
-            for copy in own_copies(1, j):
-                copy.wait_send()
+            wait_in(size, z_own.at[1, kind])
 
         @pl.when(inside)
         def _():
-            for which, (p, z) in enumerate(passes):
-                for copy in pass_copies(which, p, j, z):
-                    copy.wait_send()
+            for which in range(3):
+                wait_in(size, z_pass.at[which, kind])
 
 
 def whole_layer(head_dim, pad_cap, x, idx_t, slot_t, gate_t, attn_gain, moe_gain, qkv, proj, gate_w, up_w, down_w, experts):
@@ -575,20 +565,21 @@
     part_depth, ffn = gate_w.shape[1:]
     parts, n_src, block_cols = 4, 8, LANES
     n_sub = down_w.shape[2] // block_cols
-    blocks = parts * n_sub
     chunks = n_exp + n_sub
     n_rows = n_src * pad_cap
     half = tokens // 2
-    cos_tab, sin_tab = rope_tables(tokens, head_dim)
+    rope = np.stack(rope_tables(tokens, head_dim))
     dma = pltpu.SemaphoreType.DMA
     bf16, f32 = jnp.bfloat16, jnp.float32
     vmem, hbm = pl.BlockSpec(memory_space=pltpu.VMEM), pl.BlockSpec(memory_space=pl.ANY)
     return pl.pallas_call(
         functools.partial(layer_kernel, head_dim, pad_cap),
         out_shape=(jax.ShapeDtypeStruct(x.shape, bf16), jax.ShapeDtypeStruct((n_src, tokens + experts, d_model), bf16)),
-        in_specs=[vmem] * 8 + [hbm] * 5,
+        in_specs=[vmem] * 5 + [hbm] * 7,
         out_specs=(vmem, hbm),
         scratch_shapes=[
+            pltpu.VMEM((tokens, d_model), bf16),
+            pltpu.VMEM(rope.shape, f32),
             pltpu.VMEM((n_exp, n_rows, d_model), bf16),
             pltpu.VMEM((parts, n_exp, 2, part_depth, ffn), bf16),
             pltpu.VMEM((parts, n_sub, n_exp, ffn, block_cols), bf16),
@@ -604,16 +595,15 @@
             pltpu.VMEM((3, 2, half, block_cols), f32),
             pltpu.VMEM((3, 2, half, block_cols), f32),
             pltpu.VMEM((3, 2, half, block_cols), f32),
-            dma((42,)), dma((3, 4)), dma((3, 4)), dma((3, 4, 2, 2)), dma((4 + 2 * chunks,)),
-            dma((14,)), dma((4, 2, 2)), dma, dma((2,)),
-            dma((2, chunks, 2)), dma((3, chunks, 2)), dma((parts, chunks, 2)),
-            dma((blocks, 4)), dma((blocks, 4)), dma((blocks, 2)), dma((blocks, 2)),
-            dma((blocks, 2)), dma((blocks, 2)), dma((blocks, 2)), dma((blocks, 2)),
+            dma((3,)), dma((3,)), dma((3,)), dma((3, 3, 2)), dma((3,)), dma((5,)),
+            dma, dma((3, 2)), dma, dma, dma((2,)),
+            dma((2, 2)), dma((3, 2)), dma((parts, chunks)), dma((2, 4)), dma((2, 4)),
+            dma((3, 2)), dma((3, 2)), dma((3, 2)), dma((3, 2)), dma((3, 2)), dma((3, 2)),
         ],
         compiler_params=pltpu.CompilerParams(collective_id=1, has_side_effects=True, vmem_limit_bytes=63 * 1024 * 1024),
         cost_estimate=pl.CostEstimate(flops=40_000_000_000, bytes_accessed=30_000_000, transcendentals=0),
         name='whole_layer',
-    )(x, idx_t, slot_t, gate_t, attn_gain, moe_gain, cos_tab, sin_tab, qkv, proj, gate_w, up_w, down_w)[0]
+    )(idx_t, slot_t, gate_t, attn_gain, moe_gain, x, rope, qkv, proj, gate_w, up_w, down_w)[0]
 
 
 def solution(mesh):
@@ -629,10 +619,9 @@
         capacity = capacity_of(tokens, top_k, experts)
         pad_cap = 16 * ((capacity + 15) // 16)
         by_choice = [blk.reshape(tokens, top_k).T for blk in (idx_blk, slot_blk, gate_blk)]
-        gains = [gain.astype(jnp.float32)[None, :] for gain in (attn_gain, moe_gain)]
-        qkv = qkv_shard.reshape(qkv_shard.shape[0], -1)
+        qkv = qkv_shard.transpose(1, 2, 3, 0).reshape(3, d_model, -1)
         proj = out_shard.reshape(-1, d_model)
-        result = whole_layer(head_dim, pad_cap, x_blk.reshape(tokens, d_model), *by_choice, *gains, qkv, proj, gate_shard, up_shard, down_shard, experts)
+        result = whole_layer(head_dim, pad_cap, x_blk.reshape(tokens, d_model), *by_choice, attn_gain, moe_gain, qkv, proj, gate_shard, up_shard, down_shard, experts)
         return result.reshape(batch_rows, seq_len, d_model)
 
     return jax.shard_map(local_step, mesh=mesh, in_specs=(tok_spec, tok_spec, tok_spec, tok_spec, P(None), P('fsdp', None, None, None), P('fsdp', None, None), P(None), P('ep', 'fsdp', None), P('ep', 'fsdp', None), P('ep', None, 'fsdp')), out_specs=tok_spec, check_vma=False)

time: 254 us -> 246 us (0.969)
  Pallas kernels: 246 us -> 243 us
  local copies, waits for them, and re-layouts: 4.86 us -> 2.26 us
  other arithmetic: 2.55 us -> 0 us
    pallas_call x1, Pallas kernels: 246 us -> 243 us  [whole_layer(): pl.pallas_call(functools.partial(layer_kernel, head_dim, pad_cap), out_sh...]
    reshape x1 -> x0, local copies, waits for them, and re-layouts: 2.6 us -> none  [local_step(): qkv = qkv_shard.reshape(qkv_shard.shape[0], -1)]
    broadcast_in_dim x2 -> x0, other arithmetic: 2.55 us -> none  [local_step(): gain.astype(jnp.float32)[None, :]]
where the time goes in v5:
time: 246 us; the launch traced here: 245 us
  Pallas kernels  243 us (99%)
    pallas_call x1, Pallas kernels, whole_layer(): pl.pallas_call(functools.partial(layer_kernel, head_dim, pad_cap), out_sh...  243 us

profile of v5, /device:TPU:0, one launch (start us, length us, event | category | flops | bytes accessed | tf_op | source)
XLA Modules:
  0.0 245.4 jit_solution(15336317900887290769)
XLA Ops:
  0.0 243.1 %whole_layer.1 = (bf16[512,1024]{1,0:T(8,128)(2,1)}, bf16[8,544,1024]{2,1,0:T(8,128)(2,1)}) custom-call(s32[8,512]{1,0:T(8,128)} %bitcast.19, s32[8,512]{1,0:T(8,128)} %bitcast.20, bf16[8,512]{1,0:T(8,128)(2,1)} %bitcast.21, bf16[1024]{0:T(1024)(128)(2,1)} %attn_gain_ref.1, bf16[1024]{0:T(1024)(128)(2,1)} %moe_gain_ref.1, bf16[512,1024]{1,0:T(8,128)(2,1)} %bitcast.17, ...), custom_call_target="tpu_custom_call" | custom-call | flops 40000000000 | bytes 30000000 | tf_op jit(solution)/shard_map/whole_layer/pallas_call | solution.py:575
  243.1 2.3 copy.14

commit v6 on v5

--- a/solution.py
+++ b/solution.py
@@ -12,6 +12,8 @@
 ROPE_BASE = 10000.0
 MESH_ID = pl.DeviceIdType.MESH
 LANES = 128
+BOTH = (0, 1)
+LANES_BOTH = (((1,), (1,)), ((), ()))
 
 
 def capacity_of(tok_count, top_k, experts):
@@ -27,6 +29,14 @@
     return np.cos(angles).astype(np.float32), (np.sin(angles) * sign).astype(np.float32)
 
 
+def two(i):
+    return i % 2
+
+
+def three(i):
+    return i % 3
+
+
 def layer_place():
     dx, dz, ep = lax.axis_index('data'), lax.axis_index('fsdp'), lax.axis_index('ep')
     return dx, dz, ep // 2, ep % 2
@@ -75,10 +85,10 @@
     def direct(rel_there, half):
         return direct_sems.at[rel_there - 1, half]
 
-    for half in (0, 1):
+    for half in BOTH:
         pass_on(0, half, across_x, direct(1, half), True)
         pass_on(0, 1 - half, across_y, direct(2, 1 - half), True)
-    for half in (0, 1):
+    for half in BOTH:
         pass_on(0, half, partner, partner_sem, True)
     yield
 
@@ -134,29 +144,29 @@
         return (val * rope[0] + swapped * rope[1]).astype(jnp.bfloat16)
 
     def project(b, cols):
-        return lax.dot_general(normed[:tokens], weights[b, cols, :], (((1,), (1,)), ((), ())), preferred_element_type=jnp.float32)
+        return lax.dot_general(normed[:tokens], weights[b, cols, :], LANES_BOTH, preferred_element_type=jnp.float32)
 
     def group_body(g, carry):
         cols = pl.ds(pl.multiple_of(g * group, group), group)
         query, keys = project(0, cols), project(1, cols)
         values = project(2, cols).astype(jnp.bfloat16)
-        for pair in (0, 1):
+        for pair in BOTH:
             at = slice(pair * LANES, (pair + 1) * LANES)
             qkv[0, :tokens, at] = rotate(query[:, at])
             qkv[1, :tokens, at] = rotate(keys[:, at])
             qkv[2, :tokens, at] = values[:, at]
-        for pair in (0, 1):
+        for pair in BOTH:
             at = slice(pair * LANES, (pair + 1) * LANES)
-            for tile in (0, 1):
+            for tile in BOTH:
                 n_keys = (tile + 1) * q_tile
                 q_pair = qkv[0, tile * q_tile:(tile + 1) * q_tile, at]
                 k_pair, v_pair = qkv[1, :n_keys, at], qkv[2, :n_keys, at]
                 row_id = lax.broadcasted_iota(jnp.int32, (q_tile, n_keys), 0) + tile * q_tile
                 causal = row_id >= lax.broadcasted_iota(jnp.int32, (q_tile, n_keys), 1)
                 outs = []
-                for head in (0, 1):
+                for head in BOTH:
                     q_head = jnp.where(first_head if head == 0 else ~first_head, q_pair, jnp.zeros((), jnp.bfloat16))
-                    scores = lax.dot_general(q_head, k_pair, (((1,), (1,)), ((), ())), preferred_element_type=jnp.float32)
+                    scores = lax.dot_general(q_head, k_pair, LANES_BOTH, preferred_element_type=jnp.float32)
                     scores = jnp.where(causal, scores * scale, -1e30)
                     top = jnp.max(scores, axis=-1, keepdims=True)
                     weight = jnp.exp(scores - top)
@@ -178,11 +188,10 @@
 
 
 def layer_kernel(head_dim, pad_cap,
-                 idx_ref, slot_ref, gate_ref, attn_gain_ref, moe_gain_ref,
-                 x_hbm, rope_hbm, qkv_hbm, proj_hbm, gate_hbm, up_hbm, down_hbm,
+                 idx_hbm, slot_hbm, gate_idx_hbm, attn_gain_hbm, moe_gain_hbm, x_hbm, rope_hbm, qkv_hbm, proj_hbm, gate_hbm, up_hbm, down_hbm,
                  out_ref, tok_hbm,
-                 x_ref, rope, big, gate_up, down_all, work, own_tok, hidden, inner, comb, y_buf, send_core, acc, got_core, got_x, got_y, got_last,
-                 attn_send, attn_z_send, attn_z_recv, attn_direct, attn_partner, load_sems, tok_send, tok_direct, tok_partner, tok_sem, tok_load,
+                 idx_ref, slot_ref, gate_ref, attn_gain_ref, moe_gain_ref, x_ref, rope, gate_act, big, gate_up, down_all, work, own_tok, hidden, inner, comb, y_buf, send_core, acc, got_core, got_x, got_y, got_last,
+                 attn_send, attn_z_send, attn_z_recv, attn_direct, attn_partner, load_sems, tok_send, tok_direct, tok_partner, tok_sem, tok_load, small_sems,
                  z_own, z_pass, z_recv, core_send, core_recv, x_send, x_recv, y_send, y_recv, last_send, last_recv):
     place = layer_place()
     dx, dz, dy, dc = place
@@ -193,7 +202,7 @@
     block_cols = acc.shape[-1]
     half_tok = tokens // 2
     n_sub = down_all.shape[1]
-    chunks = n_exp + n_sub
+    chunks = n_exp + 1 + n_sub
     across_x, across_y, partner = related(place, 1, 0), related(place, 2, 0), related(place, 0, 1)
     upper = dz // 2
     inside = (dz == 1) | (dz == 2)
@@ -206,8 +215,9 @@
 
     x_copy_in = pltpu.make_async_copy(x_hbm, x_ref, load_sems.at[0])
     rope_copy_in = pltpu.make_async_copy(rope_hbm, rope, load_sems.at[1])
-    x_copy_in.start()
-    rope_copy_in.start()
+    small_copies = [pltpu.make_async_copy(src, dst, small_sems.at[n]) for n, (src, dst) in enumerate(((idx_hbm, idx_ref), (slot_hbm, slot_ref), (gate_idx_hbm, gate_ref), (attn_gain_hbm, attn_gain_ref), (moe_gain_hbm, moe_gain_ref)))]
+    for copy in [x_copy_in, rope_copy_in] + small_copies:
+        copy.start()
     barrier = pltpu.get_barrier_semaphore()
     for target in [at_z((dz + step) % 4) for step in (1, 2, 3)] + [across_x, across_y, partner]:
         pl.semaphore_signal(barrier, inc=1, device_id=dev_id(target), device_id_type=MESH_ID)
@@ -234,25 +244,34 @@
         for src, dst in ((qkv_rows(mine * col_piece, col_piece), qkv_rows(mine * col_piece, col_piece, dz)), (proj_src, proj_rows(dz * shard_rows + mine * row_piece, row_piece))):
             remote(src, dst, attn_z_send.at[index], attn_z_recv.at[index], at_z((dz + step) % 4)).start()
 
+    last_exp = n_exp - 1
+
     def chunk_refs(p, j):
-        if j < n_exp:
-            return [gate_up.at[p, j, m] for m in (0, 1)]
-        return [down_all.at[p, j - n_exp]]
+        if j < last_exp:
+            return [gate_up.at[p, j, m] for m in BOTH]
+        if j <= n_exp:
+            return [gate_up.at[p, last_exp, j - last_exp]]
+        return [down_all.at[p, j - n_exp - 1]]
 
     def chunk_srcs(j):
-        if j < n_exp:
+        if j < last_exp:
             return [gate_hbm.at[first_exp + j], up_hbm.at[first_exp + j]]
-        return [down_hbm.at[pl.ds(first_exp, n_exp), :, pl.ds((j - n_exp) * block_cols, block_cols)]]
+        if j <= n_exp:
+            return [(gate_hbm, up_hbm)[j - last_exp].at[first_exp + last_exp]]
+        return [down_hbm.at[pl.ds(first_exp, n_exp), :, pl.ds((j - n_exp - 1) * block_cols, block_cols)]]
+
+    def kind_of(j):
+        return 0 if j <= n_exp else 1
 
     def own_copies(side, j):
         target = at_z(dz - 1 if side == 0 else dz + 1)
-        return [remote(src, dst, z_own.at[side, j // n_exp], z_recv.at[dz, j], target) for src, dst in zip(chunk_srcs(j), chunk_refs(dz, j))]
+        return [remote(src, dst, z_own.at[side, kind_of(j)], z_recv.at[dz, j], target) for src, dst in zip(chunk_srcs(j), chunk_refs(dz, j))]
 
     def whole_chunk(p, j):
-        return gate_up.at[p, j] if j < n_exp else down_all.at[p, j - n_exp]
+        return gate_up.at[p, j] if j < last_exp else chunk_refs(p, j)[0]
 
     def pass_copy(which, p, j, z):
-        return remote(whole_chunk(p, j), whole_chunk(p, j), z_pass.at[which, j // n_exp], z_recv.at[p, j], at_z(z))
+        return remote(whole_chunk(p, j), whole_chunk(p, j), z_pass.at[which, kind_of(j)], z_recv.at[p, j], at_z(z))
 
     def wait_chunk(p, j):
         wait_in(whole_chunk(p, j), z_recv.at[p, j])
@@ -280,7 +299,7 @@
                     wait_chunk(p, j)
                     pass_copy(which, p, j, z).start()
 
-    near, far, expert_js, down_js = (0, 1), (2,), range(n_exp), range(n_exp, chunks)
+    near, far, expert_js, down_js = BOTH, (2,), range(n_exp + 1), range(n_exp + 1, chunks)
 
     def need(j):
         @pl.when(at_end)
@@ -295,11 +314,12 @@
         (proj_hbm, proj_rows(dz * shard_rows, shard_rows), 2),
     ]
     for j in range(chunks):
-        own_loads += [(src, dst, 3 + j // n_exp) for src, dst in zip(chunk_srcs(j), chunk_refs(dz, j))]
+        own_loads += [(src, dst, 3 + kind_of(j)) for src, dst in zip(chunk_srcs(j), chunk_refs(dz, j))]
     for src, dst, sem in own_loads:
         pltpu.make_async_copy(src, dst, load_sems.at[sem]).start()
 
-    x_copy_in.wait()
+    for copy in [x_copy_in] + small_copies:
+        copy.wait()
     norm_rows(x_ref, attn_gain_ref, own_tok, tokens)
 
     expert_ids = lax.broadcasted_iota(jnp.int32, (experts, tokens), 0)
@@ -393,23 +413,30 @@
 
     row_tile = n_rows // 4
 
+    def tile_loop(body):
+        def tile_body(t, carry):
+            body(pl.ds(pl.multiple_of(t * row_tile, row_tile), row_tile))
+            return carry
+
+        lax.fori_loop(0, 4, tile_body, 0)
+
+    def product(e, m, at):
+        return jnp.dot(big[e, at], gate_up[:, e, m].reshape(d_model, ffn), preferred_element_type=jnp.float32)
+
     def expert_inner(e):
+        def body(at):
+            gate = product(e, 0, at)
+            inner[e, at] = (gate * jax.nn.sigmoid(gate) * product(e, 1, at)).astype(jnp.bfloat16)
+
         need(e)
-
-        def tile_body(t, carry):
-            at = pl.ds(pl.multiple_of(t * row_tile, row_tile), row_tile)
-            rows = big[e, at]
-            gate_act = jnp.dot(rows, gate_up[:, e, 0].reshape(d_model, ffn), preferred_element_type=jnp.float32)
-            up_act = jnp.dot(rows, gate_up[:, e, 1].reshape(d_model, ffn), preferred_element_type=jnp.float32)
-            inner[e, at] = (gate_act * jax.nn.sigmoid(gate_act) * up_act).astype(jnp.bfloat16)
-            return carry
-
-        lax.fori_loop(0, 4, tile_body, 0)
-
-    wait_in(gate_up.at[0], load_sems.at[3])
-    wait_in(down_all.at[0], load_sems.at[4])
-    for e in range(n_exp):
-        expert_inner(e)
+        tile_loop(body)
+
+    def last_gate(at):
+        gate = product(last_exp, 0, at)
+        gate_act[at] = gate * jax.nn.sigmoid(gate)
+
+    def last_up(at):
+        inner[last_exp, at] = (gate_act[at] * product(last_exp, 1, at)).astype(jnp.bfloat16)
 
     def block_of(i):
         k, sub = i // n_sub, i % n_sub
@@ -425,26 +452,30 @@
     halves = (pl.ds(0, half_tok), pl.ds(half_tok, half_tok))
 
     def core_copy(i, rel):
-        return remote(send_core.at[i % 2, rel], got_core.at[i % 2, rel], core_send.at[i % 2, rel], core_recv.at[i % 2, rel], partner)
+        return remote(send_core.at[two(i), rel], got_core.at[two(i), rel], core_send.at[two(i), rel], core_recv.at[two(i), rel], partner)
 
     def x_copy(i, rel):
         where = (3 - rel) // 2
-        return remote(acc.at[i % 2, rel, halves[0]], got_x.at[i % 3, where], x_send.at[i % 3, where], x_recv.at[i % 3, where], across_x)
+        return remote(acc.at[two(i), rel, halves[0]], got_x.at[three(i), where], x_send.at[three(i), where], x_recv.at[three(i), where], across_x)
 
     def y_copy(i, rel):
         where = 3 - rel
-        return remote(acc.at[i % 2, rel, halves[1]], got_y.at[i % 3, where], y_send.at[i % 3, where], y_recv.at[i % 3, where], across_y)
+        return remote(acc.at[two(i), rel, halves[1]], got_y.at[three(i), where], y_send.at[three(i), where], y_recv.at[three(i), where], across_y)
 
     def last_copy(i, which):
         rel, target = ((2, across_y), (1, across_x))[which]
-        return remote(acc.at[i % 2, rel, halves[which]], got_last.at[i % 3, which], last_send.at[i % 3, which], last_recv.at[i % 3, which], target)
-
-    def y_block(i):
+        return remote(acc.at[two(i), rel, halves[which]], got_last.at[three(i), which], last_send.at[three(i), which], last_recv.at[three(i), which], target)
+
+    def wait_down(i):
         p, sub = block_of(i)
         if not (isinstance(i, int) and i < n_sub):
             @pl.when(at_end)
             def _():
-                wait_in(down_all.at[p, sub], z_recv.at[p, n_exp + sub])
+                wait_in(down_all.at[p, sub], z_recv.at[p, n_exp + 1 + sub])
+
+    def y_block(i, low=0, high=n_exp):
+        p, sub = block_of(i)
+        wait_down(i)
 
         def y_body(e, carry):
             y_tall = jnp.dot(inner[e], down_all[p, sub, e], preferred_element_type=jnp.float32).astype(jnp.bfloat16)
@@ -453,24 +484,30 @@
                 y_buf[s, at] = y_tall[s * pad_cap:(s + 1) * pad_cap]
             return carry
 
-        lax.fori_loop(0, n_exp, y_body, 0)
-
-    def sum_block(i):
+        lax.fori_loop(low, high, y_body, 0)
+
+    def sum_block(i, with_y=False):
+        p, sub = block_of(i)
+
         def partial(rel, core_rel):
             slot = rel_slot(rel, core_rel)
+            if with_y:
+                rows = pl.ds(pl.multiple_of(slot * pad_cap, pad_cap), pad_cap)
+                for e in range(n_exp):
+                    y_buf[slot, e * pad_cap:(e + 1) * pad_cap] = jnp.dot(inner[e, rows], down_all[p, sub, e], preferred_element_type=jnp.float32).astype(jnp.bfloat16)
             return jnp.dot(comb[slot], y_buf[slot], preferred_element_type=jnp.float32)
 
         def core_body(k, carry):
             rel = 3 - k
-            send_core[i % 2, rel] = partial(rel, 1)
+            send_core[two(i), rel] = partial(rel, 1)
             core_copy(i, rel).start()
             return carry
 
         def own_body(k, carry):
             rel = 3 - k
             own = partial(rel, 0)
-            wait_in(got_core.at[i % 2, rel], core_recv.at[i % 2, rel])
-            acc[i % 2, rel] = own + got_core[i % 2, rel]
+            wait_in(got_core.at[two(i), rel], core_recv.at[two(i), rel])
+            acc[two(i), rel] = own + got_core[two(i), rel]
 
             @pl.when(rel % 2 == 1)
             def _():
@@ -486,20 +523,20 @@
         lax.fori_loop(0, 4, own_body, 0)
 
     def turn_block(i):
-        wait_in(got_x.at[i % 3, 0], x_recv.at[i % 3, 0])
-        acc[i % 2, 2, halves[0]] += got_x[i % 3, 0]
+        wait_in(got_x.at[three(i), 0], x_recv.at[three(i), 0])
+        acc[two(i), 2, halves[0]] += got_x[three(i), 0]
         last_copy(i, 0).start()
-        wait_in(got_y.at[i % 3, 0], y_recv.at[i % 3, 0])
-        acc[i % 2, 1, halves[1]] += got_y[i % 3, 0]
+        wait_in(got_y.at[three(i), 0], y_recv.at[three(i), 0])
+        acc[two(i), 1, halves[1]] += got_y[three(i), 0]
         last_copy(i, 1).start()
 
     def end_block(i):
         p, sub = block_of(i)
         cols = pl.ds(pl.multiple_of((p * n_sub + sub) * block_cols, block_cols), block_cols)
         for half, got, got_sems in ((0, got_x, x_recv), (1, got_y, y_recv)):
-            wait_in(got.at[i % 3, 1], got_sems.at[i % 3, 1])
-            wait_in(got_last.at[i % 3, half], last_recv.at[i % 3, half])
-            total = acc[i % 2, 0, halves[half]] + got[i % 3, 1] + got_last[i % 3, half]
+            wait_in(got.at[three(i), 1], got_sems.at[three(i), 1])
+            wait_in(got_last.at[three(i), half], last_recv.at[three(i), half])
+            total = acc[two(i), 0, halves[half]] + got[three(i), 1] + got_last[three(i), half]
             out_ref[halves[half], cols] = (hidden[halves[half], cols].astype(jnp.float32) + total).astype(jnp.bfloat16)
         for rel in range(4):
             core_copy(i, rel).wait_send()
@@ -507,11 +544,21 @@
             x_copy(i, rel).wait_send()
         for rel in (3, 2):
             y_copy(i, rel).wait_send()
-        for which in (0, 1):
+        for which in BOTH:
             last_copy(i, which).wait_send()
 
+    wait_in(gate_up.at[0], load_sems.at[3])
+    wait_in(down_all.at[0], load_sems.at[4])
+    for e in range(last_exp):
+        expert_inner(e)
+    y_block(0, 0, last_exp)
+    need(last_exp)
+    tile_loop(last_gate)
+    need(n_exp)
+    tile_loop(last_up)
+
     blocks = 4 * n_sub
-    y_block(0)
+    y_block(0, last_exp, n_exp)
     sum_block(0)
     forward(near, down_js)
     y_block(1)
@@ -533,14 +580,14 @@
 
     lax.fori_loop(2, blocks - 3, block_body, 0)
 
-    def late_body(i, carry):
-        turn_block(i)
-        y_block(i + 1)
-        sum_block(i + 1)
-        end_block(i)
-        return carry
-
-    lax.fori_loop(blocks - 3, blocks - 1, late_body, 0)
+    turn_block(blocks - 3)
+    y_block(blocks - 2)
+    sum_block(blocks - 2)
+    end_block(blocks - 3)
+    turn_block(blocks - 2)
+    wait_down(blocks - 1)
+    sum_block(blocks - 1, with_y=True)
+    end_block(blocks - 2)
     turn_block(blocks - 1)
     end_block(blocks - 1)
 
@@ -565,21 +612,23 @@
     part_depth, ffn = gate_w.shape[1:]
     parts, n_src, block_cols = 4, 8, LANES
     n_sub = down_w.shape[2] // block_cols
-    chunks = n_exp + n_sub
+    chunks = n_exp + 1 + n_sub
     n_rows = n_src * pad_cap
     half = tokens // 2
     rope = np.stack(rope_tables(tokens, head_dim))
     dma = pltpu.SemaphoreType.DMA
     bf16, f32 = jnp.bfloat16, jnp.float32
-    vmem, hbm = pl.BlockSpec(memory_space=pltpu.VMEM), pl.BlockSpec(memory_space=pl.ANY)
+    hbm = pl.BlockSpec(memory_space=pl.ANY)
     return pl.pallas_call(
         functools.partial(layer_kernel, head_dim, pad_cap),
-        out_shape=(jax.ShapeDtypeStruct(x.shape, bf16), jax.ShapeDtypeStruct((n_src, tokens + experts, d_model), bf16)),
-        in_specs=[vmem] * 5 + [hbm] * 7,
-        out_specs=(vmem, hbm),
+        out_shape=(pltpu.VMEM(x.shape, bf16), jax.ShapeDtypeStruct((n_src, tokens + experts, d_model), bf16)),
+        in_specs=[hbm] * 12,
+        out_specs=(pl.BlockSpec(memory_space=pltpu.VMEM), hbm),
         scratch_shapes=[
+            *(pltpu.VMEM(small.shape, small.dtype) for small in (idx_t, slot_t, gate_t, attn_gain, moe_gain)),
             pltpu.VMEM((tokens, d_model), bf16),
             pltpu.VMEM(rope.shape, f32),
+            pltpu.VMEM((n_rows, ffn), f32),
             pltpu.VMEM((n_exp, n_rows, d_model), bf16),
             pltpu.VMEM((parts, n_exp, 2, part_depth, ffn), bf16),
             pltpu.VMEM((parts, n_sub, n_exp, ffn, block_cols), bf16),
@@ -589,18 +638,14 @@
             pltpu.VMEM((n_exp, n_rows, ffn), bf16),
             pltpu.VMEM((n_src, tokens, n_exp * pad_cap), bf16),
             pltpu.VMEM((n_src, n_exp * pad_cap, block_cols), bf16),
-            pltpu.VMEM((2, 4, tokens, block_cols), f32),
-            pltpu.VMEM((2, 4, tokens, block_cols), f32),
-            pltpu.VMEM((2, 4, tokens, block_cols), f32),
-            pltpu.VMEM((3, 2, half, block_cols), f32),
-            pltpu.VMEM((3, 2, half, block_cols), f32),
-            pltpu.VMEM((3, 2, half, block_cols), f32),
-            dma((3,)), dma((3,)), dma((3,)), dma((3, 3, 2)), dma((3,)), dma((5,)),
-            dma, dma((3, 2)), dma, dma, dma((2,)),
+            *[pltpu.VMEM((2, 4, tokens, block_cols), f32)] * 3,
+            *[pltpu.VMEM((3, 2, half, block_cols), f32)] * 3,
+            *[dma((3,))] * 3, dma((3, 3, 2)), dma((3,)), dma((5,)),
+            dma, dma((3, 2)), dma, dma, dma((2,)), dma((5,)),
             dma((2, 2)), dma((3, 2)), dma((parts, chunks)), dma((2, 4)), dma((2, 4)),
-            dma((3, 2)), dma((3, 2)), dma((3, 2)), dma((3, 2)), dma((3, 2)), dma((3, 2)),
+            *[dma((3, 2))] * 6,
         ],
-        compiler_params=pltpu.CompilerParams(collective_id=1, has_side_effects=True, vmem_limit_bytes=63 * 1024 * 1024),
+        compiler_params=pltpu.CompilerParams(collective_id=1, has_side_effects=True, vmem_limit_bytes=60 * 1024 * 1024),
         cost_estimate=pl.CostEstimate(flops=40_000_000_000, bytes_accessed=30_000_000, transcendentals=0),
         name='whole_layer',
     )(idx_t, slot_t, gate_t, attn_gain, moe_gain, x, rope, qkv, proj, gate_w, up_w, down_w)[0]

time: 246 us -> 241 us (0.980)
  Pallas kernels: 243 us -> 240 us
    pallas_call x1, Pallas kernels: 243 us -> 240 us  [whole_layer(): pl.pallas_call(functools.partial(layer_kernel, head_dim, pad_cap), out_sh...]
where the time goes in v6:
time: 241 us
  Pallas kernels  240 us (100%)
    pallas_call x1, Pallas kernels, whole_layer(): pl.pallas_call(functools.partial(layer_kernel, head_dim, pad_cap), out_sh...  240 us

profile of v6, /device:TPU:0, one launch (start us, length us, event | category | flops | bytes accessed | tf_op | source)
XLA Modules:
  0.0 241.1 jit_solution(16606486267412140665)
XLA Ops:
  0.0 240.1 %whole_layer.1 = (bf16[512,1024]{1,0:T(8,128)(2,1)S(1)}, bf16[8,544,1024]{2,1,0:T(8,128)(2,1)}) custom-call(s32[8,512]{1,0:T(8,128)} %bitcast.19, s32[8,512]{1,0:T(8,128)} %bitcast.20, bf16[8,512]{1,0:T(8,128)(2,1)} %bitcast.21, bf16[1024]{0:T(1024)(128)(2,1)} %attn_gain_hbm.1, bf16[1024]{0:T(1024)(128)(2,1)} %moe_gain_hbm.1, bf16[512,1024]{1,0:T(8,128)(2,1)} %bitcast.17, ...), custom_call_target="tpu_custom_call" | custom-call | flops 40000000000 | bytes 30000000 | tf_op jit(solution)/shard_map/whole_layer/pallas_call | solution.py:622
  240.1 1.0 copy.14

commit v7 on v6

--- a/solution.py
+++ b/solution.py
@@ -67,6 +67,13 @@
 
 def remote(src, dst, send_sem, recv_sem, where):
     return pltpu.make_async_remote_copy(src_ref=src, dst_ref=dst, send_sem=send_sem, recv_sem=recv_sem, device_id=dev_id(where), device_id_type=MESH_ID)
+
+
+def run_if(cond, body):
+    if not isinstance(cond, bool):
+        pl.when(cond)(body)
+    elif cond:
+        body()
 
 
 def wait_in(ref, sem):
@@ -191,11 +198,16 @@
                  idx_hbm, slot_hbm, gate_idx_hbm, attn_gain_hbm, moe_gain_hbm, x_hbm, rope_hbm, qkv_hbm, proj_hbm, gate_hbm, up_hbm, down_hbm,
                  out_ref, tok_hbm,
                  idx_ref, slot_ref, gate_ref, attn_gain_ref, moe_gain_ref, x_ref, rope, gate_act, big, gate_up, down_all, work, own_tok, hidden, inner, comb, y_buf, send_core, acc, got_core, got_x, got_y, got_last,
-                 attn_send, attn_z_send, attn_z_recv, attn_direct, attn_partner, load_sems, tok_send, tok_direct, tok_partner, tok_sem, tok_load, small_sems,
-                 z_own, z_pass, z_recv, core_send, core_recv, x_send, x_recv, y_send, y_recv, last_send, last_recv):
+                 attn_z_recv, attn_direct, attn_partner, tok_direct, tok_partner,
+                 z_own, z_pass, z_recv, core_send, core_recv, x_send, y_send, last_send):
     place = layer_place()
     dx, dz, dy, dc = place
     tokens, d_model = x_ref.shape
+    x_recv, y_recv, last_recv = [attn_direct.at[n] for n in range(3)]
+    load_sems = [x_send.at[n // 2, n % 2] for n in range(5)]
+    small_sems = [core_send.at[n // 4, n % 4] for n in range(5)]
+    attn_send, attn_z_send = [[last_send.at[n, m] for n in range(3)] for m in BOTH]
+    tok_send, tok_sem, tok_load = y_send.at[0, 0], y_send.at[0, 1], y_send.at[1]
     experts = own_tok.shape[0] - tokens
     n_exp, n_rows, ffn = inner.shape
     n_src = comb.shape[0]
@@ -213,9 +225,9 @@
     def at_z(z):
         return (dx, z, dy, dc)
 
-    x_copy_in = pltpu.make_async_copy(x_hbm, x_ref, load_sems.at[0])
-    rope_copy_in = pltpu.make_async_copy(rope_hbm, rope, load_sems.at[1])
-    small_copies = [pltpu.make_async_copy(src, dst, small_sems.at[n]) for n, (src, dst) in enumerate(((idx_hbm, idx_ref), (slot_hbm, slot_ref), (gate_idx_hbm, gate_ref), (attn_gain_hbm, attn_gain_ref), (moe_gain_hbm, moe_gain_ref)))]
+    x_copy_in = pltpu.make_async_copy(x_hbm, x_ref, load_sems[0])
+    rope_copy_in = pltpu.make_async_copy(rope_hbm, rope, load_sems[1])
+    small_copies = [pltpu.make_async_copy(src, dst, small_sems[n]) for n, (src, dst) in enumerate(((idx_hbm, idx_ref), (slot_hbm, slot_ref), (gate_idx_hbm, gate_ref), (attn_gain_hbm, attn_gain_ref), (moe_gain_hbm, moe_gain_ref)))]
     for copy in [x_copy_in, rope_copy_in] + small_copies:
         copy.start()
     barrier = pltpu.get_barrier_semaphore()
@@ -242,7 +254,7 @@
     for index, step in enumerate(z_steps):
         proj_src = proj_hbm.at[pl.ds(pl.multiple_of(mine * row_piece, row_piece), row_piece)]
         for src, dst in ((qkv_rows(mine * col_piece, col_piece), qkv_rows(mine * col_piece, col_piece, dz)), (proj_src, proj_rows(dz * shard_rows + mine * row_piece, row_piece))):
-            remote(src, dst, attn_z_send.at[index], attn_z_recv.at[index], at_z((dz + step) % 4)).start()
+            remote(src, dst, attn_z_send[index], attn_z_recv.at[index], at_z((dz + step) % 4)).start()
 
     last_exp = n_exp - 1
 
@@ -316,7 +328,7 @@
     for j in range(chunks):
         own_loads += [(src, dst, 3 + kind_of(j)) for src, dst in zip(chunk_srcs(j), chunk_refs(dz, j))]
     for src, dst, sem in own_loads:
-        pltpu.make_async_copy(src, dst, load_sems.at[sem]).start()
+        pltpu.make_async_copy(src, dst, load_sems[sem]).start()
 
     for copy in [x_copy_in] + small_copies:
         copy.wait()
@@ -340,21 +352,21 @@
             cols, rows = col_piece // 2, row_piece // 2
             return [qkv_rows(slot * col_piece + half * cols, cols, source_z), proj_rows(source_z * shard_rows + slot * row_piece + half * rows, rows)]
 
-        streams.append(spread_in_layer(place, functools.partial(part_refs, mine), part_refs, attn_send.at[index], attn_direct.at[index], attn_partner.at[index], size_of(1), size_of(8)))
+        streams.append(spread_in_layer(place, functools.partial(part_refs, mine), part_refs, attn_send[index], attn_direct.at[index], attn_partner.at[index], size_of(1), size_of(8)))
     for index, stream in enumerate(streams):
         wait_in(size_of(2), attn_z_recv.at[index])
         next(stream)
     for _ in range(4):
         for stream in streams:
             next(stream)
-    wait_in(size_of(16), load_sems.at[2])
+    wait_in(size_of(16), load_sems[2])
     rope_copy_in.wait()
 
     attend(x_ref, own_tok, big, rope, work, hidden, head_dim)
     norm_rows(hidden, moe_gain_ref, own_tok, tokens)
     for index in range(3):
-        wait_in(size_of(14), attn_send.at[index])
-        wait_in(size_of(2), attn_z_send.at[index])
+        wait_in(size_of(14), attn_send[index])
+        wait_in(size_of(2), attn_z_send[index])
 
     half_rows = own_tok.shape[0] // 2
 
@@ -509,18 +521,19 @@
             wait_in(got_core.at[two(i), rel], core_recv.at[two(i), rel])
             acc[two(i), rel] = own + got_core[two(i), rel]
 
-            @pl.when(rel % 2 == 1)
-            def _():
-                x_copy(i, rel).start()
-
-            @pl.when(rel // 2 == 1)
-            def _():
-                y_copy(i, rel).start()
+            run_if(rel % 2 == 1, lambda: x_copy(i, rel).start())
+            run_if(rel // 2 == 1, lambda: y_copy(i, rel).start())
 
             return carry
 
-        lax.fori_loop(0, 4, core_body, 0)
-        lax.fori_loop(0, 4, own_body, 0)
+        if with_y:
+            lax.fori_loop(0, 3, core_body, 0)
+            own_body(0, 0)
+            core_body(3, 0)
+            lax.fori_loop(1, 4, own_body, 0)
+        else:
+            lax.fori_loop(0, 4, core_body, 0)
+            lax.fori_loop(0, 4, own_body, 0)
 
     def turn_block(i):
         wait_in(got_x.at[three(i), 0], x_recv.at[three(i), 0])
@@ -547,8 +560,8 @@
         for which in BOTH:
             last_copy(i, which).wait_send()
 
-    wait_in(gate_up.at[0], load_sems.at[3])
-    wait_in(down_all.at[0], load_sems.at[4])
+    wait_in(gate_up.at[0], load_sems[3])
+    wait_in(down_all.at[0], load_sems[4])
     for e in range(last_exp):
         expert_inner(e)
     y_block(0, 0, last_exp)
@@ -640,10 +653,8 @@
             pltpu.VMEM((n_src, n_exp * pad_cap, block_cols), bf16),
             *[pltpu.VMEM((2, 4, tokens, block_cols), f32)] * 3,
             *[pltpu.VMEM((3, 2, half, block_cols), f32)] * 3,
-            *[dma((3,))] * 3, dma((3, 3, 2)), dma((3,)), dma((5,)),
-            dma, dma((3, 2)), dma, dma, dma((2,)), dma((5,)),
-            dma((2, 2)), dma((3, 2)), dma((parts, chunks)), dma((2, 4)), dma((2, 4)),
-            *[dma((3, 2))] * 6,
+            dma((3,)), dma((3, 3, 2)), dma((3,)), dma((3, 2)), dma,
+            dma((2, 2)), dma((3, 2)), dma((parts, chunks)), dma((2, 4)), dma((2, 4)), *[dma((3, 2))] * 3,
         ],
         compiler_params=pltpu.CompilerParams(collective_id=1, has_side_effects=True, vmem_limit_bytes=60 * 1024 * 1024),
         cost_estimate=pl.CostEstimate(flops=40_000_000_000, bytes_accessed=30_000_000, transcendentals=0),

time: 241 us -> 241 us (level)
  no operation moved by 1% of the time
where the time goes in v7:
time: 241 us; the launch traced here: 240 us
  Pallas kernels  239 us (99%)
    pallas_call x1, Pallas kernels, whole_layer(): pl.pallas_call(functools.partial(layer_kernel, head_dim, pad_cap), out_sh...  239 us

profile of v7, /device:TPU:0, one launch (start us, length us, event | category | flops | bytes accessed | tf_op | source)
XLA Modules:
  0.0 240.4 jit_solution(10708700205394083449)
XLA Ops:
  0.0 239.4 %whole_layer.1 = (bf16[512,1024]{1,0:T(8,128)(2,1)S(1)}, bf16[8,544,1024]{2,1,0:T(8,128)(2,1)}) custom-call(s32[8,512]{1,0:T(8,128)} %bitcast.19, s32[8,512]{1,0:T(8,128)} %bitcast.20, bf16[8,512]{1,0:T(8,128)(2,1)} %bitcast.21, bf16[1024]{0:T(1024)(128)(2,1)} %attn_gain_hbm.1, bf16[1024]{0:T(1024)(128)(2,1)} %moe_gain_hbm.1, bf16[512,1024]{1,0:T(8,128)(2,1)} %bitcast.17, ...), custom_call_target="tpu_custom_call" | custom-call | flops 40000000000 | bytes 30000000 | tf_op jit(solution)/shard_map/whole_layer/pallas_call | solution.py:635
  239.4 1.0 copy.14

commit v8 on v7

--- a/solution.py
+++ b/solution.py
@@ -214,7 +214,7 @@
     block_cols = acc.shape[-1]
     half_tok = tokens // 2
     n_sub = down_all.shape[1]
-    chunks = n_exp + 1 + n_sub
+    chunks = n_exp + 2 + n_sub
     across_x, across_y, partner = related(place, 1, 0), related(place, 2, 0), related(place, 0, 1)
     upper = dz // 2
     inside = (dz == 1) | (dz == 2)
@@ -256,21 +256,29 @@
         for src, dst in ((qkv_rows(mine * col_piece, col_piece), qkv_rows(mine * col_piece, col_piece, dz)), (proj_src, proj_rows(dz * shard_rows + mine * row_piece, row_piece))):
             remote(src, dst, attn_z_send[index], attn_z_recv.at[index], at_z((dz + step) % 4)).start()
 
-    last_exp = n_exp - 1
+    last_exp, last_sub = n_exp - 1, n_sub - 1
+
+    def down_part(j):
+        sub = j - n_exp - 1
+        if sub < last_sub:
+            return sub, 0, n_exp
+        return (last_sub, 0, last_exp) if sub == last_sub else (last_sub, last_exp, 1)
 
     def chunk_refs(p, j):
         if j < last_exp:
             return [gate_up.at[p, j, m] for m in BOTH]
         if j <= n_exp:
             return [gate_up.at[p, last_exp, j - last_exp]]
-        return [down_all.at[p, j - n_exp - 1]]
+        sub, low, count = down_part(j)
+        return [down_all.at[p, sub, pl.ds(low, count)]]
 
     def chunk_srcs(j):
         if j < last_exp:
             return [gate_hbm.at[first_exp + j], up_hbm.at[first_exp + j]]
         if j <= n_exp:
             return [(gate_hbm, up_hbm)[j - last_exp].at[first_exp + last_exp]]
-        return [down_hbm.at[pl.ds(first_exp, n_exp), :, pl.ds((j - n_exp - 1) * block_cols, block_cols)]]
+        sub, low, count = down_part(j)
+        return [down_hbm.at[pl.ds(first_exp + low, count), :, pl.ds(sub * block_cols, block_cols)]]
 
     def kind_of(j):
         return 0 if j <= n_exp else 1
@@ -478,16 +486,22 @@
         rel, target = ((2, across_y), (1, across_x))[which]
         return remote(acc.at[two(i), rel, halves[which]], got_last.at[three(i), which], last_send.at[three(i), which], last_recv.at[three(i), which], target)
 
-    def wait_down(i):
+    def wait_down(i, last_parts=BOTH):
         p, sub = block_of(i)
+
+        def wait_parts():
+            for part in last_parts:
+                wait_chunk(p, n_exp + 1 + last_sub + part)
+
         if not (isinstance(i, int) and i < n_sub):
             @pl.when(at_end)
             def _():
-                wait_in(down_all.at[p, sub], z_recv.at[p, n_exp + 1 + sub])
-
-    def y_block(i, low=0, high=n_exp):
+                run_if(sub < last_sub, lambda: wait_in(down_all.at[p, sub], z_recv.at[p, n_exp + 1 + sub]))
+                run_if(sub == last_sub, wait_parts)
+
+    def y_block(i, low=0, high=n_exp, last_parts=BOTH):
         p, sub = block_of(i)
-        wait_down(i)
+        wait_down(i, last_parts)
 
         def y_body(e, carry):
             y_tall = jnp.dot(inner[e], down_all[p, sub, e], preferred_element_type=jnp.float32).astype(jnp.bfloat16)
@@ -505,7 +519,7 @@
             slot = rel_slot(rel, core_rel)
             if with_y:
                 rows = pl.ds(pl.multiple_of(slot * pad_cap, pad_cap), pad_cap)
-                for e in range(n_exp):
+                for e in (last_exp,):
                     y_buf[slot, e * pad_cap:(e + 1) * pad_cap] = jnp.dot(inner[e, rows], down_all[p, sub, e], preferred_element_type=jnp.float32).astype(jnp.bfloat16)
             return jnp.dot(comb[slot], y_buf[slot], preferred_element_type=jnp.float32)
 
@@ -597,8 +611,9 @@
     y_block(blocks - 2)
     sum_block(blocks - 2)
     end_block(blocks - 3)
+    y_block(blocks - 1, 0, last_exp, (0,))
     turn_block(blocks - 2)
-    wait_down(blocks - 1)
+    wait_down(blocks - 1, (1,))
     sum_block(blocks - 1, with_y=True)
     end_block(blocks - 2)
     turn_block(blocks - 1)
@@ -625,7 +640,7 @@
     part_depth, ffn = gate_w.shape[1:]
     parts, n_src, block_cols = 4, 8, LANES
     n_sub = down_w.shape[2] // block_cols
-    chunks = n_exp + 1 + n_sub
+    chunks = n_exp + 2 + n_sub
     n_rows = n_src * pad_cap
     half = tokens // 2
     rope = np.stack(rope_tables(tokens, head_dim))

time: 241 us -> 240 us (level)
  no operation moved by 1% of the time
where the time goes in v8:
time: 240 us
  Pallas kernels  239 us (100%)
    pallas_call x1, Pallas kernels, whole_layer(): pl.pallas_call(functools.partial(layer_kernel, head_dim, pad_cap), out_sh...  239 us

profile of v8, /device:TPU:0, one launch (start us, length us, event | category | flops | bytes accessed | tf_op | source)
XLA Modules:
  0.0 240.2 jit_solution(17646616348837400502)
XLA Ops:
  0.0 239.3 %whole_layer.1 = (bf16[512,1024]{1,0:T(8,128)(2,1)S(1)}, bf16[8,544,1024]{2,1,0:T(8,128)(2,1)}) custom-call(s32[8,512]{1,0:T(8,128)} %bitcast.19, s32[8,512]{1,0:T(8,128)} %bitcast.20, bf16[8,512]{1,0:T(8,128)(2,1)} %bitcast.21, bf16[1024]{0:T(1024)(128)(2,1)} %attn_gain_hbm.1, bf16[1024]{0:T(1024)(128)(2,1)} %moe_gain_hbm.1, bf16[512,1024]{1,0:T(8,128)(2,1)} %bitcast.17, ...), custom_call_target="tpu_custom_call" | custom-call | flops 40000000000 | bytes 30000000 | tf_op jit(solution)/shard_map/whole_layer/pallas_call | solution.py:650
  239.3 1.0 copy.14
